TPU v7x, 32 devices: a whole 2x2x4 slice. The times are simulated.
32 devices in a mesh: rep: 8 (over y, x, core), grp: 4 (over z).
Axes of the slice: x: 2, y: 2, z: 4, core: 2. Of those that a mesh axis runs over, the one named last changes fastest.
Arguments:
- images: bfloat16 [320, 197, 384], P(('rep', 'grp')), may hold values from -6 to 6
- cotangent: bfloat16 [320, 197, 384], P(('rep', 'grp')), may hold values from -6 to 6
- ln1_gain: bfloat16 [2, 384], P(None, 'grp'), may hold values from 0.5 to 1.5
- ln1_bias: bfloat16 [2, 384], P(None, 'grp'), may hold values from -1.5 to 1.5
- w_qkv: bfloat16 [2, 384, 1152], P(None, 'grp'), may hold values from -2 to 2
- q_bias: bfloat16 [2, 384], P(None, 'grp'), may hold values from -1.5 to 1.5
- v_bias: bfloat16 [2, 384], P(None, 'grp'), may hold values from -1.5 to 1.5
- w_proj: bfloat16 [2, 384, 384], P(None, 'grp'), may hold values from -1.25 to 1.25
- proj_bias: bfloat16 [2, 384], P(None, 'grp'), may hold values from -1.5 to 1.5
- ln2_gain: bfloat16 [2, 384], P(None, 'grp'), may hold values from 0.5 to 1.5
- ln2_bias: bfloat16 [2, 384], P(None, 'grp'), may hold values from -1.5 to 1.5
- w_up: bfloat16 [2, 384, 1536], P(None, 'grp'), may hold values from -0.3125 to 0.3125
- up_bias: bfloat16 [2, 1536], P(None, 'grp'), may hold values from -1.5 to 1.5
- w_down: bfloat16 [2, 1536, 384], P(None, 'grp'), may hold values from -0.15625 to 0.15625
- down_bias: bfloat16 [2, 384], P(None, 'grp'), may hold values from -1.5 to 1.5
Outputs:
- encoded: bfloat16 [320, 197, 384], P(('rep', 'grp'))
- images_grad: bfloat16 [320, 197, 384], P(('rep', 'grp'))
- grad_ln1_gain: float32 [2, 384], P(None, 'grp')
- grad_ln1_bias: float32 [2, 384], P(None, 'grp')
- grad_w_qkv: float32 [2, 384, 1152], P(None, 'grp')
- grad_q_bias: float32 [2, 384], P(None, 'grp')
- grad_v_bias: float32 [2, 384], P(None, 'grp')
- grad_w_proj: float32 [2, 384, 384], P(None, 'grp')
- grad_proj_bias: float32 [2, 384], P(None, 'grp')
- grad_ln2_gain: float32 [2, 384], P(None, 'grp')
- grad_ln2_bias: float32 [2, 384], P(None, 'grp')
- grad_w_up: float32 [2, 384, 1536], P(None, 'grp')
- grad_up_bias: float32 [2, 1536], P(None, 'grp')
- grad_w_down: float32 [2, 1536, 384], P(None, 'grp')
- grad_down_bias: float32 [2, 384], P(None, 'grp')
All inputs are finite; a program needn't handle non-finite values.
Results may differ from a plain program's by a relative error of at most 0.03.
The roundings to bfloat16 on the way count: a program that leaves them out, or rounds other values in their place, can miss the bound.
Values may be sent and summed in bfloat16 or wider, within the bound.
A program may use at most 256 MiB of HBM per device.

v0:
```python
import math

import jax
import jax.numpy as jnp
from jax import lax
from jax.sharding import PartitionSpec as P

D = 384
HEADS = 6
HEAD_DIM = 64
SEQ = 197
LAYERS = 2


EPS = 1e-06
INV_ROOT_TWO = 0.7071067811865476
INV_ROOT_TAU = 0.3989422804014327


def norm_forward(hidden, gain_vec, bias_vec):
    mean_rows = jnp.mean(hidden, axis=-1, keepdims=True)
    centered = hidden - mean_rows
    variance = jnp.mean(centered * centered, axis=-1, keepdims=True)
    inv_std = lax.rsqrt(variance + EPS)
    normed = centered * inv_std
    return (normed * gain_vec.astype(jnp.float32) + bias_vec.astype(jnp.float32), normed, inv_std)


def norm_backward(out_grad, normed, inv_std, gain_vec):
    scaled = out_grad * gain_vec.astype(jnp.float32)
    in_grad = inv_std * (
        scaled
        - jnp.mean(scaled, axis=-1, keepdims=True)
        - normed * jnp.mean(scaled * normed, axis=-1, keepdims=True)
    )
    return (in_grad, jnp.sum(out_grad * normed, axis=0), jnp.sum(out_grad, axis=0))


def gelu_parts(upward):
    cumul = 0.5 * (1.0 + lax.erf(upward * INV_ROOT_TWO))
    return (upward * cumul, cumul + upward * jnp.exp(-0.5 * upward * upward) * INV_ROOT_TAU)


def weight_grad(left, right):
    return lax.dot_general(
        left, right, (((0,), (0,)), ((), ())), preferred_element_type=jnp.float32
    )


def back_dot(grad_rows, weight):
    return lax.dot_general(
        grad_rows, weight, (((1,), (1,)), ((), ())), preferred_element_type=jnp.float32
    )


def head_split(rows, num_images):
    return rows.reshape(num_images, SEQ, HEADS, HEAD_DIM)


def attn_scores(query_rows, key_rows, num_images):
    return jnp.einsum(
        "nqhd,nkhd->nhqk",
        head_split(query_rows, num_images),
        head_split(key_rows, num_images),
        preferred_element_type=jnp.float32,
    ) / math.sqrt(HEAD_DIM)


def layer_forward(hidden, weights, num_images):
    (
        gain_one,
        bias_one,
        w_qkv,
        q_bias,
        v_bias,
        w_proj,
        proj_bias,
        gain_two,
        bias_two,
        w_up,
        up_bias,
        w_down,
        down_bias,
    ) = weights
    normed_in, normed_one, inv_one = norm_forward(hidden, gain_one, bias_one)
    normed_in = normed_in.astype(jnp.bfloat16)
    projected = jnp.dot(normed_in, w_qkv, preferred_element_type=jnp.float32)
    query_rows = (projected[:, :D] + q_bias.astype(jnp.float32)).astype(jnp.bfloat16)
    key_rows = projected[:, D : 2 * D].astype(jnp.bfloat16)
    value_rows = (projected[:, 2 * D :] + v_bias.astype(jnp.float32)).astype(jnp.bfloat16)
    scores = attn_scores(query_rows, key_rows, num_images)
    row_max = jnp.max(scores, axis=-1, keepdims=True)
    row_total = jnp.sum(jnp.exp(scores - row_max), axis=-1, keepdims=True)
    attn_probs = (jnp.exp(scores - row_max) / row_total).astype(jnp.bfloat16)
    context = jnp.einsum(
        "nhqk,nkhd->nqhd",
        attn_probs,
        head_split(value_rows, num_images),
        preferred_element_type=jnp.float32,
    )
    context = context.reshape(num_images * SEQ, D).astype(jnp.bfloat16)
    mixed = (
        hidden
        + jnp.dot(context, w_proj, preferred_element_type=jnp.float32)
        + proj_bias.astype(jnp.float32)
    )
    normed_mid, normed_two, inv_two = norm_forward(mixed, gain_two, bias_two)
    normed_mid = normed_mid.astype(jnp.bfloat16)
    upward = jnp.dot(normed_mid, w_up, preferred_element_type=jnp.float32) + up_bias.astype(
        jnp.float32
    )
    active, slope = gelu_parts(upward)
    active = active.astype(jnp.bfloat16)
    output = (
        mixed
        + jnp.dot(active, w_down, preferred_element_type=jnp.float32)
        + down_bias.astype(jnp.float32)
    )
    saved = (
        normed_in,
        query_rows,
        key_rows,
        value_rows,
        row_max,
        row_total,
        context,
        normed_one,
        inv_one,
        normed_mid,
        slope,
        active,
        normed_two,
        inv_two,
    )
    return (output, saved)


def layer_backward(saved, weights, out_grad, num_images):
    (
        gain_one,
        bias_one,
        w_qkv,
        q_bias,
        v_bias,
        w_proj,
        proj_bias,
        gain_two,
        bias_two,
        w_up,
        up_bias,
        w_down,
        down_bias,
    ) = weights
    (
        normed_in,
        query_rows,
        key_rows,
        value_rows,
        row_max,
        row_total,
        context,
        normed_one,
        inv_one,
        normed_mid,
        slope,
        active,
        normed_two,
        inv_two,
    ) = saved
    out_rounded = out_grad.astype(jnp.bfloat16)
    grad_w_down = weight_grad(active, out_rounded)
    grad_down_bias = jnp.sum(out_grad, axis=0)
    up_grad = back_dot(out_rounded, w_down) * slope
    up_rounded = up_grad.astype(jnp.bfloat16)
    grad_up_bias = jnp.sum(up_grad, axis=0)
    grad_w_up = weight_grad(normed_mid, up_rounded)
    mid_grad = back_dot(up_rounded, w_up)
    mixed_part, grad_gain_two, grad_bias_two = norm_backward(
        mid_grad, normed_two, inv_two, gain_two
    )
    mixed_grad = out_grad + mixed_part
    mixed_rounded = mixed_grad.astype(jnp.bfloat16)
    grad_proj_bias = jnp.sum(mixed_grad, axis=0)
    grad_w_proj = weight_grad(context, mixed_rounded)
    context_grad = back_dot(mixed_rounded, w_proj).astype(jnp.bfloat16)
    scores = attn_scores(query_rows, key_rows, num_images)
    attn_full = jnp.exp(scores - row_max) / row_total
    attn_probs = attn_full.astype(jnp.bfloat16)
    ctx_heads = head_split(context_grad, num_images)
    prob_grad = jnp.einsum(
        "nqhd,nkhd->nhqk",
        ctx_heads,
        head_split(value_rows, num_images),
        preferred_element_type=jnp.float32,
    )
    value_grad = jnp.einsum(
        "nhqk,nqhd->nkhd", attn_probs, ctx_heads, preferred_element_type=jnp.float32
    )
    row_dot = jnp.sum(attn_full * prob_grad, axis=-1, keepdims=True)
    score_grad = (attn_full * (prob_grad - row_dot) / math.sqrt(HEAD_DIM)).astype(jnp.bfloat16)
    query_grad = jnp.einsum(
        "nhqk,nkhd->nqhd",
        score_grad,
        head_split(key_rows, num_images),
        preferred_element_type=jnp.float32,
    )
    key_grad = jnp.einsum(
        "nhqk,nqhd->nkhd",
        score_grad,
        head_split(query_rows, num_images),
        preferred_element_type=jnp.float32,
    )
    total_rows = num_images * SEQ
    query_grad = query_grad.reshape(total_rows, D)
    key_grad = key_grad.reshape(total_rows, D)
    value_grad = value_grad.reshape(total_rows, D)
    grad_q_bias = jnp.sum(query_grad, axis=0)
    grad_v_bias = jnp.sum(value_grad, axis=0)
    joint = jnp.concatenate([query_grad, key_grad, value_grad], axis=1).astype(jnp.bfloat16)
    grad_w_qkv = weight_grad(normed_in, joint)
    in_part, grad_gain_one, grad_bias_one = norm_backward(
        back_dot(joint, w_qkv), normed_one, inv_one, gain_one
    )
    grads = (
        grad_gain_one,
        grad_bias_one,
        grad_w_qkv,
        grad_q_bias,
        grad_v_bias,
        grad_w_proj,
        grad_proj_bias,
        grad_gain_two,
        grad_bias_two,
        grad_w_up,
        grad_up_bias,
        grad_w_down,
        grad_down_bias,
    )
    return (grads, mixed_grad + in_part)


def fetch_forward(params, layer_index):
    return (
        lax.all_gather(params[0][layer_index], "grp", axis=0, tiled=True),
        lax.all_gather(params[1][layer_index], "grp", axis=0, tiled=True),
        lax.all_gather(params[2][layer_index], "grp", axis=0, tiled=True),
        lax.all_gather(params[3][layer_index], "grp", axis=0, tiled=True),
        lax.all_gather(params[4][layer_index], "grp", axis=0, tiled=True),
        lax.all_gather(params[5][layer_index], "grp", axis=0, tiled=True),
        lax.all_gather(params[6][layer_index], "grp", axis=0, tiled=True),
        lax.all_gather(params[7][layer_index], "grp", axis=0, tiled=True),
        lax.all_gather(params[8][layer_index], "grp", axis=0, tiled=True),
        lax.all_gather(params[9][layer_index], "grp", axis=0, tiled=True),
        lax.all_gather(params[10][layer_index], "grp", axis=0, tiled=True),
        lax.all_gather(params[11][layer_index], "grp", axis=0, tiled=True),
        lax.all_gather(params[12][layer_index], "grp", axis=0, tiled=True),
    )


def fetch_backward(params, layer_index):
    return (
        lax.all_gather(params[0][layer_index], "grp", axis=0, tiled=True),
        lax.all_gather(params[1][layer_index], "grp", axis=0, tiled=True),
        lax.all_gather(params[2][layer_index], "grp", axis=0, tiled=True),
        lax.all_gather(params[3][layer_index], "grp", axis=0, tiled=True),
        lax.all_gather(params[4][layer_index], "grp", axis=0, tiled=True),
        lax.all_gather(params[5][layer_index], "grp", axis=0, tiled=True),
        lax.all_gather(params[6][layer_index], "grp", axis=0, tiled=True),
        lax.all_gather(params[7][layer_index], "grp", axis=0, tiled=True),
        lax.all_gather(params[8][layer_index], "grp", axis=0, tiled=True),
        lax.all_gather(params[9][layer_index], "grp", axis=0, tiled=True),
        lax.all_gather(params[10][layer_index], "grp", axis=0, tiled=True),
        lax.all_gather(params[11][layer_index], "grp", axis=0, tiled=True),
        lax.all_gather(params[12][layer_index], "grp", axis=0, tiled=True),
    )


def owners_then_replicas(grads):
    shares = (
        lax.psum_scatter(
            grads[0].astype(jnp.bfloat16), "grp", scatter_dimension=0, tiled=True
        ).astype(jnp.float32),
        lax.psum_scatter(
            grads[1].astype(jnp.bfloat16), "grp", scatter_dimension=0, tiled=True
        ).astype(jnp.float32),
        lax.psum_scatter(
            grads[2].astype(jnp.bfloat16), "grp", scatter_dimension=0, tiled=True
        ).astype(jnp.float32),
        lax.psum_scatter(
            grads[3].astype(jnp.bfloat16), "grp", scatter_dimension=0, tiled=True
        ).astype(jnp.float32),
        lax.psum_scatter(
            grads[4].astype(jnp.bfloat16), "grp", scatter_dimension=0, tiled=True
        ).astype(jnp.float32),
        lax.psum_scatter(
            grads[5].astype(jnp.bfloat16), "grp", scatter_dimension=0, tiled=True
        ).astype(jnp.float32),
        lax.psum_scatter(
            grads[6].astype(jnp.bfloat16), "grp", scatter_dimension=0, tiled=True
        ).astype(jnp.float32),
        lax.psum_scatter(
            grads[7].astype(jnp.bfloat16), "grp", scatter_dimension=0, tiled=True
        ).astype(jnp.float32),
        lax.psum_scatter(
            grads[8].astype(jnp.bfloat16), "grp", scatter_dimension=0, tiled=True
        ).astype(jnp.float32),
        lax.psum_scatter(
            grads[9].astype(jnp.bfloat16), "grp", scatter_dimension=0, tiled=True
        ).astype(jnp.float32),
        lax.psum_scatter(
            grads[10].astype(jnp.bfloat16), "grp", scatter_dimension=0, tiled=True
        ).astype(jnp.float32),
        lax.psum_scatter(
            grads[11].astype(jnp.bfloat16), "grp", scatter_dimension=0, tiled=True
        ).astype(jnp.float32),
        lax.psum_scatter(
            grads[12].astype(jnp.bfloat16), "grp", scatter_dimension=0, tiled=True
        ).astype(jnp.float32),
    )
    return (
        lax.psum(shares[0].astype(jnp.bfloat16), "rep").astype(jnp.float32),
        lax.psum(shares[1].astype(jnp.bfloat16), "rep").astype(jnp.float32),
        lax.psum(shares[2].astype(jnp.bfloat16), "rep").astype(jnp.float32),
        lax.psum(shares[3].astype(jnp.bfloat16), "rep").astype(jnp.float32),
        lax.psum(shares[4].astype(jnp.bfloat16), "rep").astype(jnp.float32),
        lax.psum(shares[5].astype(jnp.bfloat16), "rep").astype(jnp.float32),
        lax.psum(shares[6].astype(jnp.bfloat16), "rep").astype(jnp.float32),
        lax.psum(shares[7].astype(jnp.bfloat16), "rep").astype(jnp.float32),
        lax.psum(shares[8].astype(jnp.bfloat16), "rep").astype(jnp.float32),
        lax.psum(shares[9].astype(jnp.bfloat16), "rep").astype(jnp.float32),
        lax.psum(shares[10].astype(jnp.bfloat16), "rep").astype(jnp.float32),
        lax.psum(shares[11].astype(jnp.bfloat16), "rep").astype(jnp.float32),
        lax.psum(shares[12].astype(jnp.bfloat16), "rep").astype(jnp.float32),
    )


def on_device(
    images,
    cotangent,
    ln1_gain,
    ln1_bias,
    w_qkv,
    q_bias,
    v_bias,
    w_proj,
    proj_bias,
    ln2_gain,
    ln2_bias,
    w_up,
    up_bias,
    w_down,
    down_bias,
):
    params = (
        ln1_gain,
        ln1_bias,
        w_qkv,
        q_bias,
        v_bias,
        w_proj,
        proj_bias,
        ln2_gain,
        ln2_bias,
        w_up,
        up_bias,
        w_down,
        down_bias,
    )
    num_images = images.shape[0]
    total_rows = num_images * SEQ
    hidden = images.reshape(total_rows, D).astype(jnp.float32)
    kept_weights = []
    saved_list = []
    for layer_index in range(LAYERS):
        weights = fetch_forward(params, layer_index)
        kept_weights.append(weights)
        hidden, saved = layer_forward(hidden, weights, num_images)
        saved_list.append(saved)
    encoded = hidden.astype(jnp.bfloat16).reshape(images.shape)
    flowing = cotangent.reshape(total_rows, D).astype(jnp.float32)
    results = [None] * LAYERS
    for layer_index in reversed(range(LAYERS)):
        weights = fetch_backward(params, layer_index)
        grads, flowing = layer_backward(saved_list[layer_index], weights, flowing, num_images)
        results[layer_index] = owners_then_replicas(grads)
    images_grad = flowing.astype(jnp.bfloat16).reshape(images.shape)
    stacked = [
        jnp.stack([results[idx][position] for idx in range(LAYERS)])
        for position in range(len(params))
    ]
    return (
        encoded,
        images_grad,
        stacked[0],
        stacked[1],
        stacked[2],
        stacked[3],
        stacked[4],
        stacked[5],
        stacked[6],
        stacked[7],
        stacked[8],
        stacked[9],
        stacked[10],
        stacked[11],
        stacked[12],
    )


def solution(mesh):
    in_specs = (
        P(("rep", "grp"), None, None),
        P(("rep", "grp"), None, None),
        P(None, "grp"),
        P(None, "grp"),
        P(None, "grp", None),
        P(None, "grp"),
        P(None, "grp"),
        P(None, "grp", None),
        P(None, "grp"),
        P(None, "grp"),
        P(None, "grp"),
        P(None, "grp", None),
        P(None, "grp"),
        P(None, "grp", None),
        P(None, "grp"),
    )
    out_specs = (
        P(("rep", "grp"), None, None),
        P(("rep", "grp"), None, None),
        P(None, "grp"),
        P(None, "grp"),
        P(None, "grp", None),
        P(None, "grp"),
        P(None, "grp"),
        P(None, "grp", None),
        P(None, "grp"),
        P(None, "grp"),
        P(None, "grp"),
        P(None, "grp", None),
        P(None, "grp"),
        P(None, "grp", None),
        P(None, "grp"),
    )
    return jax.shard_map(
        on_device, mesh=mesh, in_specs=in_specs, out_specs=out_specs, check_vma=False
    )
```

profile of v0, /device:TPU:0, one launch (start us, length us, event | category | flops | bytes accessed | tf_op | source)
XLA Modules:
  0.0 832.8 jit_solution(8012677368147854103)
XLA Ops:
  21.7 21.6 %all-reduce.37 = (bf16[384]{0:T(512)(128)(2,1)S(1)}, bf16[384]{0:T(512)(128)(2,1)S(1)}, bf16[384]{0:T(512)(128)(2,1)S(1)}, bf16[384]{0:T(512)(128)(2,1)S(1)}, bf...) all-reduce(bf16[384]{0:T(512)(128)(2,1)S(1)} %dynamic-update-slice., ...), channel_id=3, replica_groups=mesh['rep'=8,'grp'=4] {'grp'}, use_global_device_ids=true, to_apply=%add.1 | all-reduce | flops 5760 | bytes 23040
  43.5 11.9 %all-gather.23 = bf16[1,1536]{1,0:T(2,128)(2,1)S(1)} all-gather(bf16[1,384]{1,0:T(2,128)(2,1)S(1)} %get-tuple-element.109), channel_id=25, replica_groups=mesh['rep'=8,'grp'=4] {'grp'}, dimensions={1}, use_global_device_ids=true | all-gather | bytes 3840 | tf_op jit(solution)/shard_map/all_gather | solution.py:254
  55.5 12.2 %all-gather.10 = bf16[1,1536]{1,0:T(2,128)(2,1)S(1)} all-gather(bf16[1,384]{1,0:T(2,128)(2,1)S(1)} %get-tuple-element.110), channel_id=12, replica_groups=mesh['rep'=8,'grp'=4] {'grp'}, dimensions={1}, use_global_device_ids=true | all-gather | bytes 3840 | tf_op jit(solution)/shard_map/all_gather | solution.py:254
  67.9 16.2 %all-gather.18 = bf16[1,384,384]{2,1,0:T(8,128)(2,1)} all-gather(bf16[1,96,384]{2,1,0:T(8,128)(2,1)S(1)} %get-tuple-element.107), channel_id=20, replica_groups=mesh['rep'=8,'grp'=4] {'grp'}, dimensions={1}, use_global_device_ids=true | all-gather | bytes 368640 | tf_op jit(solution)/shard_map/all_gather | solution.py:249
  84.1 16.6 %all-gather.5 = bf16[1,384,384]{2,1,0:T(8,128)(2,1)S(1)} all-gather(bf16[1,96,384]{2,1,0:T(8,128)(2,1)S(1)} %get-tuple-element.108), channel_id=7, replica_groups=mesh['rep'=8,'grp'=4] {'grp'}, dimensions={1}, use_global_device_ids=true | all-gather | bytes 368640 | tf_op jit(solution)/shard_map/all_gather | solution.py:249
  101.9 28.7 %all-gather.15 = bf16[1,384,1152]{2,1,0:T(8,128)(2,1)} all-gather(bf16[1,96,1152]{2,1,0:T(8,128)(2,1)S(1)} %get-tuple-element.105), channel_id=17, replica_groups=mesh['rep'=8,'grp'=4] {'grp'}, dimensions={1}, use_global_device_ids=true | all-gather | bytes 1105920 | tf_op jit(solution)/shard_map/all_gather | solution.py:246
  130.6 23.0 %all-gather.2 = bf16[1,384,1152]{2,1,0:T(8,128)(2,1)} all-gather(bf16[1,96,1152]{2,1,0:T(8,128)(2,1)S(1)} %get-tuple-element.106), channel_id=4, replica_groups=mesh['rep'=8,'grp'=4] {'grp'}, dimensions={1}, use_global_device_ids=true | all-gather | bytes 1105920 | tf_op jit(solution)/shard_map/all_gather | solution.py:246
  198.4 11.1 %fusion.125 = (f32[10,6,197]{2,1,0:T(8,128)S(1)}, f32[10,6,197,197]{2,3,1,0:T(8,128)}) fusion(bf16[10,197,6,64]{1,3,2,0:T(8,128)(2,1)} %copy.97, bf16[10,197,6,64]{1,3,2,0:T(8,128)(2,1)} %copy.98), kind=kOutput, calls=%fused_computation.239 | convolution fusion | flops 305038912 | bytes 12387360 | tf_op jit(solution)/shard_map/sub | solution.py:94
  230.2 10.3 %multiply_convert_fusion.3 = (bf16[1970,1536]{1,0:T(8,128)(2,1)}, f32[1970,1536]{1,0:T(8,128)}) fusion(f32[1536]{0:T(1024)S(1)} %convert_reduce_fusion.2, bf16[1,384,1536]{2,1,0:T(8,128)(2,1)} %all-gather.31.cloned.1.call-done, f32[1970,384]{1,0:T(8,128)} %copy-done.5, f32[384]{0:T(512)S(1)} %convert_element_type.436, f32[384]{0:T(512)S(1)} %convert_element_type.435, ...), kind=kOutput, calls=%fused_computation.26 | convolution fusion | flops 2345844480 | bytes 22386064 | tf_op jit(solution)/shard_map/dot_general | solution.py:109
  290.1 11.0 %fusion.128 = (f32[10,6,197]{2,1,0:T(8,128)S(1)}, f32[10,6,197,197]{2,3,1,0:T(8,128)}) fusion(bf16[10,197,6,64]{1,3,2,0:T(8,128)(2,1)} %copy.105, bf16[10,197,6,64]{1,3,2,0:T(8,128)(2,1)} %copy.106), kind=kOutput, calls=%fused_computation.242 | convolution fusion | flops 305038912 | bytes 12387360 | tf_op jit(solution)/shard_map/sub | solution.py:94
  321.7 10.0 %multiply_convert_fusion.2 = (bf16[1970,1536]{1,0:T(8,128)(2,1)}, f32[1970,1536]{1,0:T(8,128)}) fusion(f32[1536]{0:T(1024)S(1)} %convert_reduce_fusion.1, bf16[1,384,1536]{2,1,0:T(8,128)(2,1)} %all-gather.35.cloned.1.call-done, f32[1970,384]{1,0:T(8,128)} %copy-done.8, f32[384]{0:T(512)S(1)} %convert_element_type.444, f32[384]{0:T(512)S(1)} %convert_element_type.443, ...), kind=kOutput, calls=%fused_computation.24 | convolution fusion | flops 2345844480 | bytes 22386064 | tf_op jit(solution)/shard_map/dot_general | solution.py:109
  331.7 11.7 %fusion.134 = (bf16[1536]{0:T(1024)(128)(2,1)}, bf16[1970,1536]{1,0:T(8,128)(2,1)S(1)}) fusion(f32[1970,1536]{1,0:T(8,128)} %get-tuple-element.142, f32[1536]{0:T(1024)S(1)} %convert_reduce_fusion.1, bf16[1970,384]{1,0:T(8,128)(2,1)} %reshape.243, bf16[1,1536,384]{2,1,0:T(8,128)(2,1)} %all-gather.37.cloned.1.call-done), kind=kOutput, calls=%fused_computation.244 | convolution fusion | flops 2360216064 | bytes 20857344 | tf_op jit(solution)/shard_map/dot_general | solution.py:51
  369.8 9.9 %bitcast_convert_fusion.2 = (bf16[10,197,6,64]{1,3,2,0:T(8,128)(2,1)}, f32[10,6,64,197]{3,2,1,0:T(8,128)}) fusion(bf16[10,197,6,64]{1,3,2,0:T(8,128)(2,1)} %copy.111, f32[10,6,197,197]{2,3,1,0:T(8,128)} %get-tuple-element.138, f32[10,6,197]{2,1,0:T(8,128)S(1)} %get-tuple-element.137), kind=kOutput, calls=%fused_computation.45 | convolution fusion | flops 303466688 | bytes 15413280 | tf_op jit(solution)/shard_map/nhqk,nqhd->nkhd/dot_general | solution.py:196
  385.9 18.5 %convert_bitcast_fusion.1 = bf16[10,197,6,64]{1,3,2,0:T(8,128)(2,1)} fusion(bf16[10,197,6,64]{1,3,2,0:T(8,128)(2,1)} %copy.105, f32[10,6,197,197]{2,3,1,0:T(8,128)} %fusion.136, f32[10,6,197,197]{2,3,1,0:T(8,128)} %get-tuple-element.138, f32[10,6,197]{2,1,0:T(8,128)S(1)} %get-tuple-element.137), kind=kOutput, calls=%fused_computation.115 | convolution fusion | flops 315121408 | bytes 21701520 | tf_op jit(solution)/shard_map/nhqk,nqhd->nkhd/dot_general | solution.py:207
  404.4 20.6 %bitcast_convert_fusion.3 = (bf16[10,197,6,64]{1,3,2,0:T(8,128)(2,1)}, f32[10,6,64,197]{3,2,1,0:T(8,128)}) fusion(bf16[10,197,6,64]{1,3,2,0:T(8,128)(2,1)} %copy.106, f32[10,6,197,197]{2,3,1,0:T(8,128)} %fusion.136, f32[10,6,197,197]{2,3,1,0:T(8,128)} %get-tuple-element.138, f32[10,6,197]{2,1,0:T(8,128)S(1)} %get-tuple-element.137), kind=kOutput, calls=%fused_computation.47 | convolution fusion | flops 315121408 | bytes 24727440 | tf_op jit(solution)/shard_map/nhqk,nkhd->nqhd/dot_general | solution.py:201
  496.6 9.9 %bitcast_convert_fusion = (bf16[10,197,6,64]{1,3,2,0:T(8,128)(2,1)}, f32[10,6,64,197]{3,2,1,0:T(8,128)}) fusion(bf16[10,197,6,64]{1,3,2,0:T(8,128)(2,1)} %copy.123, f32[10,6,197,197]{2,3,1,0:T(8,128)} %get-tuple-element.130, f32[10,6,197]{2,1,0:T(8,128)S(1)} %copy-done.84), kind=kOutput, calls=%fused_computation.41 | convolution fusion | flops 303466688 | bytes 15413280 | tf_op jit(solution)/shard_map/nhqk,nqhd->nkhd/dot_general | solution.py:196
  523.4 20.7 %bitcast_convert_fusion.1 = (bf16[10,197,6,64]{1,3,2,0:T(8,128)(2,1)}, f32[10,6,64,197]{3,2,1,0:T(8,128)}) fusion(bf16[10,197,6,64]{1,3,2,0:T(8,128)(2,1)} %copy.98, f32[10,6,197,197]{2,3,1,0:T(8,128)} %fusion.137, f32[10,6,197,197]{2,3,1,0:T(8,128)} %get-tuple-element.130, f32[10,6,197]{2,1,0:T(8,128)S(1)} %copy-done.84), kind=kOutput, calls=%fused_computation.43 | convolution fusion | flops 315121408 | bytes 24727440 | tf_op jit(solution)/shard_map/nhqk,nkhd->nqhd/dot_general | solution.py:201
  564.7 18.8 %convert_bitcast_fusion = bf16[10,197,6,64]{1,3,2,0:T(8,128)(2,1)} fusion(bf16[10,197,6,64]{1,3,2,0:T(8,128)(2,1)} %copy.97, f32[10,6,197,197]{2,3,1,0:T(8,128)} %fusion.137, f32[10,6,197,197]{2,3,1,0:T(8,128)} %get-tuple-element.130, f32[10,6,197]{2,1,0:T(8,128)S(1)} %copy-done.84), kind=kOutput, calls=%fused_computation.114 | convolution fusion | flops 315121408 | bytes 21701520 | tf_op jit(solution)/shard_map/nhqk,nqhd->nkhd/dot_general | solution.py:207
  621.5 8.2 multiply_reduce_fusion.8
  639.7 21.2 %all-reduce.36 = (bf16[384]{0:T(512)(128)(2,1)S(1)}, bf16[384]{0:T(512)(128)(2,1)S(1)}, bf16[384]{0:T(512)(128)(2,1)S(1)}, bf16[384]{0:T(512)(128)(2,1)S(1)}, bf...) all-reduce(bf16[384]{0:T(512)(128)(2,1)S(1)} %dynamic-update-slice., ...), channel_id=27, replica_groups=mesh['rep'=8,'grp'=4] {'grp'}, use_global_device_ids=true, to_apply=%add.15 | all-reduce | flops 9600 | bytes 38400
  685.4 22.4 %all-reduce.34 = (bf16[1,96]{1,0:T(2,128)(2,1)S(1)}, bf16[1,96]{1,0:T(2,128)(2,1)S(1)}, bf16[1,96]{1,0:T(2,128)(2,1)S(1)}, bf16[1,96]{1,0:T(2,128)(2,1)S(1)}, bf...) all-reduce(bf16[1,96]{1,0:T(2,128)(2,1)S(1)} %dynamic-slice_bitcast, ...), channel_id=1, replica_groups=mesh['rep'=8,'grp'=4] {'rep'}, use_global_device_ids=true, to_apply=%region_27.0 | all-reduce | flops 2304 | bytes 9216 | tf_op jit(solution)/shard_map/psum | solution.py:321
  708.4 15.8 %reduce-scatter.21.cloned.1.call-done = bf16[384,384]{1,0:T(8,128)(2,1)} async-done(((bf16[1536,384]{1,0:T(8,128)(2,1)}), bf16[384,384]{1,0:T(8,128)(2,1)}) %reduce-scatter.21.cloned.1.call-update) | async-done | bytes 294928 | tf_op jit(solution)/shard_map/reduce_scatter | solution.py:313
  724.2 30.7 %reduce-scatter.17.cloned.1.call-done = bf16[96,1536]{1,0:T(8,128)(2,1)} async-done(((bf16[384,1536]{1,0:T(8,128)(2,1)}), bf16[96,1536]{1,0:T(8,128)(2,1)}) %reduce-scatter.17.cloned.1.call-update) | async-done | bytes 294928 | tf_op jit(solution)/shard_map/reduce_scatter | solution.py:307
  759.5 59.3 %all-reduce.40.cloned.1.call-done = (bf16[1,96,1152]{2,1,0:T(8,128)(2,1)}, bf16[1,96,1152]{2,1,0:T(8,128)(2,1)}, bf16[1,96,384]{2,1,0:T(8,128)(2,1)}, bf16[1,96,...) async-done(((bf16[1,96,1152]{2,1,0:T(8,128)(2,1)}, ...) | async-done | bytes 1769488 | tf_op jit(solution)/shard_map/psum | solution.py:323
  (420 shorter events, 374.7 us)
Async XLA Ops:
  7.2 222.9 %all-gather.31.cloned.1.call-start = ((), (), s32[]{:S(2)}) async-start(), calls=%async_computation.16 | async-start | bytes 1474560 | tf_op jit(solution)/shard_map/all_gather | solution.py:253
  9.3 231.3 %all-gather.33.cloned.1.call-start = ((), (), s32[]{:S(2)}) async-start(), calls=%async_computation.17 | async-start | bytes 1474560 | tf_op jit(solution)/shard_map/all_gather | solution.py:255
  11.3 310.4 %all-gather.35.cloned.1.call-start = ((), (), s32[]{:S(2)}) async-start(), calls=%async_computation.18 | async-start | bytes 1474560 | tf_op jit(solution)/shard_map/all_gather | solution.py:253
  12.0 319.7 %all-gather.37.cloned.1.call-start = ((), (), s32[]{:S(2)}) async-start(), calls=%async_computation.19 | async-start | bytes 1474560 | tf_op jit(solution)/shard_map/all_gather | solution.py:255
  12.6 695.7 %reduce-scatter.15.cloned.1.call-start = ((), (), s32[]{:S(2)}) async-start(), calls=%async_computation.11 | async-start | bytes 368640 | tf_op jit(solution)/shard_map/reduce_scatter | solution.py:295
  13.2 143.2 %copy-start.34 = (f32[1970]{0:T(1024)}, f32[1970]{0:T(1024)S(1)}, u32[]{:S(2)}) copy-start(f32[1970]{0:T(1024)S(1)} %div.89) | copy-start | bytes 23644
  16.2 208.6 %copy-start = (f32[1970,384]{1,0:T(8,128)}, f32[1970,384]{1,0:T(8,128)S(1)}, u32[]{:S(2)}) copy-start(f32[1970,384]{1,0:T(8,128)S(1)} %reshape.253) | copy-start | bytes 9077764
  43.3 113.1 %copy-start.49 = (f32[384]{0:T(512)}, f32[384]{0:T(512)S(1)}, u32[]{:S(2)}) copy-start(f32[384]{0:T(512)S(1)} %convert_element_type.431) | copy-start | bytes 4612
  43.3 113.1 %copy-start.43 = (f32[384]{0:T(512)}, f32[384]{0:T(512)S(1)}, u32[]{:S(2)}) copy-start(f32[384]{0:T(512)S(1)} %convert_element_type.430) | copy-start | bytes 4612
  43.3 186.8 %copy-start.57 = (f32[384]{0:T(512)}, f32[384]{0:T(512)S(1)}, u32[]{:S(2)}) copy-start(f32[384]{0:T(512)S(1)} %convert_element_type.435) | copy-start | bytes 4612
  43.4 304.8 %copy-start.53 = (f32[384]{0:T(512)}, f32[384]{0:T(512)S(1)}, u32[]{:S(2)}) copy-start(f32[384]{0:T(512)S(1)} %convert_element_type.443) | copy-start | bytes 4612
  43.4 186.8 %copy-start.63 = (f32[384]{0:T(512)}, f32[384]{0:T(512)S(1)}, u32[]{:S(2)}) copy-start(f32[384]{0:T(512)S(1)} %convert_element_type.436) | copy-start | bytes 4612
  43.4 205.4 %copy-start.51 = (f32[384]{0:T(512)}, f32[384]{0:T(512)S(1)}, u32[]{:S(2)}) copy-start(f32[384]{0:T(512)S(1)} %convert_element_type.439) | copy-start | bytes 4612
  43.4 278.2 %copy-start.65 = (f32[384]{0:T(512)}, f32[384]{0:T(512)S(1)}, u32[]{:S(2)}) copy-start(f32[384]{0:T(512)S(1)} %convert_element_type.444) | copy-start | bytes 4612
  67.7 162.4 %copy-start.55 = (f32[1536]{0:T(1024)}, f32[1536]{0:T(1024)S(1)}, u32[]{:S(2)}) copy-start(f32[1536]{0:T(1024)S(1)} %convert_reduce_fusion.2) | copy-start | bytes 18436
  100.7 124.0 %copy-start.27 = (bf16[1,384,384]{2,1,0:T(8,128)(2,1)}, bf16[1,384,384]{2,1,0:T(8,128)(2,1)S(1)}, u32[]{:S(2)}) copy-start(bf16[1,384,384]{2,1,0:T(8,128)(2,1)S(1)} %all-gather.5) | copy-start | bytes 884740
  512.7 195.7 %reduce-scatter.13.cloned.1.call-start = ((), (), s32[]{:S(2)}) async-start(), calls=%async_computation.10 | async-start | bytes 368640 | tf_op jit(solution)/shard_map/reduce_scatter | solution.py:295
  558.5 149.9 %reduce-scatter.11.cloned.1.call-start = ((), (), s32[]{:S(2)}) async-start(), calls=%async_computation.9 | async-start | bytes 1105920 | tf_op jit(solution)/shard_map/reduce_scatter | solution.py:286
  564.6 143.7 %reduce-scatter.9.cloned.1.call-start = ((), (), s32[]{:S(2)}) async-start(), calls=%async_computation.8 | async-start | bytes 1105920 | tf_op jit(solution)/shard_map/reduce_scatter | solution.py:286
  599.0 109.4 %reduce-scatter.19.cloned.1.call-start = ((), (), s32[]{:S(2)}) async-start(), calls=%async_computation.13 | async-start | bytes 1474560 | tf_op jit(solution)/shard_map/reduce_scatter | solution.py:307
  606.6 101.8 %reduce-scatter.23.cloned.1.call-start = ((), (), s32[]{:S(2)}) async-start(), calls=%async_computation.15 | async-start | bytes 1474560 | tf_op jit(solution)/shard_map/reduce_scatter | solution.py:313
  614.3 109.8 %reduce-scatter.21.cloned.1.call-start = ((), (), s32[]{:S(2)}) async-start(), calls=%async_computation.14 | async-start | bytes 1474560 | tf_op jit(solution)/shard_map/reduce_scatter | solution.py:313
  634.4 120.5 %reduce-scatter.17.cloned.1.call-start = ((), (), s32[]{:S(2)}) async-start(), calls=%async_computation.12 | async-start | bytes 1474560 | tf_op jit(solution)/shard_map/reduce_scatter | solution.py:307
  675.2 143.6 %all-reduce.40.cloned.1.call-start = ((), (), s32[]{:S(2)}) async-start(), calls=%async_computation.20 | async-start | bytes 3538944 | tf_op jit(solution)/shard_map/psum | solution.py:323
  (79 other events, 608.2 us)
Sparse Core Ops, SparseCore 0:
  10.1 33.3 all-gather.30
  45.7 34.6 all-gather.32
  82.6 44.5 all-gather.34
  129.2 33.5 all-gather.36
  512.8 21.4 reduce-scatter.14
  558.6 21.4 reduce-scatter.12
  583.0 22.9 reduce-scatter.10
  608.2 23.9 reduce-scatter.8
  635.2 28.5 reduce-scatter.18
  666.0 27.9 reduce-scatter.22
  696.2 27.9 reduce-scatter.20
  726.9 27.9 reduce-scatter.16
  759.0 59.8 all-reduce.39
where the time goes:
time: 842 us; the launch traced here: 833 us
  matrix products  284 us (34%)
  local copies, waits for them, and re-layouts  209 us (25%)
  blocking collectives  174 us (21%)
  waiting for transfers between devices  107 us (13%)
  other arithmetic  39.9 us (5%)
  between operations  17.7 us (2%)
    reshape x16, local copies, waits for them, and re-layouts, head_split(): return rows.reshape(num_images, SEQ, HEADS, HEAD_DIM)  91.8 us
    psum x1, waiting for transfers between devices, owners_then_replicas(): lax.psum(shares[2].astype(jnp.bfloat16), 'rep').astype(jnp.float32)  59.3 us
    all_gather x2, blocking collectives, fetch_forward(): lax.all_gather(params[2][layer_index], 'grp', axis=0, tiled=True)  51.7 us
    dot_general x8, matrix products, back_dot(): lax.dot_general(grad_rows, weight, (((1,), (1,)), ((), ())), preferred_el...  47.9 us
    unnamed x2, blocking collectives  42.8 us
    dot_general x8, matrix products, weight_grad(): lax.dot_general(left, right, (((0,), (0,)), ((), ())), preferred_element_...  42.3 us
    dot_general x2, matrix products, layer_backward(): jnp.einsum('nhqk,nkhd->nqhd', score_grad, head_split(key_rows, num_images...  41.3 us
    dot_general x2, matrix products, layer_backward(): jnp.einsum('nhqk,nqhd->nkhd', score_grad, head_split(query_rows, num_imag...  37.3 us
  transfers between devices with their start and end apart: 13, of which 3 were waited for; matrix products, arithmetic and copies ran while one was open for 40% of the time, Pallas kernels for 0%

commit v1 on v0

v1 whole, which is shorter than its diff:
```python
import functools

import jax
import jax.numpy as jnp
from jax import lax
from jax.experimental import pallas as pl
from jax.experimental.pallas import tpu as pltpu
from jax.sharding import PartitionSpec as P

HEAD_DIM = 64
PAIR = 2 * HEAD_DIM
EPS = 1e-06
INV_ROOT_TWO = 0.7071067811865476
INV_ROOT_TAU = 0.3989422804014327
MASKED = -1e30
F32 = jnp.float32
BF16 = jnp.bfloat16

G1, B1, QB, VB, PB, G2, B2, DB = range(8)


def dot(left, right):
    return jnp.dot(left, right, preferred_element_type=F32)


def dot_nt(left, right):
    return lax.dot_general(
        left, right, (((1,), (1,)), ((), ())), preferred_element_type=F32
    )


def col_sum(rows):
    return jnp.sum(rows, axis=0, keepdims=True)


def norm(rows):
    mean = jnp.mean(rows, axis=-1, keepdims=True)
    centered = rows - mean
    inv = lax.rsqrt(jnp.mean(centered * centered, axis=-1, keepdims=True) + EPS)
    return centered * inv, inv


def norm_backward(grad, normed, inv, gain):
    scaled = grad * gain
    return inv * (
        scaled
        - jnp.mean(scaled, axis=-1, keepdims=True)
        - normed * jnp.mean(scaled * normed, axis=-1, keepdims=True)
    )


def attn_forward(qkv, keep, image, seq, pad):
    width = qkv.shape[1] // 3
    base = image * pad
    rows = pl.ds(base, pad)
    value_t = qkv[rows, pl.ds(2 * width, width)].T
    lane = lax.broadcasted_iota(jnp.int32, (1, PAIR), 1)
    halves = [(lane < HEAD_DIM).astype(F32).astype(BF16), (lane >= HEAD_DIM).astype(F32).astype(BF16)]
    full = seq // 8 * 8
    for pair in range(width // PAIR):
        queries = qkv[rows, pl.ds(pair * PAIR, PAIR)]
        keys = qkv[rows, pl.ds(width + pair * PAIR, PAIR)]
        for half in range(2):
            head = 2 * pair + half
            scores = dot_nt(keys * halves[half], queries)
            parts = [scores[:full]]
            if full < seq:
                tail = scores[full : full + 8]
                row = lax.broadcasted_iota(jnp.int32, tail.shape, 0)
                parts.append(jnp.where(row < seq - full, tail, MASKED))
            scores = jnp.concatenate(parts, axis=0)
            top = jnp.max(scores, axis=0, keepdims=True)
            raised = jnp.exp(scores - top)
            probs = raised * (1.0 / col_sum(raised))
            rest = pad - probs.shape[0]
            if rest:
                probs = jnp.concatenate([probs, jnp.zeros((rest, pad), F32)], axis=0)
            keep["probs"][image, head] = probs
            context = dot(value_t[head * HEAD_DIM : (head + 1) * HEAD_DIM], probs.astype(BF16))
            keep["context"][image, pl.ds(head * HEAD_DIM, HEAD_DIM), :] = context.astype(BF16)


def layer_forward(hidden, weights, vecs, up_bias, keep, images, seq, pad):
    w_qkv, w_proj, w_up, w_down = weights
    width = hidden.shape[1]
    normed, _ = norm(hidden)
    rows_in = (normed * vecs[G1 : G1 + 1] + vecs[B1 : B1 + 1]).astype(BF16)
    qkv = keep["qkv"]
    projected = dot(rows_in, w_qkv[...])
    qkv[:, :width] = (projected[:, :width] + vecs[QB : QB + 1]).astype(BF16) * jnp.asarray(
        HEAD_DIM**-0.5, BF16
    )
    qkv[:, width : 2 * width] = projected[:, width : 2 * width].astype(BF16)
    qkv[:, 2 * width :] = (projected[:, 2 * width :] + vecs[VB : VB + 1]).astype(BF16)
    for image in range(images):
        attn_forward(qkv, keep, image, seq, pad)
    context = jnp.concatenate([keep["context"][image].T for image in range(images)], axis=0)
    mixed = hidden + dot(context, w_proj[...]) + vecs[PB : PB + 1]
    keep["mixed"][...] = mixed
    normed, _ = norm(mixed)
    rows_mid = (normed * vecs[G2 : G2 + 1] + vecs[B2 : B2 + 1]).astype(BF16)
    upward = dot(rows_mid, w_up[...]) + up_bias[...]
    cumul = 0.5 * (1.0 + lax.erf(upward * INV_ROOT_TWO))
    keep["active"][...] = (upward * cumul).astype(BF16)
    slope = cumul + upward * jnp.exp(-0.5 * upward * upward) * INV_ROOT_TAU
    keep["slope"][...] = slope.astype(keep["slope"].dtype)
    return mixed + dot(keep["active"][...], w_down[...]) + vecs[DB : DB + 1]


def attn_backward(qkv, keep, context_grad, joint, vec_grads, image, pad):
    width = qkv.shape[1] // 3
    rows = pl.ds(image * pad, pad)
    keys_t = qkv[rows, pl.ds(width, width)].T
    lane = lax.broadcasted_iota(jnp.int32, (1, PAIR), 1)
    low = lax.broadcasted_iota(jnp.int32, (pad, PAIR), 1) < HEAD_DIM
    halves = [(lane < HEAD_DIM).astype(F32).astype(BF16), (lane >= HEAD_DIM).astype(F32).astype(BF16)]
    query_parts = []
    for pair in range(width // PAIR):
        queries = qkv[rows, pl.ds(pair * PAIR, PAIR)]
        values = qkv[rows, pl.ds(2 * width + pair * PAIR, PAIR)]
        ctx = context_grad[rows, pl.ds(pair * PAIR, PAIR)]
        key_parts, value_parts = [], []
        for half in range(2):
            head = 2 * pair + half
            probs = keep["probs"][image, head]
            prob_grad = dot_nt(values * halves[half], ctx)
            value_parts.append(dot(probs.astype(BF16), ctx))
            row_dot = col_sum(probs * prob_grad)
            score_grad = (probs * (prob_grad - row_dot)).astype(BF16)
            key_parts.append(dot(score_grad, queries))
            query_parts.append(dot(keys_t[head * HEAD_DIM : (head + 1) * HEAD_DIM], score_grad))
        key_grad = jnp.where(low, key_parts[0], key_parts[1])
        value_grad = jnp.where(low, value_parts[0], value_parts[1])
        joint[rows, pl.ds(width + pair * PAIR, PAIR)] = key_grad.astype(BF16)
        joint[rows, pl.ds(2 * width + pair * PAIR, PAIR)] = value_grad.astype(BF16)
        vec_grads[VB : VB + 1, pl.ds(pair * PAIR, PAIR)] += col_sum(value_grad)
    query_grad = jnp.concatenate(query_parts, axis=0).T * HEAD_DIM**-0.5
    joint[rows, pl.ds(0, width)] = query_grad.astype(BF16)
    vec_grads[QB : QB + 1, :] += col_sum(query_grad)


def layer_backward(out_grad, hidden, weights, vecs, keep, acc, images, pad):
    w_qkv, w_proj, w_up, w_down = weights
    g_qkv, g_proj, g_up, g_down, vec_grads, up_bias_grad, joint, context_grad = acc
    rounded = out_grad.astype(BF16)
    vec_grads[DB : DB + 1, :] += col_sum(out_grad)
    g_down[...] += dot(rounded.T, keep["active"][...])
    up_grad = dot_nt(rounded, w_down[...]) * keep["slope"][...].astype(F32)
    up_bias_grad[...] += col_sum(up_grad)
    up_rounded = up_grad.astype(BF16)
    mixed = keep["mixed"][...]
    normed, inv = norm(mixed)
    gain = vecs[G2 : G2 + 1]
    rows_mid = (normed * gain + vecs[B2 : B2 + 1]).astype(BF16)
    g_up[...] += dot(rows_mid.T, up_rounded)
    mid_grad = dot_nt(up_rounded, w_up[...])
    vec_grads[G2 : G2 + 1, :] += col_sum(mid_grad * normed)
    vec_grads[B2 : B2 + 1, :] += col_sum(mid_grad)
    mixed_grad = out_grad + norm_backward(mid_grad, normed, inv, gain)
    vec_grads[PB : PB + 1, :] += col_sum(mixed_grad)
    mixed_rounded = mixed_grad.astype(BF16)
    part = g_proj[...]
    for image in range(images):
        part += dot(keep["context"][image], mixed_rounded[image * pad : (image + 1) * pad])
    g_proj[...] = part
    context_grad[...] = dot_nt(mixed_rounded, w_proj[...]).astype(BF16)
    for image in range(images):
        attn_backward(keep["qkv"], keep, context_grad, joint, vec_grads, image, pad)
    normed, inv = norm(hidden)
    gain = vecs[G1 : G1 + 1]
    rows_in = (normed * gain + vecs[B1 : B1 + 1]).astype(BF16)
    g_qkv[...] += dot(rows_in.T, joint[...])
    in_grad = dot_nt(joint[...], w_qkv[...])
    vec_grads[G1 : G1 + 1, :] += col_sum(in_grad * normed)
    vec_grads[B1 : B1 + 1, :] += col_sum(in_grad)
    return mixed_grad + norm_backward(in_grad, normed, inv, gain)


def load_padded(ref, buf, pad):
    images, seq, width = ref.shape
    for image in range(images):
        buf[pl.ds(image * pad, seq), :] = ref[image].astype(F32)
        if pad > seq:
            buf[pl.ds(image * pad + seq, pad - seq), :] = jnp.zeros((pad - seq, width), F32)


def store_images(ref, rows, pad):
    images, seq, _ = ref.shape
    for image in range(images):
        ref[image] = rows[image * pad : image * pad + seq].astype(ref.dtype)


KEEP = ("qkv", "probs", "context", "mixed", "active", "slope")


def keep_shapes(images, pad, width, hidden_width):
    heads = width // HEAD_DIM
    return {
        "qkv": ((images * pad, 3 * width), BF16),
        "probs": ((images, heads, pad, pad), F32),
        "context": ((images, width, pad), BF16),
        "mixed": ((images * pad, width), F32),
        "active": ((images * pad, hidden_width), BF16),
        "slope": ((images * pad, hidden_width), F32),
    }


def init_grads(acc):
    @pl.when(pl.program_id(0) == 0)
    def _():
        for ref in acc[:6]:
            ref[...] = jnp.zeros_like(ref)


def flush_grads(acc, outs):
    @pl.when(pl.program_id(0) == pl.num_programs(0) - 1)
    def _():
        g_qkv, g_proj, g_up, g_down, vec_grads, up_bias_grad = acc[:6]
        outs[0][...] = g_qkv[...].astype(BF16)
        outs[1][...] = g_proj[...].astype(BF16)
        outs[2][...] = g_up[...].astype(BF16)
        outs[3][...] = g_down[...].astype(BF16).T
        outs[4][...] = vec_grads[...]
        outs[5][...] = up_bias_grad[...]


def first_kernel(sizes, *refs):
    group, seq, pad = sizes
    images, w0, w1, w2, w3, vecs, up_bias, out = refs[:8]
    keep = dict(zip(KEEP, refs[8:14]))
    (buf,) = refs[14:]
    load_padded(images, buf, pad)
    out[...] = layer_forward(
        buf[...], (w0, w1, w2, w3), vecs, up_bias, keep, group, seq, pad
    )


def middle_kernel(sizes, *refs):
    group, seq, pad = sizes
    hidden, cotangent, w0, w1, w2, w3, vecs, up_bias, encoded, flowing = refs[:10]
    outs = refs[10:16]
    keep = dict(zip(KEEP, refs[16:22]))
    acc = refs[22:30]
    (buf,) = refs[30:]
    weights = (w0, w1, w2, w3)
    init_grads(acc)
    result = layer_forward(hidden[...], weights, vecs, up_bias, keep, group, seq, pad)
    store_images(encoded, result, pad)
    load_padded(cotangent, buf, pad)
    flowing[...] = layer_backward(buf[...], hidden[...], weights, vecs, keep, acc, group, pad)
    flush_grads(acc, outs)


def last_kernel(sizes, *refs):
    group, seq, pad = sizes
    flowing, images, w0, w1, w2, w3, vecs = refs[:7]
    keep = dict(zip(KEEP, refs[7:13]))
    images_grad = refs[13]
    outs = refs[14:20]
    acc = refs[20:28]
    (buf,) = refs[28:]
    init_grads(acc)
    load_padded(images, buf, pad)
    result = layer_backward(
        flowing[...], buf[...], (w0, w1, w2, w3), vecs, keep, acc, group, pad
    )
    store_images(images_grad, result, pad)
    flush_grads(acc, outs)


def whole(shape):
    return pl.BlockSpec(shape, lambda i: (0,) * len(shape), pipeline_mode=pl.Buffered(1))


def rows_spec(shape, steps):
    return pl.BlockSpec(
        (shape[0] // steps,) + tuple(shape[1:]), lambda i: (i,) + (0,) * (len(shape) - 1)
    )


class Plan:
    def __init__(self, images_shape, hidden_width):
        self.count, self.seq, self.width = images_shape
        self.hidden_width = hidden_width
        self.pad = -(-self.seq // 16) * 16
        self.group = 2 if self.count % 2 == 0 else 1
        self.steps = self.count // self.group
        self.rows = self.count * self.pad
        self.keep = keep_shapes(self.count, self.pad, self.width, hidden_width)
        self.keep_block = keep_shapes(self.group, self.pad, self.width, hidden_width)
        self.weight_shapes = [
            (self.width, 3 * self.width),
            (self.width, self.width),
            (self.width, hidden_width),
            (hidden_width, self.width),
        ]
        self.sizes = (self.group, self.seq, self.pad)
        block_rows = self.group * self.pad
        self.buffer = pltpu.VMEM((block_rows, self.width), F32)
        self.acc = [
            pltpu.VMEM(self.weight_shapes[0], F32),
            pltpu.VMEM(self.weight_shapes[1], F32),
            pltpu.VMEM(self.weight_shapes[2], F32),
            pltpu.VMEM((self.width, hidden_width), F32),
            pltpu.VMEM((8, self.width), F32),
            pltpu.VMEM((1, hidden_width), F32),
            pltpu.VMEM((block_rows, 3 * self.width), BF16),
            pltpu.VMEM((block_rows, self.width), BF16),
        ]
        self.grad_shapes = [jax.ShapeDtypeStruct(s, BF16) for s in self.weight_shapes] + [
            jax.ShapeDtypeStruct((8, self.width), F32),
            jax.ShapeDtypeStruct((1, hidden_width), F32),
        ]
        self.params = pltpu.CompilerParams(
            dimension_semantics=("arbitrary",), vmem_limit_bytes=60 * 2**20
        )

    def image_spec(self):
        return rows_spec((self.count, self.seq, self.width), self.steps)

    def state_spec(self):
        return rows_spec((self.rows, self.width), self.steps)

    def param_specs(self):
        return [whole(s) for s in self.weight_shapes] + [
            whole((8, self.width)),
            whole((1, self.hidden_width)),
        ]

    def keep_specs(self):
        return [rows_spec(self.keep[k][0], self.steps) for k in KEEP]

    def grad_specs(self):
        return [whole(s.shape) for s in self.grad_shapes]

    def cost(self, layers):
        rows, width, hidden = self.count * self.seq, self.width, self.hidden_width
        flops = 2 * rows * width * (4 * width + 2 * hidden) * layers
        return pl.CostEstimate(
            flops=int(flops), bytes_accessed=int(40 * 2**20), transcendentals=0
        )

    def first(self, images, weights, vecs, up_bias):
        state = jax.ShapeDtypeStruct((self.rows, self.width), F32)
        keeps = [jax.ShapeDtypeStruct(*self.keep[k]) for k in KEEP]
        out = pl.pallas_call(
            functools.partial(first_kernel, self.sizes),
            name="layer_first",
            out_shape=[state] + keeps,
            grid=(self.steps,),
            in_specs=[self.image_spec()] + self.param_specs(),
            out_specs=[self.state_spec()] + self.keep_specs(),
            scratch_shapes=[self.buffer],
            compiler_params=self.params,
            cost_estimate=self.cost(1),
        )(images, *weights, vecs, up_bias)
        return out[0], out[1:]

    def middle(self, hidden, cotangent, weights, vecs, up_bias):
        state = jax.ShapeDtypeStruct((self.rows, self.width), F32)
        out = pl.pallas_call(
            functools.partial(middle_kernel, self.sizes),
            name="layer_middle",
            out_shape=[jax.ShapeDtypeStruct(cotangent.shape, BF16), state] + self.grad_shapes,
            grid=(self.steps,),
            in_specs=[self.state_spec(), self.image_spec()] + self.param_specs(),
            out_specs=[self.image_spec(), self.state_spec()] + self.grad_specs(),
            scratch_shapes=[pltpu.VMEM(*self.keep_block[k]) for k in KEEP]
            + self.acc
            + [self.buffer],
            compiler_params=self.params,
            cost_estimate=self.cost(3),
        )(hidden, cotangent, *weights, vecs, up_bias)
        return out[0], out[1], out[2:]

    def last(self, flowing, images, weights, vecs, keeps):
        out = pl.pallas_call(
            functools.partial(last_kernel, self.sizes),
            name="layer_last",
            out_shape=[jax.ShapeDtypeStruct(images.shape, BF16)] + self.grad_shapes,
            grid=(self.steps,),
            in_specs=[self.state_spec(), self.image_spec()]
            + self.param_specs()[:5]
            + self.keep_specs(),
            out_specs=[self.image_spec()] + self.grad_specs(),
            scratch_shapes=self.acc + [self.buffer],
            compiler_params=self.params,
            cost_estimate=self.cost(2),
        )(flowing, images, *weights, vecs, *keeps)
        return out[0], out[1:]


def reduce_weights(grads):
    shares = [
        lax.psum_scatter(g, "grp", scatter_dimension=0, tiled=True) for g in grads
    ]
    return [lax.psum(s, "rep").astype(F32) for s in shares]


def on_device(
    images,
    cotangent,
    ln1_gain,
    ln1_bias,
    w_qkv,
    q_bias,
    v_bias,
    w_proj,
    proj_bias,
    ln2_gain,
    ln2_bias,
    w_up,
    up_bias,
    w_down,
    down_bias,
):
    groups = lax.axis_size("grp")
    layers, part = ln1_gain.shape
    width = part * groups
    hidden_part = up_bias.shape[1]
    plan = Plan(images.shape, hidden_part * groups)
    vectors = [ln1_gain, ln1_bias, q_bias, v_bias, proj_bias, ln2_gain, ln2_bias, down_bias]
    packed = jnp.concatenate(vectors + [up_bias], axis=1)
    packed = lax.all_gather(packed, "grp", axis=0, tiled=False)
    vecs = packed[:, :, : 8 * part].reshape(groups, layers, 8, part)
    vecs = vecs.transpose(1, 2, 0, 3).reshape(layers, 8, width).astype(F32)
    up_vecs = packed[:, :, 8 * part :].transpose(1, 0, 2).reshape(layers, 1, -1).astype(F32)
    weights = [
        [
            lax.all_gather(w[layer], "grp", axis=0, tiled=True)
            for w in (w_qkv, w_proj, w_up, w_down)
        ]
        for layer in range(layers)
    ]
    hidden, keeps = plan.first(images, weights[0], vecs[0], up_vecs[0])
    encoded, flowing, grads1 = plan.middle(hidden, cotangent, weights[1], vecs[1], up_vecs[1])
    shares1 = reduce_weights(grads1[:4])
    images_grad, grads0 = plan.last(flowing, images, weights[0], vecs[0], keeps)
    shares0 = reduce_weights(grads0[:4])
    small = jnp.stack([jnp.concatenate([g[4].reshape(-1), g[5].reshape(-1)]) for g in (grads0, grads1)])
    small = lax.psum(small, ("rep", "grp"))
    me = lax.axis_index("grp")
    vec_out = lax.dynamic_slice_in_dim(
        small[:, : 8 * width].reshape(layers, 8, width), me * part, part, axis=2
    )
    up_out = lax.dynamic_slice_in_dim(small[:, 8 * width :], me * hidden_part, hidden_part, axis=1)
    full = [jnp.stack([a, b]) for a, b in zip(shares0, shares1)]
    return (
        encoded,
        images_grad,
        vec_out[:, G1],
        vec_out[:, B1],
        full[0],
        vec_out[:, QB],
        vec_out[:, VB],
        full[1],
        vec_out[:, PB],
        vec_out[:, G2],
        vec_out[:, B2],
        full[2],
        up_out,
        full[3],
        vec_out[:, DB],
    )


def solution(mesh):
    batch = P(("rep", "grp"), None, None)
    vector = P(None, "grp")
    matrix = P(None, "grp", None)
    params = (
        vector,
        vector,
        matrix,
        vector,
        vector,
        matrix,
        vector,
        vector,
        vector,
        matrix,
        vector,
        matrix,
        vector,
    )
    specs = (batch, batch) + params
    return jax.shard_map(
        on_device, mesh=mesh, in_specs=specs, out_specs=specs, check_vma=False
    )
```

time: 842 us -> 574 us (0.68); the launches traced: 833 us -> 573 us
  matrix products: 284 us -> 0 us
  local copies, waits for them, and re-layouts: 209 us -> 6.53 us
  Pallas kernels: 0 us -> 155 us
  waiting for transfers between devices: 107 us -> 247 us
  other arithmetic: 39.9 us -> 5.12 us
  blocking collectives: 174 us -> 145 us
    dot_general x34 -> x0, matrix products: 262 us -> none  [the longest x8 47.9 us: back_dot(): lax.dot_general(grad_rows, weight, (((1,), (1,)), ((), ())), preferred_el...]
    reduce_scatter x8, waiting for transfers between devices: 46.5 us -> 210 us  [reduce_weights(): lax.psum_scatter(g, 'grp', scatter_dimension=0, tiled=True)]
    pallas_call x0 -> x3, Pallas kernels: none -> 155 us  [the longest x1 72.1 us: middle(): pl.pallas_call(functools.partial(middle_kernel, self.sizes), name='layer_...]
    reshape x25 -> x2, local copies, waits for them, and re-layouts: 133 us -> 0.01 us  [on_device(): g[4].reshape(-1)]
    unnamed x2 -> x0, blocking collectives: 42.8 us -> none
    psum x1, waiting for transfers between devices: 59.3 us -> 23.5 us  [reduce_weights(): return [lax.psum(s, 'rep').astype(F32) for s in shares]]
    sub x2 -> x0, matrix products: 22.1 us -> none  [layer_forward(): attn_probs = (jnp.exp(scores - row_max) / row_total).astype(jnp.bfloat16)]
    unnamed x227 -> x44, local copies, waits for them, and re-layouts: 22.1 us -> 0.09 us
  transfers between devices with their start and end apart: 13 -> 13, of which waited for: 3 -> 10; matrix products, arithmetic and copies ran while one was open for 40% -> 1% of each run, Pallas kernels for 0% -> 6%
where the time goes in v1:
time: 574 us; the launch traced here: 573 us
  waiting for transfers between devices  247 us (43%)
  Pallas kernels  155 us (27%)
  blocking collectives  145 us (25%)
  between operations  14.3 us (2%)
  local copies, waits for them, and re-layouts  6.53 us (1%)
    reduce_scatter x8, waiting for transfers between devices, reduce_weights(): lax.psum_scatter(g, 'grp', scatter_dimension=0, tiled=True)  210 us
    all_gather x4, blocking collectives, on_device(): lax.all_gather(w[layer], 'grp', axis=0, tiled=True)  90.5 us
    pallas_call x1, Pallas kernels, middle(): pl.pallas_call(functools.partial(middle_kernel, self.sizes), name='layer_...  72.1 us
    pallas_call x1, Pallas kernels, last(): pl.pallas_call(functools.partial(last_kernel, self.sizes), name='layer_la...  48.6 us
    psum x1, blocking collectives, on_device(): small = lax.psum(small, ('rep', 'grp'))  39.1 us
    pallas_call x1, Pallas kernels, first(): pl.pallas_call(functools.partial(first_kernel, self.sizes), name='layer_f...  34.4 us
    psum x1, waiting for transfers between devices, reduce_weights(): return [lax.psum(s, 'rep').astype(F32) for s in shares]  23.5 us
    all_gather x1, blocking collectives, on_device(): packed = lax.all_gather(packed, 'grp', axis=0, tiled=False)  15 us
  transfers between devices with their start and end apart: 13, of which 10 were waited for; matrix products, arithmetic and copies ran while one was open for 1% of the time, Pallas kernels for 6%

profile of v1, /device:TPU:0, one launch (start us, length us, event | category | flops | bytes accessed | tf_op | source)
XLA Modules:
  0.0 573.3 jit_solution(17075920840989146931)
XLA Ops:
  7.3 2.0 fusion.9
  9.5 0.9 fusion.8
  11.9 15.0 %all-gather.9 = bf16[4,2,1152]{2,1,0:T(2,128)(2,1)S(1)} all-gather(bf16[1,2,1152]{2,1,0:T(2,128)(2,1)S(1)} %bitcast.57), channel_id=6, replica_groups=mesh['rep'=8,'grp'=4] {'grp'}, dimensions={0}, use_global_device_ids=true | all-gather | bytes 23040 | tf_op jit(solution)/shard_map/all_gather | solution.py:424
  27.8 17.6 %all-gather.1 = bf16[1,384,384]{2,1,0:T(8,128)(2,1)} all-gather(bf16[1,96,384]{2,1,0:T(8,128)(2,1)S(1)} %get-tuple-element.74), channel_id=3, replica_groups=mesh['rep'=8,'grp'=4] {'grp'}, dimensions={1}, use_global_device_ids=true | all-gather | bytes 368640 | tf_op jit(solution)/shard_map/all_gather | solution.py:430
  46.7 16.1 %all-gather.6 = bf16[1,384,384]{2,1,0:T(8,128)(2,1)} all-gather(bf16[1,96,384]{2,1,0:T(8,128)(2,1)S(1)} %get-tuple-element.73), channel_id=8, replica_groups=mesh['rep'=8,'grp'=4] {'grp'}, dimensions={1}, use_global_device_ids=true | all-gather | bytes 368640 | tf_op jit(solution)/shard_map/all_gather | solution.py:430
  62.8 31.9 %all-gather = bf16[1,384,1152]{2,1,0:T(8,128)(2,1)} all-gather(bf16[1,96,1152]{2,1,0:T(8,128)(2,1)S(1)} %get-tuple-element.72), channel_id=2, replica_groups=mesh['rep'=8,'grp'=4] {'grp'}, dimensions={1}, use_global_device_ids=true | all-gather | bytes 1105920 | tf_op jit(solution)/shard_map/all_gather | solution.py:430
  94.8 24.8 %all-gather.5 = bf16[1,384,1152]{2,1,0:T(8,128)(2,1)} all-gather(bf16[1,96,1152]{2,1,0:T(8,128)(2,1)S(1)} %get-tuple-element.71), channel_id=7, replica_groups=mesh['rep'=8,'grp'=4] {'grp'}, dimensions={1}, use_global_device_ids=true | all-gather | bytes 1105920 | tf_op jit(solution)/shard_map/all_gather | solution.py:430
  119.6 34.4 %layer_first.1 = (f32[2080,384]{1,0:T(8,128)}, bf16[2080,1152]{1,0:T(8,128)(2,1)}, f32[10,6,208,208]{3,2,1,0:T(8,128)}, bf16[10,384,208]{2,1,0:T(8,128)(2,1)}, f...) custom-call(bf16[10,197,384]{2,1,0:T(8,128)(2,1)} %refs_1_.3, bf16[384,1152]{1,0:T(8,128)(2,1)} %bitcast.41, ...), custom_call_target="tpu_custom_call" | custom-call | flops 6971719680 | bytes 41943040 | tf_op jit(solution)/shard_map/layer_first/pallas_call | solution.py:346
  154.1 7.8 %all-gather.21.cloned.1.call-done = bf16[1,1536,384]{2,1,0:T(8,128)(2,1)} async-done(((bf16[1,384,384]{2,1,0:T(8,128)(2,1)}), bf16[1,1536,384]{2,1,0:T(8,128)(2,1)}) %all-gather.21.cloned.1.call-update) | async-done | bytes 1179664 | tf_op jit(solution)/shard_map/all_gather | solution.py:430
  161.9 72.1 %layer_middle.1 = (bf16[10,197,384]{2,1,0:T(8,128)(2,1)}, f32[2080,384]{1,0:T(8,128)}, bf16[384,1152]{1,0:T(8,128)(2,1)}, bf16[384,384]{1,0:T(8,128)(2,1)}, bf16...) custom-call(f32[2080,384]{1,0:T(8,128)} %get-tuple-element.37.refs_0_, ...), custom_call_target="tpu_custom_call" | custom-call | flops 20915159040 | bytes 41943040 | tf_op jit(solution)/shard_map/layer_middle/pallas_call | solution.py:361
  234.0 48.6 %layer_last.1 = (bf16[10,197,384]{2,1,0:T(8,128)(2,1)}, bf16[384,1152]{1,0:T(8,128)(2,1)}, bf16[384,384]{1,0:T(8,128)(2,1)}, bf16[384,1536]{1,0:T(8,128)(2,1)}, ...) custom-call(f32[2080,384]{1,0:T(8,128)} %get-tuple-element.39.refs_0_, ...), custom_call_target="tpu_custom_call" | custom-call | flops 13943439360 | bytes 41943040 | tf_op jit(solution)/shard_map/layer_last/pallas_call | solution.py:377
  287.6 14.6 %reduce-scatter.13.cloned.1.call-done = bf16[96,384]{1,0:T(8,128)(2,1)} async-done(((bf16[384,384]{1,0:T(8,128)(2,1)}), bf16[96,384]{1,0:T(8,128)(2,1)}) %reduce-scatter.13.cloned.1.call-update) | async-done | bytes 73744 | tf_op jit(solution)/shard_map/reduce_scatter | solution.py:395
  302.2 21.2 %reduce-scatter.15.cloned.1.call-done = bf16[96,384]{1,0:T(8,128)(2,1)} async-done(((bf16[384,384]{1,0:T(8,128)(2,1)}), bf16[96,384]{1,0:T(8,128)(2,1)}) %reduce-scatter.15.cloned.1.call-update) | async-done | bytes 73744 | tf_op jit(solution)/shard_map/reduce_scatter | solution.py:395
  323.4 25.3 %reduce-scatter.9.cloned.1.call-done = bf16[96,1152]{1,0:T(8,128)(2,1)} async-done(((bf16[384,1152]{1,0:T(8,128)(2,1)}), bf16[96,1152]{1,0:T(8,128)(2,1)}) %reduce-scatter.9.cloned.1.call-update) | async-done | bytes 221200 | tf_op jit(solution)/shard_map/reduce_scatter | solution.py:395
  348.7 26.7 %reduce-scatter.11.cloned.1.call-done = bf16[96,1152]{1,0:T(8,128)(2,1)} async-done(((bf16[384,1152]{1,0:T(8,128)(2,1)}), bf16[96,1152]{1,0:T(8,128)(2,1)}) %reduce-scatter.11.cloned.1.call-update) | async-done | bytes 221200 | tf_op jit(solution)/shard_map/reduce_scatter | solution.py:395
  375.3 30.7 %reduce-scatter.17.cloned.1.call-done = bf16[96,1536]{1,0:T(8,128)(2,1)} async-done(((bf16[384,1536]{1,0:T(8,128)(2,1)}), bf16[96,1536]{1,0:T(8,128)(2,1)}) %reduce-scatter.17.cloned.1.call-update) | async-done | bytes 294928 | tf_op jit(solution)/shard_map/reduce_scatter | solution.py:395
  406.0 30.1 %reduce-scatter.21.cloned.1.call-done = bf16[384,384]{1,0:T(8,128)(2,1)} async-done(((bf16[1536,384]{1,0:T(8,128)(2,1)}), bf16[384,384]{1,0:T(8,128)(2,1)}) %reduce-scatter.21.cloned.1.call-update) | async-done | bytes 294928 | tf_op jit(solution)/shard_map/reduce_scatter | solution.py:395
  436.2 30.9 %reduce-scatter.19.cloned.1.call-done = bf16[96,1536]{1,0:T(8,128)(2,1)} async-done(((bf16[384,1536]{1,0:T(8,128)(2,1)}), bf16[96,1536]{1,0:T(8,128)(2,1)}) %reduce-scatter.19.cloned.1.call-update) | async-done | bytes 294928 | tf_op jit(solution)/shard_map/reduce_scatter | solution.py:395
  467.0 30.7 %reduce-scatter.23.cloned.1.call-done = bf16[384,384]{1,0:T(8,128)(2,1)} async-done(((bf16[1536,384]{1,0:T(8,128)(2,1)}), bf16[384,384]{1,0:T(8,128)(2,1)}) %reduce-scatter.23.cloned.1.call-update) | async-done | bytes 294928 | tf_op jit(solution)/shard_map/reduce_scatter | solution.py:395
  497.8 39.1 %psum.63 = f32[2,4608]{1,0:T(2,128)S(1)} all-reduce(f32[2,4608]{1,0:T(2,128)S(1)} %pad_maximum_fusion), channel_id=1, replica_groups=mesh['rep'=8,'grp'=4] {'rep','grp'}, use_global_device_ids=true, to_apply=%region_0.0 | all-reduce | flops 9216 | bytes 73728 | tf_op jit(solution)/shard_map/psum | solution.py:441
  538.2 23.5 %all-reduce.3.cloned.1.call-done = (bf16[1,96,1152]{2,1,0:T(8,128)(2,1)}, bf16[1,96,1152]{2,1,0:T(8,128)(2,1)}, bf16[1,96,384]{2,1,0:T(8,128)(2,1)}, bf16[1,96,3...) async-done(((bf16[1,96,1152]{2,1,0:T(8,128)(2,1)}, ...) | async-done | bytes 1769488 | tf_op jit(solution)/shard_map/psum | solution.py:397
  561.7 2.2 maximum_convert_fusion.1
  563.9 1.1 maximum_convert_fusion
  565.8 1.0 maximum_convert_fusion.2
  (98 shorter events, 10.6 us)
Async XLA Ops:
  7.2 4.5 copy-start.14
  7.2 4.5 copy-start.15
  7.2 4.5 copy-start.16
  7.2 4.5 copy-start.17
  7.2 4.5 copy-start.18
  7.2 4.5 copy-start.19
  7.3 4.5 copy-start.20
  7.3 4.5 copy-start.13
  7.3 4.5 copy-start.21
  7.3 112.3 %all-gather.15.cloned.1.call-start = ((), (), s32[]{:S(2)}) async-start(), calls=%async_computation.16 | async-start | bytes 1474560 | tf_op jit(solution)/shard_map/all_gather | solution.py:430
  9.4 18.4 %copy-start.6 = (bf16[2,96,384]{2,1,0:T(8,128)(2,1)S(1)}, bf16[2,96,384]{2,1,0:T(8,128)(2,1)}, u32[]{:S(2)}) copy-start(bf16[2,96,384]{2,1,0:T(8,128)(2,1)} %param.22) | copy-start | bytes 442372
  9.4 53.4 %copy-start.1 = (bf16[2,96,1152]{2,1,0:T(8,128)(2,1)S(1)}, bf16[2,96,1152]{2,1,0:T(8,128)(2,1)}, u32[]{:S(2)}) copy-start(bf16[2,96,1152]{2,1,0:T(8,128)(2,1)} %param.19) | copy-start | bytes 1327108
  9.4 110.2 %all-gather.17.cloned.1.call-start = ((), (), s32[]{:S(2)}) async-start(), calls=%async_computation.17 | async-start | bytes 1474560 | tf_op jit(solution)/shard_map/all_gather | solution.py:430
  10.4 143.7 %all-gather.19.cloned.1.call-start = ((), (), s32[]{:S(2)}) async-start(), calls=%async_computation.18 | async-start | bytes 1474560 | tf_op jit(solution)/shard_map/all_gather | solution.py:430
  11.1 150.8 %all-gather.21.cloned.1.call-start = ((), (), s32[]{:S(2)}) async-start(), calls=%async_computation.19 | async-start | bytes 1474560 | tf_op jit(solution)/shard_map/all_gather | solution.py:430
  11.7 290.5 %reduce-scatter.13.cloned.1.call-start = ((), (), s32[]{:S(2)}) async-start(), calls=%async_computation.10 | async-start | bytes 368640 | tf_op jit(solution)/shard_map/reduce_scatter | solution.py:395
  282.6 40.8 %reduce-scatter.15.cloned.1.call-start = ((), (), s32[]{:S(2)}) async-start(), calls=%async_computation.11 | async-start | bytes 368640 | tf_op jit(solution)/shard_map/reduce_scatter | solution.py:395
  283.2 65.5 %reduce-scatter.9.cloned.1.call-start = ((), (), s32[]{:S(2)}) async-start(), calls=%async_computation.8 | async-start | bytes 1105920 | tf_op jit(solution)/shard_map/reduce_scatter | solution.py:395
  284.0 91.4 %reduce-scatter.11.cloned.1.call-start = ((), (), s32[]{:S(2)}) async-start(), calls=%async_computation.9 | async-start | bytes 1105920 | tf_op jit(solution)/shard_map/reduce_scatter | solution.py:395
  284.7 121.3 %reduce-scatter.17.cloned.1.call-start = ((), (), s32[]{:S(2)}) async-start(), calls=%async_computation.12 | async-start | bytes 1474560 | tf_op jit(solution)/shard_map/reduce_scatter | solution.py:395
  285.5 150.7 %reduce-scatter.21.cloned.1.call-start = ((), (), s32[]{:S(2)}) async-start(), calls=%async_computation.14 | async-start | bytes 1474560 | tf_op jit(solution)/shard_map/reduce_scatter | solution.py:395
  286.1 180.9 %reduce-scatter.19.cloned.1.call-start = ((), (), s32[]{:S(2)}) async-start(), calls=%async_computation.13 | async-start | bytes 1474560 | tf_op jit(solution)/shard_map/reduce_scatter | solution.py:395
  286.8 210.9 %reduce-scatter.23.cloned.1.call-start = ((), (), s32[]{:S(2)}) async-start(), calls=%async_computation.15 | async-start | bytes 1474560 | tf_op jit(solution)/shard_map/reduce_scatter | solution.py:395
  287.4 274.3 %all-reduce.3.cloned.1.call-start = ((), (), s32[]{:S(2)}) async-start(), calls=%async_computation.20 | async-start | bytes 3538944 | tf_op jit(solution)/shard_map/psum | solution.py:397
  (11 other events, 23.9 us)
Sparse Core Ops, SparseCore 0:
  10.2 38.6 all-gather.14
  51.1 43.5 all-gather.16
  96.8 32.6 all-gather.18
  131.5 30.3 all-gather.20
  282.8 19.4 reduce-scatter.12
  304.9 18.4 reduce-scatter.14
  325.7 22.9 reduce-scatter.8
  351.6 23.7 reduce-scatter.10
  377.7 28.3 reduce-scatter.16
  408.2 27.9 reduce-scatter.20
  439.1 27.9 reduce-scatter.18
  469.8 27.9 reduce-scatter.22
  501.8 59.8 all-reduce.2

commit v2 on v1

--- a/solution.py
+++ b/solution.py
@@ -1,4 +1,5 @@
 import functools
+import math
 
 import jax
 import jax.numpy as jnp
@@ -16,7 +17,8 @@
 F32 = jnp.float32
 BF16 = jnp.bfloat16
 
-G1, B1, QB, VB, PB, G2, B2, DB = range(8)
+VECTORS = 8
+G1, B1, QB, VB, PB, G2, B2, DB = range(VECTORS)
 
 
 def dot(left, right):
@@ -80,9 +82,25 @@
             keep["context"][image, pl.ds(head * HEAD_DIM, HEAD_DIM), :] = context.astype(BF16)
 
 
-def layer_forward(hidden, weights, vecs, up_bias, keep, images, seq, pad):
+def split_weights(wide, w_down):
+    width = w_down.shape[1]
+    return (
+        wide.at[:, pl.ds(0, 3 * width)],
+        wide.at[:, pl.ds(3 * width, width)],
+        wide.at[:, pl.ds(4 * width, w_down.shape[0])],
+        w_down,
+    )
+
+
+def up_bias_of(vecs, hidden_width):
+    rows = hidden_width // vecs.shape[1]
+    return jnp.concatenate([vecs[VECTORS + i : VECTORS + i + 1] for i in range(rows)], axis=1)
+
+
+def layer_forward(hidden, weights, vecs, keep, images, seq, pad):
     w_qkv, w_proj, w_up, w_down = weights
     width = hidden.shape[1]
+    up_bias = up_bias_of(vecs, w_down.shape[0])
     normed, _ = norm(hidden)
     rows_in = (normed * vecs[G1 : G1 + 1] + vecs[B1 : B1 + 1]).astype(BF16)
     qkv = keep["qkv"]
@@ -99,7 +117,7 @@
     keep["mixed"][...] = mixed
     normed, _ = norm(mixed)
     rows_mid = (normed * vecs[G2 : G2 + 1] + vecs[B2 : B2 + 1]).astype(BF16)
-    upward = dot(rows_mid, w_up[...]) + up_bias[...]
+    upward = dot(rows_mid, w_up[...]) + up_bias
     cumul = 0.5 * (1.0 + lax.erf(upward * INV_ROOT_TWO))
     keep["active"][...] = (upward * cumul).astype(BF16)
     slope = cumul + upward * jnp.exp(-0.5 * upward * upward) * INV_ROOT_TAU
@@ -216,35 +234,43 @@
     @pl.when(pl.program_id(0) == pl.num_programs(0) - 1)
     def _():
         g_qkv, g_proj, g_up, g_down, vec_grads, up_bias_grad = acc[:6]
-        outs[0][...] = g_qkv[...].astype(BF16)
-        outs[1][...] = g_proj[...].astype(BF16)
-        outs[2][...] = g_up[...].astype(BF16)
-        outs[3][...] = g_down[...].astype(BF16).T
-        outs[4][...] = vec_grads[...]
-        outs[5][...] = up_bias_grad[...]
+        wide, down, vecs = outs
+        g_qkv_out, g_proj_out, g_up_out, g_down_out = split_weights(wide, down)
+        g_qkv_out[...] = g_qkv[...].astype(BF16)
+        g_proj_out[...] = g_proj[...].astype(BF16)
+        g_up_out[...] = g_up[...].astype(BF16)
+        g_down_out[...] = g_down[...].astype(BF16).T
+        width = vecs.shape[1]
+        extra = up_bias_grad.shape[1] // width
+        vecs[:VECTORS, :] = vec_grads[...]
+        for i in range(extra):
+            vecs[VECTORS + i : VECTORS + i + 1, :] = up_bias_grad[:, i * width : (i + 1) * width]
+        rest = vecs.shape[0] - VECTORS - extra
+        if rest:
+            vecs[VECTORS + extra :, :] = jnp.zeros((rest, width), F32)
 
 
 def first_kernel(sizes, *refs):
     group, seq, pad = sizes
-    images, w0, w1, w2, w3, vecs, up_bias, out = refs[:8]
-    keep = dict(zip(KEEP, refs[8:14]))
-    (buf,) = refs[14:]
+    images, wide, down, vecs, out = refs[:5]
+    keep = dict(zip(KEEP, refs[5:11]))
+    (buf,) = refs[11:]
     load_padded(images, buf, pad)
     out[...] = layer_forward(
-        buf[...], (w0, w1, w2, w3), vecs, up_bias, keep, group, seq, pad
+        buf[...], split_weights(wide, down), vecs, keep, group, seq, pad
     )
 
 
 def middle_kernel(sizes, *refs):
     group, seq, pad = sizes
-    hidden, cotangent, w0, w1, w2, w3, vecs, up_bias, encoded, flowing = refs[:10]
-    outs = refs[10:16]
-    keep = dict(zip(KEEP, refs[16:22]))
-    acc = refs[22:30]
-    (buf,) = refs[30:]
-    weights = (w0, w1, w2, w3)
+    hidden, cotangent, wide, down, vecs, encoded, flowing = refs[:7]
+    outs = refs[7:10]
+    keep = dict(zip(KEEP, refs[10:16]))
+    acc = refs[16:24]
+    (buf,) = refs[24:]
+    weights = split_weights(wide, down)
     init_grads(acc)
-    result = layer_forward(hidden[...], weights, vecs, up_bias, keep, group, seq, pad)
+    result = layer_forward(hidden[...], weights, vecs, keep, group, seq, pad)
     store_images(encoded, result, pad)
     load_padded(cotangent, buf, pad)
     flowing[...] = layer_backward(buf[...], hidden[...], weights, vecs, keep, acc, group, pad)
@@ -253,16 +279,16 @@
 
 def last_kernel(sizes, *refs):
     group, seq, pad = sizes
-    flowing, images, w0, w1, w2, w3, vecs = refs[:7]
-    keep = dict(zip(KEEP, refs[7:13]))
-    images_grad = refs[13]
-    outs = refs[14:20]
-    acc = refs[20:28]
-    (buf,) = refs[28:]
+    flowing, images, wide, down, vecs = refs[:5]
+    keep = dict(zip(KEEP, refs[5:11]))
+    images_grad = refs[11]
+    outs = refs[12:15]
+    acc = refs[15:23]
+    (buf,) = refs[23:]
     init_grads(acc)
     load_padded(images, buf, pad)
     result = layer_backward(
-        flowing[...], buf[...], (w0, w1, w2, w3), vecs, keep, acc, group, pad
+        flowing[...], buf[...], split_weights(wide, down), vecs, keep, acc, group, pad
     )
     store_images(images_grad, result, pad)
     flush_grads(acc, outs)
@@ -307,9 +333,14 @@
             pltpu.VMEM((block_rows, 3 * self.width), BF16),
             pltpu.VMEM((block_rows, self.width), BF16),
         ]
-        self.grad_shapes = [jax.ShapeDtypeStruct(s, BF16) for s in self.weight_shapes] + [
-            jax.ShapeDtypeStruct((8, self.width), F32),
-            jax.ShapeDtypeStruct((1, hidden_width), F32),
+        self.vec_rows = -(-(VECTORS + hidden_width // self.width) // 8) * 8
+        self.packed_shapes = [
+            (self.width, 4 * self.width + hidden_width),
+            (hidden_width, self.width),
+        ]
+        self.vec_shape = (self.vec_rows, self.width)
+        self.grad_shapes = [jax.ShapeDtypeStruct(s, BF16) for s in self.packed_shapes] + [
+            jax.ShapeDtypeStruct(self.vec_shape, F32)
         ]
         self.params = pltpu.CompilerParams(
             dimension_semantics=("arbitrary",), vmem_limit_bytes=60 * 2**20
@@ -322,10 +353,7 @@
         return rows_spec((self.rows, self.width), self.steps)
 
     def param_specs(self):
-        return [whole(s) for s in self.weight_shapes] + [
-            whole((8, self.width)),
-            whole((1, self.hidden_width)),
-        ]
+        return [whole(s) for s in self.packed_shapes + [self.vec_shape]]
 
     def keep_specs(self):
         return [rows_spec(self.keep[k][0], self.steps) for k in KEEP]
@@ -340,7 +368,7 @@
             flops=int(flops), bytes_accessed=int(40 * 2**20), transcendentals=0
         )
 
-    def first(self, images, weights, vecs, up_bias):
+    def first(self, images, weights, vecs):
         state = jax.ShapeDtypeStruct((self.rows, self.width), F32)
         keeps = [jax.ShapeDtypeStruct(*self.keep[k]) for k in KEEP]
         out = pl.pallas_call(
@@ -353,10 +381,10 @@
             scratch_shapes=[self.buffer],
             compiler_params=self.params,
             cost_estimate=self.cost(1),
-        )(images, *weights, vecs, up_bias)
+        )(images, *weights, vecs)
         return out[0], out[1:]
 
-    def middle(self, hidden, cotangent, weights, vecs, up_bias):
+    def middle(self, hidden, cotangent, weights, vecs):
         state = jax.ShapeDtypeStruct((self.rows, self.width), F32)
         out = pl.pallas_call(
             functools.partial(middle_kernel, self.sizes),
@@ -370,7 +398,7 @@
             + [self.buffer],
             compiler_params=self.params,
             cost_estimate=self.cost(3),
-        )(hidden, cotangent, *weights, vecs, up_bias)
+        )(hidden, cotangent, *weights, vecs)
         return out[0], out[1], out[2:]
 
     def last(self, flowing, images, weights, vecs, keeps):
@@ -380,7 +408,7 @@
             out_shape=[jax.ShapeDtypeStruct(images.shape, BF16)] + self.grad_shapes,
             grid=(self.steps,),
             in_specs=[self.state_spec(), self.image_spec()]
-            + self.param_specs()[:5]
+            + self.param_specs()
             + self.keep_specs(),
             out_specs=[self.image_spec()] + self.grad_specs(),
             scratch_shapes=self.acc + [self.buffer],
@@ -390,14 +418,328 @@
         return out[0], out[1:]
 
 
-def reduce_weights(grads):
-    shares = [
-        lax.psum_scatter(g, "grp", scatter_dimension=0, tiled=True) for g in grads
+def peers_of(reps):
+    rep = lax.axis_index("rep")
+    cores = 2 if reps % 2 == 0 else 1
+    return rep // cores, lax.rem(rep, cores), cores, reps // cores
+
+
+def greet(targets):
+    barrier = pltpu.get_barrier_semaphore()
+    for target in targets:
+        pl.semaphore_signal(
+            barrier, inc=1, device_id=target, device_id_type=pl.DeviceIdType.MESH
+        )
+    pl.semaphore_wait(barrier, len(targets))
+
+
+def send(src, dst, sems, at, target):
+    copy = pltpu.make_async_remote_copy(
+        src_ref=src,
+        dst_ref=dst,
+        send_sem=sems[0].at[at],
+        recv_sem=sems[1].at[at],
+        device_id=target,
+        device_id_type=pl.DeviceIdType.MESH,
+    )
+    copy.start()
+    return copy
+
+
+class Split:
+    def __init__(self, blocks, columns, cores, chips):
+        self.by_columns = columns % (128 * cores) == 0
+        self.columns = columns // cores if self.by_columns else columns
+        self.blocks = blocks if self.by_columns else blocks // cores
+        self.pieces = math.gcd(self.blocks, chips)
+        self.run = self.blocks // self.pieces
+
+    def half(self, ref, core, shard=slice(None)):
+        if self.by_columns:
+            start = pl.multiple_of(core * self.columns, 128)
+            return ref.at[shard, :, :, pl.ds(start, self.columns)]
+        return ref.at[shard, pl.ds(core * self.blocks, self.blocks)]
+
+    def part(self, ref, core, piece, shard=slice(None)):
+        if self.by_columns:
+            start = pl.multiple_of(core * self.columns, 128)
+            return ref.at[shard, pl.ds(piece * self.run, self.run), :, pl.ds(start, self.columns)]
+        return ref.at[shard, pl.ds(core * self.blocks + piece * self.run, self.run)]
+
+
+def gather_kernel(splits, sizes, *refs):
+    groups, reps = sizes
+    count = len(splits)
+    vec_in, vec_out = refs[count], refs[2 * count + 1]
+    ins, outs = refs[:count], refs[count + 1 : 2 * count + 1]
+    own_sem, vec_sem = refs[2 * count + 2], refs[2 * count + 3]
+    vec_sems, shard_sems, chip_sems, core_sems = (
+        refs[2 * count + 4 + 2 * i : 2 * count + 6 + 2 * i] for i in range(4)
+    )
+    chip, core, cores, chips = peers_of(reps)
+    mine = lax.axis_index("grp")
+    rep = lax.axis_index("rep")
+    shard_peers = [(rep, lax.rem(mine + d, groups)) for d in range(1, groups)]
+    chip_steps = sorted({e for s in splits for e in range(1, s.pieces)})
+
+    def chip_at(split, step):
+        base = chip // split.pieces * split.pieces
+        return base + lax.rem(lax.rem(chip, split.pieces) + step, split.pieces)
+
+    most = max(splits, key=lambda s: s.pieces)
+    chip_peers = [(chip_at(most, e) * cores + core, mine) for e in chip_steps]
+    core_peers = [(chip * cores + 1 - core, mine)] if cores > 1 else []
+    greet(shard_peers + chip_peers + core_peers)
+
+    started = []
+    own, over_shards = [], []
+    for i, split in enumerate(splits):
+        piece = lax.rem(chip, split.pieces)
+        src = split.part(ins[i], core, piece, 0)
+        dst = split.part(outs[i], core, piece, mine)
+        over_shards.append(
+            [send(src, dst, shard_sems, (i, d), t) for d, t in enumerate(shard_peers)]
+        )
+        copy = pltpu.make_async_copy(src, dst, own_sem.at[i])
+        copy.start()
+        own.append(copy)
+        if i == 0:
+            vec_copies = [
+                send(vec_in.at[0], vec_out.at[mine], vec_sems, d, t)
+                for d, t in enumerate(shard_peers)
+            ]
+            vec_own = pltpu.make_async_copy(vec_in.at[0], vec_out.at[mine], vec_sem)
+            vec_own.start()
+    over_chips = []
+    for i, split in enumerate(splits):
+        own[i].wait()
+        for copy in over_shards[i]:
+            copy.wait_recv()
+        piece = lax.rem(chip, split.pieces)
+        block = split.part(outs[i], core, piece)
+        over_chips.append(
+            [
+                send(block, block, chip_sems, (i, e - 1), (chip_at(split, e) * cores + core, mine))
+                for e in range(1, split.pieces)
+            ]
+        )
+    over_cores = []
+    for i, split in enumerate(splits):
+        for copy in over_chips[i]:
+            copy.wait_recv()
+        if cores > 1:
+            block = split.half(outs[i], core)
+            over_cores.append(send(block, block, core_sems, i, core_peers[0]))
+    for copy in over_cores:
+        copy.wait_recv()
+    for copy in vec_copies:
+        copy.wait()
+    vec_own.wait()
+    for copy in sum(over_shards, []) + sum(over_chips, []) + over_cores:
+        copy.wait_send()
+
+
+def dma_pair(*shape):
+    return [pltpu.SemaphoreType.DMA(shape), pltpu.SemaphoreType.DMA(shape)]
+
+
+VMEM_SPEC = pl.BlockSpec(memory_space=pltpu.VMEM)
+
+
+def gather(shards, vec, sizes, collective_id):
+    groups, reps = sizes
+    cores = 2 if reps % 2 == 0 else 1
+    splits = [Split(s.shape[0], s.shape[2], cores, reps // cores) for s in shards]
+    count = len(shards)
+    most = max(s.pieces for s in splits)
+    return pl.pallas_call(
+        functools.partial(gather_kernel, splits, sizes),
+        name="gather_params",
+        out_shape=[jax.ShapeDtypeStruct((groups,) + s.shape, s.dtype) for s in shards]
+        + [jax.ShapeDtypeStruct((groups,) + vec.shape, vec.dtype)],
+        in_specs=[VMEM_SPEC] * (count + 1),
+        out_specs=[VMEM_SPEC] * (count + 1),
+        scratch_shapes=[pltpu.SemaphoreType.DMA((count,)), pltpu.SemaphoreType.DMA]
+        + dma_pair(groups - 1)
+        + dma_pair(count, groups - 1)
+        + dma_pair(count, max(most - 1, 1))
+        + dma_pair(count),
+        compiler_params=pltpu.CompilerParams(
+            collective_id=collective_id, has_side_effects=True, vmem_limit_bytes=40 * 2**20
+        ),
+    )(*[s[None] for s in shards], vec[None])
+
+
+def add_up(first, rest):
+    total = first.astype(F32)
+    for term in rest:
+        total = total + term.astype(F32)
+    return total
+
+
+def reduce_kernel(splits, sizes, *refs):
+    groups, reps = sizes
+    count = len(splits)
+    ins, vec_in = refs[:count], refs[count]
+    outs, vec_out = refs[count + 1 : 2 * count + 1], refs[2 * count + 1]
+    at = 2 * count + 2
+    from_core, core_sum, from_chips, chip_sum, from_shards = (
+        refs[at + i * count : at + (i + 1) * count] for i in range(5)
+    )
+    at += 5 * count
+    vec_parts, vec_held = refs[at], refs[at + 1]
+    at += 2
+    core_sems, chip_sems, shard_sems, spread_sems, join_sems, vec_sems = (
+        refs[at + 2 * i : at + 2 * i + 2] for i in range(6)
+    )
+    chip, core, cores, chips = peers_of(reps)
+    mine = lax.axis_index("grp")
+    rep = lax.axis_index("rep")
+    shard_peers = [(rep, lax.rem(mine + d, groups)) for d in range(1, groups)]
+    chip_ids = [lax.rem(chip + e, chips) for e in range(1, chips)]
+    chip_peers = [(c * cores + core, mine) for c in chip_ids]
+    core_peers = [(chip * cores + 1 - core, mine)] if cores > 1 else []
+    greet(shard_peers + chip_peers + core_peers)
+    sent = []
+    arrivals = []
+    if cores > 1:
+        for i, split in enumerate(splits):
+            arrivals.append(
+                send(split.half(ins[i], 1 - core), from_core[i], core_sems, i, core_peers[0])
+            )
+        vec_core = send(vec_in, vec_parts.at[0], vec_sems, 0, core_peers[0])
+        sent += arrivals + [vec_core]
+    chip_arrivals = []
+    for i, split in enumerate(splits):
+        own = split.half(ins[i], core)[...]
+        if cores > 1:
+            arrivals[i].wait_recv()
+            own = add_up(own, [from_core[i][...]]).astype(BF16)
+        core_sum[i][...] = own
+        copies = []
+        for e, target in enumerate(chip_peers):
+            piece = lax.rem(chip_ids[e], split.pieces)
+            src = core_sum[i].at[:, pl.ds(piece * split.run, split.run)]
+            copies.append(send(src, from_chips[i].at[e], chip_sems, (i, e), target))
+        chip_arrivals.append(copies)
+        sent += copies
+    own = vec_in[...]
+    if cores > 1:
+        vec_core.wait_recv()
+        own = own + vec_parts[0]
+    vec_held[0] = own
+    vec_chip = [
+        send(vec_held.at[0], vec_parts.at[1 + e], vec_sems, 1 + e, t)
+        for e, t in enumerate(chip_peers)
     ]
-    return [lax.psum(s, "rep").astype(F32) for s in shares]
+    sent += vec_chip
+    shard_arrivals = []
+    for i, split in enumerate(splits):
+        piece = lax.rem(chip, split.pieces)
+        own = core_sum[i][:, pl.ds(piece * split.run, split.run)]
+        for copy in chip_arrivals[i]:
+            copy.wait_recv()
+        total = add_up(own, [from_chips[i][e] for e in range(len(chip_peers))])
+        chip_sum[i][...] = total.astype(BF16)
+        copies = [
+            send(
+                chip_sum[i].at[lax.rem(mine + d + 1, groups)],
+                from_shards[i].at[d],
+                shard_sems,
+                (i, d),
+                target,
+            )
+            for d, target in enumerate(shard_peers)
+        ]
+        shard_arrivals.append(copies)
+        sent += copies
+    own = vec_held[0]
+    for e, copy in enumerate(vec_chip):
+        copy.wait_recv()
+        own = own + vec_parts[1 + e]
+    vec_held[1] = own
+    vec_shard = [
+        send(vec_held.at[1], vec_parts.at[chips + d], vec_sems, chips + d, t)
+        for d, t in enumerate(shard_peers)
+    ]
+    sent += vec_shard
+    spreads = []
+    for i, split in enumerate(splits):
+        piece = lax.rem(chip, split.pieces)
+        own = chip_sum[i][mine]
+        for copy in shard_arrivals[i]:
+            copy.wait_recv()
+        total = add_up(own, [from_shards[i][d] for d in range(len(shard_peers))])
+        block = split.part(outs[i], core, piece, 0)
+        block[...] = total.astype(BF16)
+        base = chip // split.pieces * split.pieces
+        copies = []
+        for e in range(1, split.pieces):
+            other = base + lax.rem(piece + e, split.pieces)
+            copies.append(
+                send(block, block, spread_sems, (i, e - 1), (other * cores + core, mine))
+            )
+        spreads.append(copies)
+        sent += copies
+    own = vec_held[1]
+    for d, copy in enumerate(vec_shard):
+        copy.wait_recv()
+        own = own + vec_parts[chips + d]
+    vec_out[...] = own
+    joins = []
+    for i, split in enumerate(splits):
+        for copy in spreads[i]:
+            copy.wait_recv()
+        if cores > 1:
+            block = split.half(outs[i], core, 0)
+            joins.append(send(block, block, join_sems, i, core_peers[0]))
+    for copy in joins:
+        copy.wait_recv()
+    for copy in sent + joins:
+        copy.wait_send()
+
+
+def reduce_grads(grads, vec, sizes, collective_id):
+    groups, reps = sizes
+    cores = 2 if reps % 2 == 0 else 1
+    chips = reps // cores
+    splits = [Split(g.shape[1], g.shape[3], cores, chips) for g in grads]
+    count = len(grads)
+    most = max(s.pieces for s in splits)
+    half = [(groups, s.blocks, 8, s.columns) for s in splits]
+    piece = [(groups, s.run, 8, s.columns) for s in splits]
+    shapes = (
+        half
+        + half
+        + [(chips - 1,) + p for p in piece]
+        + piece
+        + [(groups - 1,) + p[1:] for p in piece]
+    )
+    vec_terms = chips + groups - 1
+    out = pl.pallas_call(
+        functools.partial(reduce_kernel, splits, sizes),
+        name="reduce_grads",
+        out_shape=[jax.ShapeDtypeStruct((1,) + g.shape[1:], BF16) for g in grads]
+        + [jax.ShapeDtypeStruct(vec.shape, F32)],
+        in_specs=[VMEM_SPEC] * (count + 1),
+        out_specs=[VMEM_SPEC] * (count + 1),
+        scratch_shapes=[pltpu.VMEM(s, BF16) for s in shapes]
+        + [pltpu.VMEM((vec_terms,) + vec.shape, F32), pltpu.VMEM((2,) + vec.shape, F32)]
+        + dma_pair(count)
+        + dma_pair(count, chips - 1)
+        + dma_pair(count, groups - 1)
+        + dma_pair(count, max(most - 1, 1))
+        + dma_pair(count)
+        + dma_pair(vec_terms),
+        compiler_params=pltpu.CompilerParams(
+            collective_id=collective_id, has_side_effects=True, vmem_limit_bytes=40 * 2**20
+        ),
+    )(*grads, vec)
+    return [o[0] for o in out[:count]], out[count]
 
 
 def on_device(
+    reps,
     images,
     cotangent,
     ln1_gain,
@@ -415,51 +757,64 @@
     down_bias,
 ):
     groups = lax.axis_size("grp")
+    sizes = (groups, reps)
     layers, part = ln1_gain.shape
     width = part * groups
     hidden_part = up_bias.shape[1]
     plan = Plan(images.shape, hidden_part * groups)
     vectors = [ln1_gain, ln1_bias, q_bias, v_bias, proj_bias, ln2_gain, ln2_bias, down_bias]
-    packed = jnp.concatenate(vectors + [up_bias], axis=1)
-    packed = lax.all_gather(packed, "grp", axis=0, tiled=False)
-    vecs = packed[:, :, : 8 * part].reshape(groups, layers, 8, part)
-    vecs = vecs.transpose(1, 2, 0, 3).reshape(layers, 8, width).astype(F32)
-    up_vecs = packed[:, :, 8 * part :].transpose(1, 0, 2).reshape(layers, 1, -1).astype(F32)
-    weights = [
-        [
-            lax.all_gather(w[layer], "grp", axis=0, tiled=True)
-            for w in (w_qkv, w_proj, w_up, w_down)
+    extra = hidden_part // part
+    packed = jnp.stack(vectors, axis=1)
+    packed = jnp.concatenate([packed, up_bias.reshape(layers, extra, part)], axis=1)
+    packed = packed.astype(F32)
+    wide = jnp.concatenate([w_qkv, w_proj, w_up], axis=2)
+
+    def layer_params(layer):
+        shards = [wide[layer].reshape(-1, 8, wide.shape[2]), w_down[layer].reshape(-1, 8, width)]
+        big, down, vecs = gather(shards, packed[layer], sizes, layer)
+        vectors = vecs[:, :VECTORS].transpose(1, 0, 2).reshape(VECTORS, width)
+        up = vecs[:, VECTORS:].reshape(extra, width)
+        rest = plan.vec_rows - VECTORS - extra
+        vecs = jnp.concatenate([vectors, up, jnp.zeros((rest, width), F32)], axis=0)
+        return [big.reshape(width, -1), down.reshape(-1, width)], vecs
+
+    def reduced(grads, layer):
+        blocks = [
+            grads[0].reshape(groups, -1, 8, grads[0].shape[1]),
+            grads[1].reshape(groups, -1, 8, width),
         ]
-        for layer in range(layers)
-    ]
-    hidden, keeps = plan.first(images, weights[0], vecs[0], up_vecs[0])
-    encoded, flowing, grads1 = plan.middle(hidden, cotangent, weights[1], vecs[1], up_vecs[1])
-    shares1 = reduce_weights(grads1[:4])
-    images_grad, grads0 = plan.last(flowing, images, weights[0], vecs[0], keeps)
-    shares0 = reduce_weights(grads0[:4])
-    small = jnp.stack([jnp.concatenate([g[4].reshape(-1), g[5].reshape(-1)]) for g in (grads0, grads1)])
-    small = lax.psum(small, ("rep", "grp"))
+        shares, vec = reduce_grads(blocks, grads[2], sizes, layers + layer)
+        return [s.reshape(-1, s.shape[2]) for s in shares], vec
+
+    weights0, vecs0 = layer_params(0)
+    weights1, vecs1 = layer_params(1)
+    hidden, keeps = plan.first(images, weights0, vecs0)
+    encoded, flowing, grads1 = plan.middle(hidden, cotangent, weights1, vecs1)
+    shares1, small1 = reduced(grads1, 1)
+    images_grad, grads0 = plan.last(flowing, images, weights0, vecs0, keeps)
+    shares0, small0 = reduced(grads0, 0)
+    small = jnp.stack([small0, small1])
     me = lax.axis_index("grp")
-    vec_out = lax.dynamic_slice_in_dim(
-        small[:, : 8 * width].reshape(layers, 8, width), me * part, part, axis=2
-    )
-    up_out = lax.dynamic_slice_in_dim(small[:, 8 * width :], me * hidden_part, hidden_part, axis=1)
-    full = [jnp.stack([a, b]) for a, b in zip(shares0, shares1)]
+    vec_out = lax.dynamic_slice_in_dim(small[:, :VECTORS], me * part, part, axis=2)
+    up_out = small[:, VECTORS : VECTORS + extra].reshape(layers, -1)
+    up_out = lax.dynamic_slice_in_dim(up_out, me * hidden_part, hidden_part, axis=1)
+    full = [jnp.stack([a, b]).astype(F32) for a, b in zip(shares0, shares1)]
+    columns = w_qkv.shape[2], w_qkv.shape[2] + width
     return (
         encoded,
         images_grad,
         vec_out[:, G1],
         vec_out[:, B1],
-        full[0],
+        full[0][:, :, : columns[0]],
         vec_out[:, QB],
         vec_out[:, VB],
-        full[1],
+        full[0][:, :, columns[0] : columns[1]],
         vec_out[:, PB],
         vec_out[:, G2],
         vec_out[:, B2],
-        full[2],
+        full[0][:, :, columns[1] :],
         up_out,
-        full[3],
+        full[1],
         vec_out[:, DB],
     )
 
@@ -485,5 +840,5 @@
     )
     specs = (batch, batch) + params
     return jax.shard_map(
-        on_device, mesh=mesh, in_specs=specs, out_specs=specs, check_vma=False
-    )
+        functools.partial(on_device, mesh.shape["rep"]), mesh=mesh, in_specs=specs, out_specs=specs, check_vma=False
+    )

time: 574 us -> 322 us (0.56)
  waiting for transfers between devices: 247 us -> 0 us
  Pallas kernels: 155 us -> 302 us
  blocking collectives: 145 us -> 0 us
  between operations: 14.3 us -> 1.01 us
  local copies, waits for them, and re-layouts: 6.53 us -> 15.6 us
    reduce_scatter x8 -> x0, waiting for transfers between devices: 210 us -> none  [reduce_weights(): lax.psum_scatter(g, 'grp', scatter_dimension=0, tiled=True)]
    pallas_call x0 -> x4, Pallas kernels: none -> 146 us  [the longest x2 78.2 us: reduce_grads(): pl.pallas_call(functools.partial(reduce_kernel, splits, sizes), name='red...]
    all_gather x5 -> x0, blocking collectives: 105 us -> none  [the longest x4 90.5 us: on_device(): lax.all_gather(w[layer], 'grp', axis=0, tiled=True)]
    psum x1 -> x0, blocking collectives: 39.1 us -> none  [on_device(): small = lax.psum(small, ('rep', 'grp'))]
    psum x1 -> x0, waiting for transfers between devices: 23.5 us -> none  [reduce_weights(): return [lax.psum(s, 'rep').astype(F32) for s in shares]]
    unnamed x44 -> x45, local copies, waits for them, and re-layouts: 0.09 us -> 11.5 us
    all_gather x4 -> x0, waiting for transfers between devices: 7.87 us -> none  [on_device(): lax.all_gather(w[layer], 'grp', axis=0, tiled=True)]
  transfers between devices with their start and end apart: 13 -> 0, of which waited for: 10 -> 0; matrix products, arithmetic and copies ran while one was open for 1% -> 0% of each run, Pallas kernels for 6% -> 0%
where the time goes in v2:
time: 322 us; the launch traced here: 321 us
  Pallas kernels  302 us (94%)
  local copies, waits for them, and re-layouts  15.6 us (5%)
    pallas_call x2, Pallas kernels, reduce_grads(): pl.pallas_call(functools.partial(reduce_kernel, splits, sizes), name='red...  78.2 us
    pallas_call x1, Pallas kernels, middle(): pl.pallas_call(functools.partial(middle_kernel, self.sizes), name='layer_...  72.2 us
    pallas_call x2, Pallas kernels, gather(): pl.pallas_call(functools.partial(gather_kernel, splits, sizes), name='gat...  67.9 us
    pallas_call x1, Pallas kernels, last(): pl.pallas_call(functools.partial(last_kernel, self.sizes), name='layer_la...  48.6 us
    pallas_call x1, Pallas kernels, first(): pl.pallas_call(functools.partial(first_kernel, self.sizes), name='layer_f...  35.2 us
    unnamed x45, local copies, waits for them, and re-layouts  11.5 us

profile of v2, /device:TPU:0, one launch (start us, length us, event | category | flops | bytes accessed | tf_op | source)
XLA Modules:
  0.0 321.4 jit_solution(16936968959026656778)
XLA Ops:
  0.7 1.1 constant_dynamic-update-slice_fusion.2
  1.8 0.9 constant_dynamic-update-slice_fusion.1
  3.0 0.9 copy-done.11
  4.3 33.3 %gather_params.2 = (bf16[4,12,8,3072]{3,2,1,0:T(8,128)(2,1)S(1)}, bf16[4,48,8,384]{3,2,1,0:T(8,128)(2,1)S(1)}, f32[4,12,96]{2,1,0:T(8,128)S(1)}) custom-call(bf16[1,12,8,3072]{3,2,1,0:T(8,128)(2,1)S(1)} %get-tuple-element.72.refs_0_, bf16[1,48,8,384]{3,2,1,0:T(8,128)(2,1)S(1)} %get-tuple-element.74.refs_1_, f32[1,12,96]{2,1,0:T(8,128)S(1)} %get-tuple-element.84.refs_2_), custom_call_target="tpu_custom_call" | custom-call | tf_op jit(solution)/shard_map/gather_params/pallas_call | solution.py:555
  37.6 1.4 copy-done.6
  39.0 1.0 copy-done.8
  40.1 34.5 %gather_params.3 = (bf16[4,12,8,3072]{3,2,1,0:T(8,128)(2,1)S(1)}, bf16[4,48,8,384]{3,2,1,0:T(8,128)(2,1)S(1)}, f32[4,12,96]{2,1,0:T(8,128)S(1)}) custom-call(bf16[1,12,8,3072]{3,2,1,0:T(8,128)(2,1)S(1)} %get-tuple-element.71.refs_0_, bf16[1,48,8,384]{3,2,1,0:T(8,128)(2,1)S(1)} %get-tuple-element.73.refs_1_, f32[1,12,96]{2,1,0:T(8,128)S(1)} %get-tuple-element.83.refs_2_), custom_call_target="tpu_custom_call" | custom-call | tf_op jit(solution)/shard_map/gather_params/pallas_call | solution.py:555
  74.7 1.4 copy-done.7
  76.1 1.0 copy-done.9
  77.4 0.7 maximum_maximum_fusion.1
  78.1 35.2 %layer_first.1 = (f32[2080,384]{1,0:T(8,128)}, bf16[2080,1152]{1,0:T(8,128)(2,1)}, f32[10,6,208,208]{3,2,1,0:T(8,128)}, bf16[10,384,208]{2,1,0:T(8,128)(2,1)}, f...) custom-call(bf16[10,197,384]{2,1,0:T(8,128)(2,1)} %refs_1_.3, bf16[384,3072]{1,0:T(8,128)(2,1)} %bitcast.59, ...), custom_call_target="tpu_custom_call" | custom-call | flops 6971719680 | bytes 41943040 | tf_op jit(solution)/shard_map/layer_first/pallas_call | solution.py:374
  113.3 72.2 %layer_middle.1 = (bf16[10,197,384]{2,1,0:T(8,128)(2,1)}, f32[2080,384]{1,0:T(8,128)}, bf16[384,3072]{1,0:T(8,128)(2,1)}, bf16[1536,384]{1,0:T(8,128)(2,1)}, f32[16,384]{1,0:T(8,128)}) custom-call(f32[2080,384]{1,0:T(8,128)} %get-tuple-element.46.refs_0_, bf16[10,197,384]{2,1,0:T(8,128)(2,1)} %refs_1_.2, bf16[384,3072]{1,0:T(8,128)(2,1)} %bitcast.61, ...), custom_call_target="tpu_custom_call" | custom-call | flops 20915159040 | bytes 41943040 | tf_op jit(solution)/shard_map/layer_middle/pallas_call | solution.py:389
  185.6 48.6 %layer_last.1 = (bf16[10,197,384]{2,1,0:T(8,128)(2,1)}, bf16[384,3072]{1,0:T(8,128)(2,1)}, bf16[1536,384]{1,0:T(8,128)(2,1)}, f32[16,384]{1,0:T(8,128)}) custom-call(f32[2080,384]{1,0:T(8,128)} %get-tuple-element.51.refs_0_, bf16[10,197,384]{2,1,0:T(8,128)(2,1)} %refs_1_.3, bf16[384,3072]{1,0:T(8,128)(2,1)} %bitcast.60, bf16[1536,384]{1,0:T(8,128)(2,1)} %bitcast.63, ...), custom_call_target="tpu_custom_call" | custom-call | flops 13943439360 | bytes 41943040 | tf_op jit(solution)/shard_map/layer_last/pallas_call | solution.py:405
  234.2 1.7 copy-done.1
  235.8 1.3 copy-done.3
  237.1 0.7 copy-done.5
  237.9 40.3 %reduce_grads.2 = (bf16[1,12,8,3072]{3,2,1,0:T(8,128)(2,1)S(1)}, bf16[1,48,8,384]{3,2,1,0:T(8,128)(2,1)S(1)}, f32[16,384]{1,0:T(8,128)S(1)}) custom-call(bf16[4,12,8,3072]{3,2,1,0:T(8,128)(2,1)S(1)} %bitcast.46, bf16[4,48,8,384]{3,2,1,0:T(8,128)(2,1)S(1)} %bitcast.52, f32[16,384]{1,0:T(8,128)S(1)} %copy-done.5), custom_call_target="tpu_custom_call" | custom-call | tf_op jit(solution)/shard_map/reduce_grads/pallas_call | solution.py:719
  278.2 37.8 %reduce_grads.3 = (bf16[1,12,8,3072]{3,2,1,0:T(8,128)(2,1)S(1)}, bf16[1,48,8,384]{3,2,1,0:T(8,128)(2,1)S(1)}, f32[16,384]{1,0:T(8,128)S(1)}) custom-call(bf16[4,12,8,3072]{3,2,1,0:T(8,128)(2,1)S(1)} %bitcast.45, bf16[4,48,8,384]{3,2,1,0:T(8,128)(2,1)S(1)} %bitcast.51, f32[16,384]{1,0:T(8,128)S(1)} %copy-done.4), custom_call_target="tpu_custom_call" | custom-call | tf_op jit(solution)/shard_map/reduce_grads/pallas_call | solution.py:719
  316.1 1.1 maximum_convert_fusion.1
  317.2 0.6 constant_dynamic-slice_fusion
  317.8 0.7 maximum_convert_fusion.2
  318.7 1.1 slice.106
  319.8 1.0 slice.100
  320.8 0.6 fusion.1
  (65 shorter events, 1.2 us)
Async XLA Ops:
  0.6 2.1 copy-start.10
  2.8 1.1 copy-start.11
  2.9 1.0 copy-start.12
  2.9 1.1 copy-start.13
  2.9 1.1 copy-start.14
  3.0 1.1 copy-start.15
  3.0 1.1 copy-start.16
  3.0 1.1 copy-start.17
  3.0 1.2 copy-start.18
  3.0 1.2 copy-start.19
  3.0 1.2 copy-start.20
  37.6 1.4 copy-start.6
  39.0 1.0 copy-start.8
  74.7 1.4 copy-start.7
  76.1 1.0 copy-start.9
  234.2 1.7 copy-start.1
  235.8 1.3 copy-start.3
  237.1 0.7 copy-start.5
  237.9 40.4 %copy-start = (bf16[384,3072]{1,0:T(8,128)(2,1)S(1)}, bf16[384,3072]{1,0:T(8,128)(2,1)}, u32[]{:S(2)}) copy-start(bf16[384,3072]{1,0:T(8,128)(2,1)} %get-tuple-element.63) | copy-start | bytes 7077892
  237.9 40.4 %copy-start.2 = (bf16[1536,384]{1,0:T(8,128)(2,1)S(1)}, bf16[1536,384]{1,0:T(8,128)(2,1)}, u32[]{:S(2)}) copy-start(bf16[1536,384]{1,0:T(8,128)(2,1)} %get-tuple-element.64) | copy-start | bytes 3538948
  237.9 40.4 %copy-start.4 = (f32[16,384]{1,0:T(8,128)S(1)}, f32[16,384]{1,0:T(8,128)}, u32[]{:S(2)}) copy-start(f32[16,384]{1,0:T(8,128)} %get-tuple-element.65.refs_2_) | copy-start | bytes 73732

commit v3 on v1

--- a/solution.py
+++ b/solution.py
@@ -1,4 +1,5 @@
 import functools
+import math
 
 import jax
 import jax.numpy as jnp
@@ -16,7 +17,8 @@
 F32 = jnp.float32
 BF16 = jnp.bfloat16
 
-G1, B1, QB, VB, PB, G2, B2, DB = range(8)
+VECTORS = 8
+G1, B1, QB, VB, PB, G2, B2, DB = range(VECTORS)
 
 
 def dot(left, right):
@@ -80,9 +82,25 @@
             keep["context"][image, pl.ds(head * HEAD_DIM, HEAD_DIM), :] = context.astype(BF16)
 
 
-def layer_forward(hidden, weights, vecs, up_bias, keep, images, seq, pad):
+def split_weights(wide, w_down):
+    width = w_down.shape[1]
+    return (
+        wide.at[:, pl.ds(0, 3 * width)],
+        wide.at[:, pl.ds(3 * width, width)],
+        wide.at[:, pl.ds(4 * width, w_down.shape[0])],
+        w_down,
+    )
+
+
+def up_bias_of(vecs, hidden_width):
+    rows = hidden_width // vecs.shape[1]
+    return jnp.concatenate([vecs[VECTORS + i : VECTORS + i + 1] for i in range(rows)], axis=1)
+
+
+def layer_forward(hidden, weights, vecs, keep, images, seq, pad):
     w_qkv, w_proj, w_up, w_down = weights
     width = hidden.shape[1]
+    up_bias = up_bias_of(vecs, w_down.shape[0])
     normed, _ = norm(hidden)
     rows_in = (normed * vecs[G1 : G1 + 1] + vecs[B1 : B1 + 1]).astype(BF16)
     qkv = keep["qkv"]
@@ -99,7 +117,7 @@
     keep["mixed"][...] = mixed
     normed, _ = norm(mixed)
     rows_mid = (normed * vecs[G2 : G2 + 1] + vecs[B2 : B2 + 1]).astype(BF16)
-    upward = dot(rows_mid, w_up[...]) + up_bias[...]
+    upward = dot(rows_mid, w_up[...]) + up_bias
     cumul = 0.5 * (1.0 + lax.erf(upward * INV_ROOT_TWO))
     keep["active"][...] = (upward * cumul).astype(BF16)
     slope = cumul + upward * jnp.exp(-0.5 * upward * upward) * INV_ROOT_TAU
@@ -216,56 +234,125 @@
     @pl.when(pl.program_id(0) == pl.num_programs(0) - 1)
     def _():
         g_qkv, g_proj, g_up, g_down, vec_grads, up_bias_grad = acc[:6]
-        outs[0][...] = g_qkv[...].astype(BF16)
-        outs[1][...] = g_proj[...].astype(BF16)
-        outs[2][...] = g_up[...].astype(BF16)
-        outs[3][...] = g_down[...].astype(BF16).T
-        outs[4][...] = vec_grads[...]
-        outs[5][...] = up_bias_grad[...]
-
-
-def first_kernel(sizes, *refs):
+        wide, down, vecs = outs
+        g_qkv_out, g_proj_out, g_up_out, g_down_out = split_weights(wide, down)
+        g_qkv_out[...] = g_qkv[...].astype(BF16)
+        g_proj_out[...] = g_proj[...].astype(BF16)
+        g_up_out[...] = g_up[...].astype(BF16)
+        g_down_out[...] = g_down[...].astype(BF16).T
+        width = vecs.shape[1]
+        extra = up_bias_grad.shape[1] // width
+        vecs[:VECTORS, :] = vec_grads[...]
+        for i in range(extra):
+            vecs[VECTORS + i : VECTORS + i + 1, :] = up_bias_grad[:, i * width : (i + 1) * width]
+        rest = vecs.shape[0] - VECTORS - extra
+        if rest:
+            vecs[VECTORS + extra :, :] = jnp.zeros((rest, width), F32)
+
+
+def step_at(step, body):
+    pl.when(pl.program_id(0) == step)(body)
+
+
+def first_kernel(sizes, steps, chunks, mesh_sizes, *refs):
     group, seq, pad = sizes
-    images, w0, w1, w2, w3, vecs, up_bias, out = refs[:8]
+    images, wide, down, vecs = refs[:4]
+    out = refs[7]
     keep = dict(zip(KEEP, refs[8:14]))
-    (buf,) = refs[14:]
+    buf = refs[17]
+    work = Gather(chunks, mesh_sizes, refs[4:6], refs[6], refs[14:16], refs[16], refs[18:])
+    every = list(range(len(chunks)))
+    early = every[: len(every) // 2]
+    late = every[len(every) // 2 :]
+    plans = [
+        (0, lambda: work.begin()),
+        (steps // 5, lambda: [work.to_chips(i) for i in early]),
+        (2 * steps // 5, lambda: [work.to_chips(i) for i in late]),
+        (3 * steps // 5, lambda: [work.to_cores(i) for i in early]),
+    ]
+    for step, body in plans:
+        step_at(step, lambda body=body: (body(), None)[1])
     load_padded(images, buf, pad)
     out[...] = layer_forward(
-        buf[...], (w0, w1, w2, w3), vecs, up_bias, keep, group, seq, pad
-    )
+        buf[...], split_weights(wide, down), vecs, keep, group, seq, pad
+    )
+
+    @pl.when(pl.program_id(0) == steps - 1)
+    def _():
+        for i in late:
+            work.to_cores(i)
+        work.finish()
 
 
 def middle_kernel(sizes, *refs):
     group, seq, pad = sizes
-    hidden, cotangent, w0, w1, w2, w3, vecs, up_bias, encoded, flowing = refs[:10]
-    outs = refs[10:16]
-    keep = dict(zip(KEEP, refs[16:22]))
-    acc = refs[22:30]
-    (buf,) = refs[30:]
-    weights = (w0, w1, w2, w3)
+    hidden, cotangent, wide, down, vecs, encoded, flowing = refs[:7]
+    outs = refs[7:10]
+    keep = dict(zip(KEEP, refs[10:16]))
+    acc = refs[16:24]
+    (buf,) = refs[24:]
+    weights = split_weights(wide, down)
     init_grads(acc)
-    result = layer_forward(hidden[...], weights, vecs, up_bias, keep, group, seq, pad)
+    result = layer_forward(hidden[...], weights, vecs, keep, group, seq, pad)
     store_images(encoded, result, pad)
     load_padded(cotangent, buf, pad)
     flowing[...] = layer_backward(buf[...], hidden[...], weights, vecs, keep, acc, group, pad)
     flush_grads(acc, outs)
 
 
-def last_kernel(sizes, *refs):
+def last_kernel(sizes, steps, chunks, mesh_sizes, *refs):
     group, seq, pad = sizes
-    flowing, images, w0, w1, w2, w3, vecs = refs[:7]
-    keep = dict(zip(KEEP, refs[7:13]))
-    images_grad = refs[13]
-    outs = refs[14:20]
-    acc = refs[20:28]
-    (buf,) = refs[28:]
+    flowing, images, wide, down, vecs = refs[:5]
+    keep = dict(zip(KEEP, refs[5:11]))
+    images_grad = refs[14]
+    outs = refs[15:18]
+    acc = refs[21:29]
+    buf = refs[29]
+    shares = refs[30:32]
+    work = Reduce(chunks, mesh_sizes, refs[11:13], refs[13], shares, refs[20], refs[32:])
+    every = range(len(chunks))
+
+    @pl.when(pl.program_id(0) == 0)
+    def _():
+        work.begin()
+
+    @pl.when(pl.program_id(0) == steps // 5)
+    def _():
+        for i in every:
+            work.to_chips(i)
+        work.vec_to_chips()
+
+    @pl.when(pl.program_id(0) == 3 * steps // 5)
+    def _():
+        for i in every:
+            work.to_shards(i)
+        work.vec_to_shards()
+
+    @pl.when(pl.program_id(0) == 4 * steps // 5)
+    def _():
+        for i in every:
+            work.to_spread(i)
+        work.vec_end()
+
     init_grads(acc)
     load_padded(images, buf, pad)
     result = layer_backward(
-        flowing[...], buf[...], (w0, w1, w2, w3), vecs, keep, acc, group, pad
+        flowing[...], buf[...], split_weights(wide, down), vecs, keep, acc, group, pad
     )
     store_images(images_grad, result, pad)
+
+    @pl.when(pl.program_id(0) == steps - 1)
+    def _():
+        for i in every:
+            work.to_join(i)
+
     flush_grads(acc, outs)
+
+    @pl.when(pl.program_id(0) == steps - 1)
+    def _():
+        work.finish()
+        for share, ref in zip(shares, refs[18:20]):
+            ref[...] = share[...]
 
 
 def whole(shape):
@@ -307,9 +394,14 @@
             pltpu.VMEM((block_rows, 3 * self.width), BF16),
             pltpu.VMEM((block_rows, self.width), BF16),
         ]
-        self.grad_shapes = [jax.ShapeDtypeStruct(s, BF16) for s in self.weight_shapes] + [
-            jax.ShapeDtypeStruct((8, self.width), F32),
-            jax.ShapeDtypeStruct((1, hidden_width), F32),
+        self.vec_rows = -(-(VECTORS + hidden_width // self.width) // 8) * 8
+        self.packed_shapes = [
+            (self.width, 4 * self.width + hidden_width),
+            (hidden_width, self.width),
+        ]
+        self.vec_shape = (self.vec_rows, self.width)
+        self.grad_shapes = [jax.ShapeDtypeStruct(s, BF16) for s in self.packed_shapes] + [
+            jax.ShapeDtypeStruct(self.vec_shape, F32)
         ]
         self.params = pltpu.CompilerParams(
             dimension_semantics=("arbitrary",), vmem_limit_bytes=60 * 2**20
@@ -322,10 +414,7 @@
         return rows_spec((self.rows, self.width), self.steps)
 
     def param_specs(self):
-        return [whole(s) for s in self.weight_shapes] + [
-            whole((8, self.width)),
-            whole((1, self.hidden_width)),
-        ]
+        return [whole(s) for s in self.packed_shapes + [self.vec_shape]]
 
     def keep_specs(self):
         return [rows_spec(self.keep[k][0], self.steps) for k in KEEP]
@@ -340,23 +429,32 @@
             flops=int(flops), bytes_accessed=int(40 * 2**20), transcendentals=0
         )
 
-    def first(self, images, weights, vecs, up_bias):
+    def comm_params(self, collective_id):
+        return pltpu.CompilerParams(
+            dimension_semantics=("arbitrary",),
+            vmem_limit_bytes=62 * 2**20,
+            collective_id=collective_id,
+            has_side_effects=True,
+        )
+
+    def first(self, images, weights, vecs, shards, mesh_sizes, collective_id):
         state = jax.ShapeDtypeStruct((self.rows, self.width), F32)
         keeps = [jax.ShapeDtypeStruct(*self.keep[k]) for k in KEEP]
+        chunks = chunks_of([(s.shape[1], s.shape[3]) for s in shards[:2]], mesh_sizes[1])
         out = pl.pallas_call(
-            functools.partial(first_kernel, self.sizes),
+            functools.partial(first_kernel, self.sizes, self.steps, chunks, mesh_sizes),
             name="layer_first",
-            out_shape=[state] + keeps,
+            out_shape=[state] + keeps + gathered_shapes(shards, mesh_sizes[0]),
             grid=(self.steps,),
-            in_specs=[self.image_spec()] + self.param_specs(),
-            out_specs=[self.state_spec()] + self.keep_specs(),
-            scratch_shapes=[self.buffer],
-            compiler_params=self.params,
+            in_specs=[self.image_spec()] + self.param_specs() + [ANY_SPEC] * 3,
+            out_specs=[self.state_spec()] + self.keep_specs() + [ANY_SPEC] * 3,
+            scratch_shapes=[self.buffer] + Gather.semaphores(chunks, mesh_sizes),
+            compiler_params=self.comm_params(collective_id),
             cost_estimate=self.cost(1),
-        )(images, *weights, vecs, up_bias)
-        return out[0], out[1:]
-
-    def middle(self, hidden, cotangent, weights, vecs, up_bias):
+        )(images, *weights, vecs, *shards)
+        return out[0], out[1:7], out[7:]
+
+    def middle(self, hidden, cotangent, weights, vecs):
         state = jax.ShapeDtypeStruct((self.rows, self.width), F32)
         out = pl.pallas_call(
             functools.partial(middle_kernel, self.sizes),
@@ -370,34 +468,503 @@
             + [self.buffer],
             compiler_params=self.params,
             cost_estimate=self.cost(3),
-        )(hidden, cotangent, *weights, vecs, up_bias)
+        )(hidden, cotangent, *weights, vecs)
         return out[0], out[1], out[2:]
 
-    def last(self, flowing, images, weights, vecs, keeps):
+    def last(self, flowing, images, weights, vecs, keeps, grads, mesh_sizes, collective_id):
+        chunks = chunks_of([(g.shape[1], g.shape[3]) for g in grads[:2]], mesh_sizes[1])
+        shares = reduced_shapes(grads)
         out = pl.pallas_call(
-            functools.partial(last_kernel, self.sizes),
+            functools.partial(last_kernel, self.sizes, self.steps, chunks, mesh_sizes),
             name="layer_last",
-            out_shape=[jax.ShapeDtypeStruct(images.shape, BF16)] + self.grad_shapes,
+            out_shape=[jax.ShapeDtypeStruct(images.shape, BF16)] + self.grad_shapes + shares,
             grid=(self.steps,),
             in_specs=[self.state_spec(), self.image_spec()]
-            + self.param_specs()[:5]
-            + self.keep_specs(),
-            out_specs=[self.image_spec()] + self.grad_specs(),
-            scratch_shapes=self.acc + [self.buffer],
-            compiler_params=self.params,
+            + self.param_specs()
+            + self.keep_specs()
+            + [whole(g.shape) for g in grads],
+            out_specs=[self.image_spec()] + self.grad_specs() + [whole(s.shape) for s in shares],
+            scratch_shapes=self.acc
+            + [self.buffer]
+            + [pltpu.VMEM(s.shape, s.dtype) for s in shares[:2]]
+            + Reduce.scratch(chunks, mesh_sizes, grads[2].shape),
+            compiler_params=self.comm_params(collective_id),
             cost_estimate=self.cost(2),
-        )(flowing, images, *weights, vecs, *keeps)
-        return out[0], out[1:]
-
-
-def reduce_weights(grads):
-    shares = [
-        lax.psum_scatter(g, "grp", scatter_dimension=0, tiled=True) for g in grads
+        )(flowing, images, *weights, vecs, *keeps, *grads)
+        return out[0], out[1:4], out[4:]
+
+
+def greet(targets):
+    barrier = pltpu.get_barrier_semaphore()
+    for target in targets:
+        pl.semaphore_signal(
+            barrier, inc=1, device_id=target, device_id_type=pl.DeviceIdType.MESH
+        )
+    pl.semaphore_wait(barrier, len(targets))
+
+
+def transfer(src, dst, sems, at, target):
+    return pltpu.make_async_remote_copy(
+        src_ref=src,
+        dst_ref=dst,
+        send_sem=sems[0].at[at],
+        recv_sem=sems[1].at[at],
+        device_id=target,
+        device_id_type=pl.DeviceIdType.MESH,
+    )
+
+
+class Chunk:
+    def __init__(self, array, blocks, columns, by_columns, extent, start, chips):
+        self.array, self.by_columns, self.start, self.extent = array, by_columns, start, extent
+        self.blocks = blocks if by_columns else extent
+        self.columns = extent if by_columns else columns
+        self.stride = (columns if by_columns else blocks) // 2
+        self.pieces = math.gcd(self.blocks, chips)
+        self.run = self.blocks // self.pieces
+
+    def part(self, ref, core, piece=None, shard=slice(None)):
+        at = core * self.stride + self.start
+        first, size = (0, self.blocks) if piece is None else (piece * self.run, self.run)
+        if self.by_columns:
+            columns = pl.ds(pl.multiple_of(at, 128), self.columns)
+            return ref.at[shard, pl.ds(first, size), :, columns]
+        return ref.at[shard, pl.ds(at + first, size)]
+
+
+def chunks_of(shapes, reps):
+    chips = reps // 2
+    lists = []
+    for array, (blocks, columns) in enumerate(shapes):
+        by_columns = columns % 256 == 0
+        half = columns // 2 if by_columns else blocks // 2
+        unit = 128 if by_columns else 1
+        want = 3 if by_columns else 2
+        parts = want if half % (want * unit) == 0 else 1
+        extent = half // parts
+        lists.append(
+            [
+                Chunk(array, blocks, columns, by_columns, extent, j * extent, chips)
+                for j in range(parts)
+            ]
+        )
+    merged = []
+    for j in range(max(len(part) for part in lists)):
+        merged += [part[j] for part in lists if j < len(part)]
+    return merged
+
+
+class Place:
+    def __init__(self, sizes):
+        self.groups, self.reps = sizes
+        self.rep, self.mine = lax.axis_index("rep"), lax.axis_index("grp")
+        self.chip, self.core = self.rep // 2, lax.rem(self.rep, 2)
+        self.chips = self.reps // 2
+        self.shard_peers = [
+            (self.rep, lax.rem(self.mine + d, self.groups)) for d in range(1, self.groups)
+        ]
+        self.core_peer = (self.chip * 2 + 1 - self.core, self.mine)
+
+    def piece(self, chunk):
+        return lax.rem(self.chip, chunk.pieces)
+
+    def mate(self, chunk, step):
+        piece = self.piece(chunk)
+        return self.chip - piece + lax.rem(piece + step, chunk.pieces)
+
+    def at(self, chip):
+        return (chip * 2 + self.core, self.mine)
+
+
+class Gather:
+    def __init__(self, chunks, sizes, ins, vec_in, outs, vec_out, sems):
+        self.chunks, self.place = chunks, Place(sizes)
+        self.ins, self.outs, self.vec_in, self.vec_out = ins, outs, vec_in, vec_out
+        self.own_sem, self.vec_own_sem = sems[:2]
+        self.vec_sems, self.shard_sems, self.chip_sems, self.core_sems = (
+            sems[2 + 2 * i : 4 + 2 * i] for i in range(4)
+        )
+
+    @staticmethod
+    def semaphores(chunks, sizes):
+        groups = sizes[0]
+        most = max(c.pieces for c in chunks)
+        count = len(chunks)
+        return (
+            [pltpu.SemaphoreType.DMA((count,)), pltpu.SemaphoreType.DMA]
+            + dma_pair(groups - 1)
+            + dma_pair(count, groups - 1)
+            + dma_pair(count, max(most - 1, 1))
+            + dma_pair(count)
+        )
+
+    def shards(self, i):
+        chunk, place = self.chunks[i], self.place
+        piece = place.piece(chunk)
+        src = chunk.part(self.ins[chunk.array], place.core, piece, 0)
+        dst = chunk.part(self.outs[chunk.array], place.core, piece, place.mine)
+        return [
+            transfer(src, dst, self.shard_sems, (i, d), t)
+            for d, t in enumerate(place.shard_peers)
+        ]
+
+    def own(self, i):
+        chunk, place = self.chunks[i], self.place
+        piece = place.piece(chunk)
+        src = chunk.part(self.ins[chunk.array], place.core, piece, 0)
+        dst = chunk.part(self.outs[chunk.array], place.core, piece, place.mine)
+        return pltpu.make_async_copy(src, dst, self.own_sem.at[i])
+
+    def vectors(self):
+        return [
+            transfer(self.vec_in.at[0], self.vec_out.at[self.place.mine], self.vec_sems, d, t)
+            for d, t in enumerate(self.place.shard_peers)
+        ]
+
+    def vector_own(self):
+        return pltpu.make_async_copy(
+            self.vec_in.at[0], self.vec_out.at[self.place.mine], self.vec_own_sem
+        )
+
+    def chips(self, i):
+        chunk, place = self.chunks[i], self.place
+        block = chunk.part(self.outs[chunk.array], place.core, place.piece(chunk))
+        return [
+            transfer(block, block, self.chip_sems, (i, e - 1), place.at(place.mate(chunk, e)))
+            for e in range(1, chunk.pieces)
+        ]
+
+    def cores(self, i):
+        chunk, place = self.chunks[i], self.place
+        block = chunk.part(self.outs[chunk.array], place.core)
+        return [transfer(block, block, self.core_sems, i, place.core_peer)]
+
+    def begin(self):
+        place = self.place
+        most = max(self.chunks, key=lambda c: c.pieces)
+        greet(
+            place.shard_peers
+            + [place.at(place.mate(most, e)) for e in range(1, most.pieces)]
+            + [place.core_peer]
+        )
+        for i in range(len(self.chunks)):
+            start(self.shards(i))
+            self.own(i).start()
+            if i == 0:
+                start(self.vectors())
+                self.vector_own().start()
+
+    def to_chips(self, i):
+        self.own(i).wait()
+        arrive(self.shards(i))
+        start(self.chips(i))
+
+    def to_cores(self, i):
+        arrive(self.chips(i))
+        start(self.cores(i))
+
+    def finish(self):
+        every = range(len(self.chunks))
+        for i in every:
+            arrive(self.cores(i))
+        arrive(self.vectors())
+        self.vector_own().wait()
+        for copy in self.vectors():
+            copy.wait_send()
+        for i in every:
+            for copy in self.shards(i) + self.chips(i) + self.cores(i):
+                copy.wait_send()
+
+
+def start(copies):
+    for copy in copies:
+        copy.start()
+
+
+def arrive(copies):
+    for copy in copies:
+        copy.wait_recv()
+
+
+def gather_kernel(chunks, sizes, *refs):
+    work = Gather(chunks, sizes, refs[:2], refs[2], refs[3:5], refs[5], refs[6:])
+    work.begin()
+    for i in range(len(chunks)):
+        work.to_chips(i)
+    for i in range(len(chunks)):
+        work.to_cores(i)
+    work.finish()
+
+
+def dma_pair(*shape):
+    return [pltpu.SemaphoreType.DMA(shape), pltpu.SemaphoreType.DMA(shape)]
+
+
+VMEM_SPEC = pl.BlockSpec(memory_space=pltpu.VMEM)
+ANY_SPEC = pl.BlockSpec(memory_space=pl.ANY)
+
+
+def gathered_shapes(shards, groups):
+    return [jax.ShapeDtypeStruct((groups,) + s.shape[1:], s.dtype) for s in shards]
+
+
+def gather(shards, sizes, collective_id):
+    chunks = chunks_of([(s.shape[1], s.shape[3]) for s in shards[:2]], sizes[1])
+    return pl.pallas_call(
+        functools.partial(gather_kernel, chunks, sizes),
+        name="gather_params",
+        out_shape=gathered_shapes(shards, sizes[0]),
+        in_specs=[VMEM_SPEC] * 3,
+        out_specs=[VMEM_SPEC] * 3,
+        scratch_shapes=Gather.semaphores(chunks, sizes),
+        compiler_params=pltpu.CompilerParams(
+            collective_id=collective_id, has_side_effects=True, vmem_limit_bytes=40 * 2**20
+        ),
+    )(*shards)
+
+
+def add_up(first, rest):
+    total = first.astype(F32)
+    for term in rest:
+        total = total + term.astype(F32)
+    return total
+
+
+class Reduce:
+    def __init__(self, chunks, sizes, ins, vec_in, outs, vec_out, scratch):
+        count = len(chunks)
+        self.chunks, self.place = chunks, Place(sizes)
+        self.ins, self.vec_in, self.outs, self.vec_out = ins, vec_in, outs, vec_out
+        self.from_core, self.core_sum, self.from_chips, self.chip_sum, self.from_shards = (
+            scratch[i * count : (i + 1) * count] for i in range(5)
+        )
+        self.vec_parts, self.vec_held = scratch[5 * count : 5 * count + 2]
+        sems = scratch[5 * count + 2 :]
+        (
+            self.core_sems,
+            self.chip_sems,
+            self.shard_sems,
+            self.spread_sems,
+            self.join_sems,
+            self.vec_sems,
+        ) = (sems[2 * i : 2 * i + 2] for i in range(6))
+
+    @staticmethod
+    def scratch(chunks, sizes, vec_shape):
+        groups, reps = sizes
+        chips, count = reps // 2, len(chunks)
+        most = max(c.pieces for c in chunks)
+        half = [(groups, c.blocks, 8, c.columns) for c in chunks]
+        piece = [(groups, c.run, 8, c.columns) for c in chunks]
+        shapes = (
+            half
+            + half
+            + [(chips - 1,) + p for p in piece]
+            + piece
+            + [(groups - 1,) + p[1:] for p in piece]
+        )
+        terms = chips + groups - 1
+        return (
+            [pltpu.VMEM(s, BF16) for s in shapes]
+            + [pltpu.VMEM((terms,) + vec_shape, F32), pltpu.VMEM((2,) + vec_shape, F32)]
+            + dma_pair(count)
+            + dma_pair(count, chips - 1)
+            + dma_pair(count, groups - 1)
+            + dma_pair(count, max(most - 1, 1))
+            + dma_pair(count)
+            + dma_pair(terms)
+        )
+
+    def chip_ids(self):
+        place = self.place
+        return [lax.rem(place.chip + e, place.chips) for e in range(1, place.chips)]
+
+    def cores(self, i):
+        chunk, place = self.chunks[i], self.place
+        src = chunk.part(self.ins[chunk.array], 1 - place.core)
+        return [transfer(src, self.from_core[i], self.core_sems, i, place.core_peer)]
+
+    def chips(self, i):
+        chunk, copies = self.chunks[i], []
+        for e, chip in enumerate(self.chip_ids()):
+            piece = lax.rem(chip, chunk.pieces)
+            src = self.core_sum[i].at[:, pl.ds(piece * chunk.run, chunk.run)]
+            dst = self.from_chips[i].at[e]
+            copies.append(transfer(src, dst, self.chip_sems, (i, e), self.place.at(chip)))
+        return copies
+
+    def shards(self, i):
+        place = self.place
+        return [
+            transfer(
+                self.chip_sum[i].at[lax.rem(place.mine + d + 1, place.groups)],
+                self.from_shards[i].at[d],
+                self.shard_sems,
+                (i, d),
+                target,
+            )
+            for d, target in enumerate(place.shard_peers)
+        ]
+
+    def spread(self, i):
+        chunk, place = self.chunks[i], self.place
+        block = chunk.part(self.outs[chunk.array], place.core, place.piece(chunk), 0)
+        return [
+            transfer(block, block, self.spread_sems, (i, e - 1), place.at(place.mate(chunk, e)))
+            for e in range(1, chunk.pieces)
+        ]
+
+    def join(self, i):
+        chunk, place = self.chunks[i], self.place
+        block = chunk.part(self.outs[chunk.array], place.core, None, 0)
+        return [transfer(block, block, self.join_sems, i, place.core_peer)]
+
+    def vec_cores(self):
+        return [transfer(self.vec_in, self.vec_parts.at[0], self.vec_sems, 0, self.place.core_peer)]
+
+    def vec_chips(self):
+        return [
+            transfer(
+                self.vec_held.at[0],
+                self.vec_parts.at[1 + e],
+                self.vec_sems,
+                1 + e,
+                self.place.at(chip),
+            )
+            for e, chip in enumerate(self.chip_ids())
+        ]
+
+    def vec_shards(self):
+        chips = self.place.chips
+        return [
+            transfer(
+                self.vec_held.at[1],
+                self.vec_parts.at[chips + d],
+                self.vec_sems,
+                chips + d,
+                target,
+            )
+            for d, target in enumerate(self.place.shard_peers)
+        ]
+
+    def begin(self):
+        place = self.place
+        greet(
+            place.shard_peers + [place.at(c) for c in self.chip_ids()] + [place.core_peer]
+        )
+        for i in range(len(self.chunks)):
+            start(self.cores(i))
+        start(self.vec_cores())
+
+    def to_chips(self, i):
+        chunk = self.chunks[i]
+        own = chunk.part(self.ins[chunk.array], self.place.core)[...]
+        arrive(self.cores(i))
+        self.core_sum[i][...] = add_up(own, [self.from_core[i][...]]).astype(BF16)
+        start(self.chips(i))
+
+    def vec_to_chips(self):
+        arrive(self.vec_cores())
+        self.vec_held[0] = self.vec_in[...] + self.vec_parts[0]
+        start(self.vec_chips())
+
+    def to_shards(self, i):
+        chunk = self.chunks[i]
+        piece = self.place.piece(chunk)
+        own = self.core_sum[i][:, pl.ds(piece * chunk.run, chunk.run)]
+        copies = self.chips(i)
+        arrive(copies)
+        total = add_up(own, [self.from_chips[i][e] for e in range(len(copies))])
+        self.chip_sum[i][...] = total.astype(BF16)
+        start(self.shards(i))
+
+    def vec_to_shards(self):
+        copies = self.vec_chips()
+        arrive(copies)
+        self.vec_held[1] = add_up(
+            self.vec_held[0], [self.vec_parts[1 + e] for e in range(len(copies))]
+        )
+        start(self.vec_shards())
+
+    def to_spread(self, i):
+        chunk, place = self.chunks[i], self.place
+        copies = self.shards(i)
+        arrive(copies)
+        total = add_up(
+            self.chip_sum[i][place.mine], [self.from_shards[i][d] for d in range(len(copies))]
+        )
+        block = chunk.part(self.outs[chunk.array], place.core, place.piece(chunk), 0)
+        block[...] = total.astype(BF16)
+        start(self.spread(i))
+
+    def vec_end(self):
+        copies = self.vec_shards()
+        arrive(copies)
+        self.vec_out[...] = add_up(
+            self.vec_held[1], [self.vec_parts[self.place.chips + d] for d in range(len(copies))]
+        )
+
+    def to_join(self, i):
+        arrive(self.spread(i))
+        start(self.join(i))
+
+    def finish(self):
+        every = range(len(self.chunks))
+        for i in every:
+            arrive(self.join(i))
+        copies = self.vec_cores() + self.vec_chips() + self.vec_shards()
+        for i in every:
+            copies += self.cores(i) + self.chips(i) + self.shards(i)
+            copies += self.spread(i) + self.join(i)
+        for copy in copies:
+            copy.wait_send()
+
+
+def reduce_kernel(chunks, sizes, *refs):
+    work = Reduce(chunks, sizes, refs[:2], refs[2], refs[3:5], refs[5], refs[6:])
+    count = len(chunks)
+    work.begin()
+    for i in range(count):
+        work.to_chips(i)
+    work.vec_to_chips()
+    for i in range(count):
+        work.to_shards(i)
+        if i == 0:
+            work.vec_to_shards()
+        if i > 0:
+            work.to_spread(i - 1)
+        if i > 1:
+            work.to_join(i - 2)
+    work.to_spread(count - 1)
+    work.vec_end()
+    for i in range(max(count - 2, 0), count):
+        work.to_join(i)
+    work.finish()
+
+
+def reduced_shapes(grads):
+    return [jax.ShapeDtypeStruct((1,) + g.shape[1:], BF16) for g in grads[:2]] + [
+        jax.ShapeDtypeStruct(grads[2].shape, F32)
     ]
-    return [lax.psum(s, "rep").astype(F32) for s in shares]
+
+
+def reduce_grads(grads, sizes, collective_id):
+    chunks = chunks_of([(g.shape[1], g.shape[3]) for g in grads[:2]], sizes[1])
+    return pl.pallas_call(
+        functools.partial(reduce_kernel, chunks, sizes),
+        name="reduce_grads",
+        out_shape=reduced_shapes(grads),
+        in_specs=[VMEM_SPEC] * 3,
+        out_specs=[VMEM_SPEC] * 3,
+        scratch_shapes=Reduce.scratch(chunks, sizes, grads[2].shape),
+        compiler_params=pltpu.CompilerParams(
+            collective_id=collective_id, has_side_effects=True, vmem_limit_bytes=40 * 2**20
+        ),
+    )(*grads)
 
 
 def on_device(
+    reps,
     images,
     cotangent,
     ln1_gain,
@@ -415,51 +982,74 @@
     down_bias,
 ):
     groups = lax.axis_size("grp")
+    sizes = (groups, reps)
     layers, part = ln1_gain.shape
     width = part * groups
     hidden_part = up_bias.shape[1]
     plan = Plan(images.shape, hidden_part * groups)
     vectors = [ln1_gain, ln1_bias, q_bias, v_bias, proj_bias, ln2_gain, ln2_bias, down_bias]
-    packed = jnp.concatenate(vectors + [up_bias], axis=1)
-    packed = lax.all_gather(packed, "grp", axis=0, tiled=False)
-    vecs = packed[:, :, : 8 * part].reshape(groups, layers, 8, part)
-    vecs = vecs.transpose(1, 2, 0, 3).reshape(layers, 8, width).astype(F32)
-    up_vecs = packed[:, :, 8 * part :].transpose(1, 0, 2).reshape(layers, 1, -1).astype(F32)
-    weights = [
-        [
-            lax.all_gather(w[layer], "grp", axis=0, tiled=True)
-            for w in (w_qkv, w_proj, w_up, w_down)
-        ]
-        for layer in range(layers)
-    ]
-    hidden, keeps = plan.first(images, weights[0], vecs[0], up_vecs[0])
-    encoded, flowing, grads1 = plan.middle(hidden, cotangent, weights[1], vecs[1], up_vecs[1])
-    shares1 = reduce_weights(grads1[:4])
-    images_grad, grads0 = plan.last(flowing, images, weights[0], vecs[0], keeps)
-    shares0 = reduce_weights(grads0[:4])
-    small = jnp.stack([jnp.concatenate([g[4].reshape(-1), g[5].reshape(-1)]) for g in (grads0, grads1)])
-    small = lax.psum(small, ("rep", "grp"))
+    extra = hidden_part // part
+    packed = jnp.stack(vectors, axis=1)
+    packed = jnp.concatenate([packed, up_bias.reshape(layers, extra, part)], axis=1)
+    packed = packed.astype(F32)
+    wide = jnp.concatenate([w_qkv, w_proj, w_up], axis=2)
+
+    def shards_of(layer):
+        return [
+            wide[layer].reshape(1, -1, 8, wide.shape[2]),
+            w_down[layer].reshape(1, -1, 8, width),
+            packed[layer][None],
+        ]
+
+    def unpack(gathered):
+        big, down, vecs = gathered
+        vectors = vecs[:, :VECTORS].transpose(1, 0, 2).reshape(VECTORS, width)
+        up = vecs[:, VECTORS:].reshape(extra, width)
+        rest = plan.vec_rows - VECTORS - extra
+        vecs = jnp.concatenate([vectors, up, jnp.zeros((rest, width), F32)], axis=0)
+        return [big.reshape(width, -1), down.reshape(-1, width)], vecs
+
+    def blocks_of(grads):
+        return [
+            grads[0].reshape(groups, -1, 8, grads[0].shape[1]),
+            grads[1].reshape(groups, -1, 8, width),
+            grads[2],
+        ]
+
+    weights0, vecs0 = unpack(gather(shards_of(0), sizes, 0))
+    hidden, keeps, gathered = plan.first(images, weights0, vecs0, shards_of(1), sizes, 1)
+    weights1, vecs1 = unpack(gathered)
+    encoded, flowing, grads1 = plan.middle(hidden, cotangent, weights1, vecs1)
+    images_grad, grads0, reduced1 = plan.last(
+        flowing, images, weights0, vecs0, keeps, blocks_of(grads1), sizes, 2
+    )
+    reduced0 = reduce_grads(blocks_of(grads0), sizes, 3)
+    small0, small1 = reduced0[2], reduced1[2]
+    shares0, shares1 = (
+        [s.reshape(-1, s.shape[3]) for s in reduced[:2]] for reduced in (reduced0, reduced1)
+    )
+    small = jnp.stack([small0, small1])
     me = lax.axis_index("grp")
-    vec_out = lax.dynamic_slice_in_dim(
-        small[:, : 8 * width].reshape(layers, 8, width), me * part, part, axis=2
-    )
-    up_out = lax.dynamic_slice_in_dim(small[:, 8 * width :], me * hidden_part, hidden_part, axis=1)
-    full = [jnp.stack([a, b]) for a, b in zip(shares0, shares1)]
+    vec_out = lax.dynamic_slice_in_dim(small[:, :VECTORS], me * part, part, axis=2)
+    up_out = small[:, VECTORS : VECTORS + extra].reshape(layers, -1)
+    up_out = lax.dynamic_slice_in_dim(up_out, me * hidden_part, hidden_part, axis=1)
+    full = [jnp.stack([a, b]).astype(F32) for a, b in zip(shares0, shares1)]
+    columns = w_qkv.shape[2], w_qkv.shape[2] + width
     return (
         encoded,
         images_grad,
         vec_out[:, G1],
         vec_out[:, B1],
-        full[0],
+        full[0][:, :, : columns[0]],
         vec_out[:, QB],
         vec_out[:, VB],
-        full[1],
+        full[0][:, :, columns[0] : columns[1]],
         vec_out[:, PB],
         vec_out[:, G2],
         vec_out[:, B2],
-        full[2],
+        full[0][:, :, columns[1] :],
         up_out,
-        full[3],
+        full[1],
         vec_out[:, DB],
     )
 
@@ -485,5 +1075,5 @@
     )
     specs = (batch, batch) + params
     return jax.shard_map(
-        on_device, mesh=mesh, in_specs=specs, out_specs=specs, check_vma=False
-    )
+        functools.partial(on_device, mesh.shape["rep"]), mesh=mesh, in_specs=specs, out_specs=specs, check_vma=False
+    )

time: 574 us -> 277 us (0.48)
  waiting for transfers between devices: 247 us -> 0 us
  blocking collectives: 145 us -> 0 us
  Pallas kernels: 155 us -> 255 us
  between operations: 14.3 us -> 0.95 us
  local copies, waits for them, and re-layouts: 6.53 us -> 17.4 us
    reduce_scatter x8 -> x0, waiting for transfers between devices: 210 us -> none  [reduce_weights(): lax.psum_scatter(g, 'grp', scatter_dimension=0, tiled=True)]
    all_gather x5 -> x0, blocking collectives: 105 us -> none  [the longest x4 90.5 us: on_device(): lax.all_gather(w[layer], 'grp', axis=0, tiled=True)]
    pallas_call x2 -> x4, Pallas kernels: 83 us -> 183 us  [the longest x1 61.2 us: last(): pl.pallas_call(functools.partial(last_kernel, self.sizes, self.steps, chu...]
    psum x1 -> x0, blocking collectives: 39.1 us -> none  [on_device(): small = lax.psum(small, ('rep', 'grp'))]
    psum x1 -> x0, waiting for transfers between devices: 23.5 us -> none  [reduce_weights(): return [lax.psum(s, 'rep').astype(F32) for s in shares]]
    unnamed x44, local copies, waits for them, and re-layouts: 0.09 us -> 9.7 us
    all_gather x4 -> x0, waiting for transfers between devices: 7.87 us -> none  [on_device(): lax.all_gather(w[layer], 'grp', axis=0, tiled=True)]
  transfers between devices with their start and end apart: 13 -> 0, of which waited for: 10 -> 0; matrix products, arithmetic and copies ran while one was open for 1% -> 0% of each run, Pallas kernels for 6% -> 0%
where the time goes in v3:
time: 277 us; the launch traced here: 276 us
  Pallas kernels  255 us (92%)
  local copies, waits for them, and re-layouts  17.4 us (6%)
  other arithmetic  3.42 us (1%)
    pallas_call x1, Pallas kernels, middle(): pl.pallas_call(functools.partial(middle_kernel, self.sizes), name='layer_...  72 us
    pallas_call x1, Pallas kernels, last(): pl.pallas_call(functools.partial(last_kernel, self.sizes, self.steps, chu...  61.2 us
    pallas_call x1, Pallas kernels, reduce_grads(): pl.pallas_call(functools.partial(reduce_kernel, chunks, sizes), name='red...  46.4 us
    pallas_call x1, Pallas kernels, first(): pl.pallas_call(functools.partial(first_kernel, self.sizes, self.steps, ch...  44.3 us
    pallas_call x1, Pallas kernels, gather(): pl.pallas_call(functools.partial(gather_kernel, chunks, sizes), name='gat...  30.6 us
    unnamed x44, local copies, waits for them, and re-layouts  9.7 us

profile of v3, /device:TPU:0, one launch (start us, length us, event | category | flops | bytes accessed | tf_op | source)
XLA Modules:
  0.0 276.3 jit_solution(11879993361660166265)
XLA Ops:
  0.7 1.1 constant_dynamic-update-slice_fusion.2
  1.8 0.9 constant_dynamic-update-slice_fusion.1
  2.8 0.9 slice_bitcast_fusion
  4.1 0.8 slice_bitcast_fusion.2
  5.2 0.6 fusion.2
  5.8 30.6 %gather_params.1 = (bf16[4,12,8,3072]{3,2,1,0:T(8,128)(2,1)S(1)}, bf16[4,48,8,384]{3,2,1,0:T(8,128)(2,1)S(1)}, f32[4,12,96]{2,1,0:T(8,128)S(1)}) custom-call(bf16[1,12,8,3072]{3,2,1,0:T(8,128)(2,1)S(1)} %get-tuple-element.72.refs_0_, bf16[1,48,8,384]{3,2,1,0:T(8,128)(2,1)S(1)} %get-tuple-element.74.refs_1_, f32[1,12,96]{2,1,0:T(8,128)S(1)} %get-tuple-element.84.refs_2_), custom_call_target="tpu_custom_call" | custom-call | tf_op jit(solution)/shard_map/gather_params/pallas_call | solution.py:713
  36.4 1.4 copy-done
  37.8 1.0 copy-done.2
  39.1 0.7 maximum_maximum_fusion.refs_3_.refs_4_
  39.8 44.3 %layer_first.1 = (f32[2080,384]{1,0:T(8,128)}, bf16[2080,1152]{1,0:T(8,128)(2,1)}, f32[10,6,208,208]{3,2,1,0:T(8,128)}, bf16[10,384,208]{2,1,0:T(8,128)(2,1)}, f...) custom-call(bf16[10,197,384]{2,1,0:T(8,128)(2,1)} %refs_1_.3, ...), custom_call_target="tpu_custom_call" | custom-call | flops 6971719680 | bytes 41943040 | tf_op jit(solution)/shard_map/layer_first/pallas_call | solution.py:444
  84.1 0.7 slice_bitcast_fusion.4
  84.9 0.7 slice.78
  85.7 0.7 maximum_maximum_fusion.1.refs_4_
  86.4 72.0 %layer_middle.1 = (bf16[10,197,384]{2,1,0:T(8,128)(2,1)}, f32[2080,384]{1,0:T(8,128)}, bf16[384,3072]{1,0:T(8,128)(2,1)}, bf16[1536,384]{1,0:T(8,128)(2,1)}, f32[16,384]{1,0:T(8,128)}) custom-call(f32[2080,384]{1,0:T(8,128)} %get-tuple-element.46.refs_0_, bf16[10,197,384]{2,1,0:T(8,128)(2,1)} %refs_1_.2, bf16[384,3072]{1,0:T(8,128)(2,1)} %bitcast.80, ...), custom_call_target="tpu_custom_call" | custom-call | flops 20915159040 | bytes 41943040 | tf_op jit(solution)/shard_map/layer_middle/pallas_call | solution.py:459
  158.4 61.2 %layer_last.1 = (bf16[10,197,384]{2,1,0:T(8,128)(2,1)}, bf16[384,3072]{1,0:T(8,128)(2,1)}, bf16[1536,384]{1,0:T(8,128)(2,1)}, f32[16,384]{1,0:T(8,128)}, bf16[1,...) custom-call(f32[2080,384]{1,0:T(8,128)} %get-tuple-element.51.refs_0_, ...), custom_call_target="tpu_custom_call" | custom-call | flops 13943439360 | bytes 41943040 | tf_op jit(solution)/shard_map/layer_last/pallas_call | solution.py:477
  219.6 1.7 copy-done.1
  221.3 1.3 copy-done.3
  222.6 0.7 copy-done.4
  223.3 46.4 %reduce_grads.1 = (bf16[1,12,8,3072]{3,2,1,0:T(8,128)(2,1)S(1)}, bf16[1,48,8,384]{3,2,1,0:T(8,128)(2,1)S(1)}, f32[16,384]{1,0:T(8,128)S(1)}) custom-call(bf16[4,12,8,3072]{3,2,1,0:T(8,128)(2,1)S(1)} %bitcast.47, bf16[4,48,8,384]{3,2,1,0:T(8,128)(2,1)S(1)} %bitcast.52, f32[16,384]{1,0:T(8,128)S(1)} %copy-done.4), custom_call_target="tpu_custom_call" | custom-call | tf_op jit(solution)/shard_map/reduce_grads/pallas_call | solution.py:953
  269.8 1.1 maximum_convert_fusion.1
  271.5 0.7 maximum_convert_fusion.2
  272.4 1.1 slice.106
  273.5 1.0 slice.100
  275.2 1.1 copy.46
  (63 shorter events, 2.5 us)
Async XLA Ops:
  0.6 2.1 copy-start.7
  2.8 1.3 copy-start.8
  3.7 1.1 copy-start.11
  3.7 1.2 copy-start.12
  3.7 1.2 copy-start.13
  3.7 1.2 copy-start.14
  3.7 1.3 copy-start.15
  3.7 1.3 copy-start.16
  3.8 1.3 copy-start.17
  3.8 1.3 copy-start.18
  3.8 1.3 copy-start.19
  36.4 1.4 copy-start
  37.8 1.0 copy-start.2
  219.6 1.7 copy-start.1
  221.3 1.3 copy-start.3
  222.6 0.7 copy-start.4
  223.3 46.5 %copy-start.9 = (bf16[1,48,8,384]{3,2,1,0:T(8,128)(2,1)S(1)}, bf16[1,48,8,384]{3,2,1,0:T(8,128)(2,1)}, u32[]{:S(2)}) copy-start(bf16[1,48,8,384]{3,2,1,0:T(8,128)(2,1)} %get-tuple-element.70) | copy-start | bytes 884740
  269.8 1.1 copy-start.10
  269.8 1.7 copy-start.5
  273.5 1.7 copy-start.6

commit v4 on v3

--- a/solution.py
+++ b/solution.py
@@ -82,14 +82,9 @@
             keep["context"][image, pl.ds(head * HEAD_DIM, HEAD_DIM), :] = context.astype(BF16)
 
 
-def split_weights(wide, w_down):
-    width = w_down.shape[1]
-    return (
-        wide.at[:, pl.ds(0, 3 * width)],
-        wide.at[:, pl.ds(3 * width, width)],
-        wide.at[:, pl.ds(4 * width, w_down.shape[0])],
-        w_down,
-    )
+def split_attention(packed):
+    width = packed.shape[0]
+    return packed.at[:, pl.ds(0, 3 * width)], packed.at[:, pl.ds(3 * width, width)]
 
 
 def up_bias_of(vecs, hidden_width):
@@ -97,10 +92,9 @@
     return jnp.concatenate([vecs[VECTORS + i : VECTORS + i + 1] for i in range(rows)], axis=1)
 
 
-def layer_forward(hidden, weights, vecs, keep, images, seq, pad):
-    w_qkv, w_proj, w_up, w_down = weights
+def attention_part(hidden, packed, vecs, keep, images, seq, pad):
+    w_qkv, w_proj = split_attention(packed)
     width = hidden.shape[1]
-    up_bias = up_bias_of(vecs, w_down.shape[0])
     normed, _ = norm(hidden)
     rows_in = (normed * vecs[G1 : G1 + 1] + vecs[B1 : B1 + 1]).astype(BF16)
     qkv = keep["qkv"]
@@ -115,6 +109,11 @@
     context = jnp.concatenate([keep["context"][image].T for image in range(images)], axis=0)
     mixed = hidden + dot(context, w_proj[...]) + vecs[PB : PB + 1]
     keep["mixed"][...] = mixed
+    return mixed
+
+
+def mlp_part(mixed, w_up, w_down, vecs, keep):
+    up_bias = up_bias_of(vecs, w_down.shape[0])
     normed, _ = norm(mixed)
     rows_mid = (normed * vecs[G2 : G2 + 1] + vecs[B2 : B2 + 1]).astype(BF16)
     upward = dot(rows_mid, w_up[...]) + up_bias
@@ -157,24 +156,27 @@
     vec_grads[QB : QB + 1, :] += col_sum(query_grad)
 
 
-def layer_backward(out_grad, hidden, weights, vecs, keep, acc, images, pad):
-    w_qkv, w_proj, w_up, w_down = weights
-    g_qkv, g_proj, g_up, g_down, vec_grads, up_bias_grad, joint, context_grad = acc
+def mlp_backward(out_grad, w_up, w_down, vecs, keep, acc):
+    _, _, g_up, g_down, vec_grads, up_bias_grad = acc[:6]
     rounded = out_grad.astype(BF16)
     vec_grads[DB : DB + 1, :] += col_sum(out_grad)
     g_down[...] += dot(rounded.T, keep["active"][...])
     up_grad = dot_nt(rounded, w_down[...]) * keep["slope"][...].astype(F32)
     up_bias_grad[...] += col_sum(up_grad)
     up_rounded = up_grad.astype(BF16)
-    mixed = keep["mixed"][...]
-    normed, inv = norm(mixed)
+    normed, inv = norm(keep["mixed"][...])
     gain = vecs[G2 : G2 + 1]
     rows_mid = (normed * gain + vecs[B2 : B2 + 1]).astype(BF16)
     g_up[...] += dot(rows_mid.T, up_rounded)
     mid_grad = dot_nt(up_rounded, w_up[...])
     vec_grads[G2 : G2 + 1, :] += col_sum(mid_grad * normed)
     vec_grads[B2 : B2 + 1, :] += col_sum(mid_grad)
-    mixed_grad = out_grad + norm_backward(mid_grad, normed, inv, gain)
+    return out_grad + norm_backward(mid_grad, normed, inv, gain)
+
+
+def attention_backward(mixed_grad, hidden, packed, vecs, keep, acc, images, pad):
+    w_qkv, w_proj = split_attention(packed)
+    g_qkv, g_proj, _, _, vec_grads, _, joint, context_grad = acc
     vec_grads[PB : PB + 1, :] += col_sum(mixed_grad)
     mixed_rounded = mixed_grad.astype(BF16)
     part = g_proj[...]
@@ -230,138 +232,212 @@
             ref[...] = jnp.zeros_like(ref)
 
 
-def flush_grads(acc, outs):
-    @pl.when(pl.program_id(0) == pl.num_programs(0) - 1)
-    def _():
-        g_qkv, g_proj, g_up, g_down, vec_grads, up_bias_grad = acc[:6]
-        wide, down, vecs = outs
-        g_qkv_out, g_proj_out, g_up_out, g_down_out = split_weights(wide, down)
-        g_qkv_out[...] = g_qkv[...].astype(BF16)
-        g_proj_out[...] = g_proj[...].astype(BF16)
-        g_up_out[...] = g_up[...].astype(BF16)
-        g_down_out[...] = g_down[...].astype(BF16).T
-        width = vecs.shape[1]
-        extra = up_bias_grad.shape[1] // width
-        vecs[:VECTORS, :] = vec_grads[...]
-        for i in range(extra):
-            vecs[VECTORS + i : VECTORS + i + 1, :] = up_bias_grad[:, i * width : (i + 1) * width]
-        rest = vecs.shape[0] - VECTORS - extra
-        if rest:
-            vecs[VECTORS + extra :, :] = jnp.zeros((rest, width), F32)
-
-
-def step_at(step, body):
-    pl.when(pl.program_id(0) == step)(body)
-
-
-def first_kernel(sizes, steps, chunks, mesh_sizes, *refs):
+def flush_vectors(acc, vecs):
+    vec_grads, up_bias_grad = acc[4:6]
+    width = vecs.shape[1]
+    extra = up_bias_grad.shape[1] // width
+    vecs[:VECTORS, :] = vec_grads[...]
+    for i in range(extra):
+        vecs[VECTORS + i : VECTORS + i + 1, :] = up_bias_grad[:, i * width : (i + 1) * width]
+    rest = vecs.shape[0] - VECTORS - extra
+    if rest:
+        vecs[VECTORS + extra :, :] = jnp.zeros((rest, width), F32)
+
+
+def step_at(step):
+    return pl.when(pl.program_id(0) == step)
+
+
+def first_kernel(sizes, steps, mesh_sizes, chunks, *refs):
     group, seq, pad = sizes
-    images, wide, down, vecs = refs[:4]
-    out = refs[7]
-    keep = dict(zip(KEEP, refs[8:14]))
-    buf = refs[17]
-    work = Gather(chunks, mesh_sizes, refs[4:6], refs[6], refs[14:16], refs[16], refs[18:])
-    every = list(range(len(chunks)))
-    early = every[: len(every) // 2]
-    late = every[len(every) // 2 :]
-    plans = [
-        (0, lambda: work.begin()),
-        (steps // 5, lambda: [work.to_chips(i) for i in early]),
-        (2 * steps // 5, lambda: [work.to_chips(i) for i in late]),
-        (3 * steps // 5, lambda: [work.to_cores(i) for i in early]),
-    ]
-    for step, body in plans:
-        step_at(step, lambda body=body: (body(), None)[1])
-    load_padded(images, buf, pad)
-    out[...] = layer_forward(
-        buf[...], split_weights(wide, down), vecs, keep, group, seq, pad
-    )
-
-    @pl.when(pl.program_id(0) == steps - 1)
-    def _():
-        for i in late:
-            work.to_cores(i)
-        work.finish()
+    images, packed, vecs = refs[:3]
+    shards0, shards1 = refs[3:5], refs[5:9]
+    out = refs[9]
+    keep = dict(zip(KEEP, refs[10:16]))
+    mlp_out = refs[16:18]
+    full1 = refs[18:22]
+    buf, mixed_rows = refs[22:24]
+    landed = refs[24:26]
+    rest = refs[26:]
+    half = len(rest) // 2
+    now = Gather(chunks[0], mesh_sizes, shards0, None, landed, None, rest[:half])
+    later = Gather(
+        chunks[1], mesh_sizes, shards1[:3], shards1[3], full1[:3], full1[3], rest[half:]
+    )
+    step = pl.program_id(0)
+    rows = group * pad
+
+    @step_at(0)
+    def _():
+        now.greet()
+        now.begin()
+        later.begin()
+
+    @step_at(2 * steps // 5)
+    def _():
+        now.all_to_chips()
+
+    @step_at(4 * steps // 5)
+    def _():
+        later.all_to_chips()
+
+    @pl.when(step < steps)
+    def _():
+        load_padded(images, buf, pad)
+        mixed = attention_part(buf[...], packed, vecs, keep, group, seq, pad)
+        mixed_rows[pl.ds(pl.multiple_of(step * rows, rows), rows), :] = mixed
+
+    @step_at(steps)
+    def _():
+        now.all_to_cores()
+        now.finish()
+        for matrix, source in zip(mlp_out, landed):
+            flat = source[...].astype(F32).reshape(matrix.shape)
+            matrix[...] = flat.astype(BF16)
+
+    @step_at(2 * steps - 1)
+    def _():
+        later.all_to_cores()
+
+    @pl.when(step >= steps)
+    def _():
+        at = pl.multiple_of((step - steps) * rows, rows)
+        mixed = mixed_rows[pl.ds(at, rows), :]
+        out[...] = mlp_part(mixed, mlp_out[0], mlp_out[1], vecs, keep)
+
+    @step_at(2 * steps - 1)
+    def _():
+        later.finish()
 
 
 def middle_kernel(sizes, *refs):
     group, seq, pad = sizes
-    hidden, cotangent, wide, down, vecs, encoded, flowing = refs[:7]
-    outs = refs[7:10]
-    keep = dict(zip(KEEP, refs[10:16]))
-    acc = refs[16:24]
-    (buf,) = refs[24:]
-    weights = split_weights(wide, down)
+    hidden, cotangent, packed, w_up, w_down, vecs, encoded, flowing = refs[:8]
+    outs, vec_out = refs[8:11], refs[11]
+    keep = dict(zip(KEEP, refs[12:18]))
+    acc = refs[18:26]
+    (buf,) = refs[26:]
     init_grads(acc)
-    result = layer_forward(hidden[...], weights, vecs, keep, group, seq, pad)
+    mixed = attention_part(hidden[...], packed, vecs, keep, group, seq, pad)
+    result = mlp_part(mixed, w_up, w_down, vecs, keep)
     store_images(encoded, result, pad)
     load_padded(cotangent, buf, pad)
-    flowing[...] = layer_backward(buf[...], hidden[...], weights, vecs, keep, acc, group, pad)
-    flush_grads(acc, outs)
-
-
-def last_kernel(sizes, steps, chunks, mesh_sizes, *refs):
+    mixed_grad = mlp_backward(buf[...], w_up, w_down, vecs, keep, acc)
+    flowing[...] = attention_backward(
+        mixed_grad, hidden[...], packed, vecs, keep, acc, group, pad
+    )
+
+    @step_at(pl.num_programs(0) - 1)
+    def _():
+        g_qkv_out, g_proj_out = split_attention(outs[0])
+        g_qkv_out[...] = acc[0][...].astype(BF16)
+        g_proj_out[...] = acc[1][...].astype(BF16)
+        outs[1][...] = acc[2][...].astype(BF16)
+        outs[2][...] = acc[3][...].astype(BF16).T
+        flush_vectors(acc, vec_out)
+
+
+def last_kernel(sizes, steps, mesh_sizes, chunks, counts, *refs):
     group, seq, pad = sizes
-    flowing, images, wide, down, vecs = refs[:5]
-    keep = dict(zip(KEEP, refs[5:11]))
-    images_grad = refs[14]
-    outs = refs[15:18]
-    acc = refs[21:29]
-    buf = refs[29]
-    shares = refs[30:32]
-    work = Reduce(chunks, mesh_sizes, refs[11:13], refs[13], shares, refs[20], refs[32:])
-    every = range(len(chunks))
-
-    @pl.when(pl.program_id(0) == 0)
-    def _():
-        work.begin()
-
-    @pl.when(pl.program_id(0) == steps // 5)
-    def _():
-        for i in every:
-            work.to_chips(i)
-        work.vec_to_chips()
-
-    @pl.when(pl.program_id(0) == 3 * steps // 5)
-    def _():
-        for i in every:
-            work.to_shards(i)
-        work.vec_to_shards()
-
-    @pl.when(pl.program_id(0) == 4 * steps // 5)
-    def _():
-        for i in every:
-            work.to_spread(i)
-        work.vec_end()
+    flowing, images, packed, w_up, w_down, vecs = refs[:6]
+    keep = dict(zip(KEEP, refs[6:12]))
+    grads1, vec1 = refs[12:15], refs[15]
+    images_grad, sums, vec_out0, vec_out1 = refs[16], refs[17:20], refs[20], refs[21]
+    acc = refs[22:30]
+    buf, grad_rows, vec0 = refs[30:33]
+    grads0, shares0, shares1 = refs[33:36], refs[36:39], refs[39:42]
+    scratch = refs[42:]
+    ends = [sum(counts[: i + 1]) for i in range(3)]
+    later = Reduce(chunks[0], mesh_sizes, grads1, vec1, shares1, vec_out1, scratch[: ends[0]])
+    mlp = Reduce(
+        chunks[1], mesh_sizes, grads0[1:], None, shares0[1:], None, scratch[ends[0] : ends[1]]
+    )
+    tail = Reduce(
+        chunks[2], mesh_sizes, grads0[:1], vec0, shares0[:1], vec_out0, scratch[ends[1] :]
+    )
+    step = pl.program_id(0)
+    rows = group * pad
+    last = 2 * steps - 1
+
+    @step_at(0)
+    def _():
+        later.greet()
+        later.begin()
+
+    @step_at(1 * steps // 5)
+    def _():
+        later.all_to_chips()
 
     init_grads(acc)
-    load_padded(images, buf, pad)
-    result = layer_backward(
-        flowing[...], buf[...], split_weights(wide, down), vecs, keep, acc, group, pad
-    )
-    store_images(images_grad, result, pad)
-
-    @pl.when(pl.program_id(0) == steps - 1)
-    def _():
-        for i in every:
-            work.to_join(i)
-
-    flush_grads(acc, outs)
-
-    @pl.when(pl.program_id(0) == steps - 1)
-    def _():
-        work.finish()
-        for share, ref in zip(shares, refs[18:20]):
-            ref[...] = share[...]
+
+    @pl.when(step < steps)
+    def _():
+        mixed_grad = mlp_backward(flowing[...], w_up, w_down, vecs, keep, acc)
+        grad_rows[pl.ds(pl.multiple_of(step * rows, rows), rows), :] = mixed_grad
+
+    @step_at(steps)
+    def _():
+        grads0[1][...] = acc[2][...].reshape(grads0[1].shape).astype(BF16)
+        grads0[2][...] = acc[3][...].T.reshape(grads0[2].shape).astype(BF16)
+        mlp.begin()
+
+    @step_at(steps + 1 * steps // 5)
+    def _():
+        later.all_to_shards()
+        mlp.all_to_chips()
+
+    @step_at(steps + 3 * steps // 5)
+    def _():
+        later.all_to_spread()
+        mlp.all_to_shards()
+
+    @step_at(last)
+    def _():
+        later.all_to_join()
+
+    @pl.when(step >= steps)
+    def _():
+        load_padded(images, buf, pad)
+        at = pl.multiple_of((step - steps) * rows, rows)
+        result = attention_backward(
+            grad_rows[pl.ds(at, rows), :], buf[...], packed, vecs, keep, acc, group, pad
+        )
+        store_images(images_grad, result, pad)
+
+    @step_at(last)
+    def _():
+        shape = grads0[0].shape
+        three = acc[0].shape[1]
+        grads0[0][:, :, :, :three] = acc[0][...].reshape(shape[:3] + (three,)).astype(BF16)
+        grads0[0][:, :, :, three:] = (
+            acc[1][...].reshape(shape[:3] + (shape[3] - three,)).astype(BF16)
+        )
+        flush_vectors(acc, vec0)
+        tail.begin()
+        mlp.all_to_spread()
+        tail.all_to_chips()
+        later.finish()
+        for total, share in zip(sums, shares1):
+            total[1] = share[0].astype(F32)
+        tail.all_to_shards()
+        mlp.all_to_join()
+        tail.all_to_spread()
+        mlp.finish()
+        for total, share in zip(sums[1:], shares0[1:]):
+            total[0] = share[0].astype(F32)
+        tail.all_to_join()
+        tail.finish()
+        sums[0][0] = shares0[0][0].astype(F32)
 
 
 def whole(shape):
     return pl.BlockSpec(shape, lambda i: (0,) * len(shape), pipeline_mode=pl.Buffered(1))
 
 
-def rows_spec(shape, steps):
+def rows_spec(shape, steps, start=0):
     return pl.BlockSpec(
-        (shape[0] // steps,) + tuple(shape[1:]), lambda i: (i,) + (0,) * (len(shape) - 1)
+        (shape[0] // steps,) + tuple(shape[1:]),
+        lambda i: (jnp.clip(i - start, 0, steps - 1),) + (0,) * (len(shape) - 1),
     )
 
 
@@ -396,7 +472,8 @@
         ]
         self.vec_rows = -(-(VECTORS + hidden_width // self.width) // 8) * 8
         self.packed_shapes = [
-            (self.width, 4 * self.width + hidden_width),
+            (self.width, 4 * self.width),
+            (self.width, hidden_width),
             (hidden_width, self.width),
         ]
         self.vec_shape = (self.vec_rows, self.width)
@@ -407,17 +484,17 @@
             dimension_semantics=("arbitrary",), vmem_limit_bytes=60 * 2**20
         )
 
-    def image_spec(self):
-        return rows_spec((self.count, self.seq, self.width), self.steps)
-
-    def state_spec(self):
-        return rows_spec((self.rows, self.width), self.steps)
+    def image_spec(self, start=0):
+        return rows_spec((self.count, self.seq, self.width), self.steps, start)
+
+    def state_spec(self, start=0):
+        return rows_spec((self.rows, self.width), self.steps, start)
 
     def param_specs(self):
         return [whole(s) for s in self.packed_shapes + [self.vec_shape]]
 
-    def keep_specs(self):
-        return [rows_spec(self.keep[k][0], self.steps) for k in KEEP]
+    def keep_specs(self, starts):
+        return [rows_spec(self.keep[k][0], self.steps, at) for k, at in zip(KEEP, starts)]
 
     def grad_specs(self):
         return [whole(s.shape) for s in self.grad_shapes]
@@ -437,22 +514,31 @@
             has_side_effects=True,
         )
 
-    def first(self, images, weights, vecs, shards, mesh_sizes, collective_id):
+    def first(self, images, packed, vecs, shards0, shards1, mesh_sizes, collective_id):
         state = jax.ShapeDtypeStruct((self.rows, self.width), F32)
         keeps = [jax.ShapeDtypeStruct(*self.keep[k]) for k in KEEP]
-        chunks = chunks_of([(s.shape[1], s.shape[3]) for s in shards[:2]], mesh_sizes[1])
+        mlp = [jax.ShapeDtypeStruct(s, BF16) for s in self.packed_shapes[1:]]
+        chunks = [chunks_of(shards0, mesh_sizes), chunks_of(shards1[:3], mesh_sizes)]
+        n = self.steps
         out = pl.pallas_call(
-            functools.partial(first_kernel, self.sizes, self.steps, chunks, mesh_sizes),
+            functools.partial(first_kernel, self.sizes, n, mesh_sizes, chunks),
             name="layer_first",
-            out_shape=[state] + keeps + gathered_shapes(shards, mesh_sizes[0]),
-            grid=(self.steps,),
-            in_specs=[self.image_spec()] + self.param_specs() + [ANY_SPEC] * 3,
-            out_specs=[self.state_spec()] + self.keep_specs() + [ANY_SPEC] * 3,
-            scratch_shapes=[self.buffer] + Gather.semaphores(chunks, mesh_sizes),
+            out_shape=[state] + keeps + mlp + gathered_shapes(shards1, mesh_sizes[0]),
+            grid=(2 * n,),
+            in_specs=[self.image_spec(), whole(packed.shape), whole(self.vec_shape)]
+            + [ANY_SPEC] * 6,
+            out_specs=[self.state_spec(n)]
+            + self.keep_specs((0, 0, 0, 0, n, n))
+            + [whole(m.shape) for m in mlp]
+            + [ANY_SPEC] * 4,
+            scratch_shapes=[self.buffer, pltpu.VMEM((self.rows, self.width), F32)]
+            + [pltpu.VMEM(s.shape, BF16) for s in gathered_shapes(shards0, mesh_sizes[0])]
+            + Gather.semaphores(chunks[0], mesh_sizes)
+            + Gather.semaphores(chunks[1], mesh_sizes),
             compiler_params=self.comm_params(collective_id),
             cost_estimate=self.cost(1),
-        )(images, *weights, vecs, *shards)
-        return out[0], out[1:7], out[7:]
+        )(images, packed, vecs, *shards0, *shards1)
+        return out[0], out[1:7], out[7:9], out[9:]
 
     def middle(self, hidden, cotangent, weights, vecs):
         state = jax.ShapeDtypeStruct((self.rows, self.width), F32)
@@ -472,26 +558,51 @@
         return out[0], out[1], out[2:]
 
     def last(self, flowing, images, weights, vecs, keeps, grads, mesh_sizes, collective_id):
-        chunks = chunks_of([(g.shape[1], g.shape[3]) for g in grads[:2]], mesh_sizes[1])
-        shares = reduced_shapes(grads)
+        groups = mesh_sizes[0]
+        whole_grads = [
+            jax.ShapeDtypeStruct(g.shape, BF16) for g in grads[:3]
+        ]
+        chunks = [
+            chunks_of(whole_grads, mesh_sizes),
+            chunks_of(whole_grads[1:], mesh_sizes),
+            chunks_of(whole_grads[:1], mesh_sizes, 2),
+        ]
+        shares = [(1,) + g.shape[1:] for g in whole_grads]
+        sums = [jax.ShapeDtypeStruct((2,) + g.shape[1:], F32) for g in whole_grads]
+        vec = jax.ShapeDtypeStruct(self.vec_shape, F32)
+        scratch = [
+            Reduce.scratch(chunks[0], mesh_sizes, self.vec_shape),
+            Reduce.scratch(chunks[1], mesh_sizes, None),
+            Reduce.scratch(chunks[2], mesh_sizes, self.vec_shape),
+        ]
+        n = self.steps
+        outs = [jax.ShapeDtypeStruct(images.shape, BF16)] + sums + [vec, vec]
         out = pl.pallas_call(
-            functools.partial(last_kernel, self.sizes, self.steps, chunks, mesh_sizes),
+            functools.partial(
+                last_kernel, self.sizes, n, mesh_sizes, chunks, [len(x) for x in scratch]
+            ),
             name="layer_last",
-            out_shape=[jax.ShapeDtypeStruct(images.shape, BF16)] + self.grad_shapes + shares,
-            grid=(self.steps,),
-            in_specs=[self.state_spec(), self.image_spec()]
+            out_shape=outs,
+            grid=(2 * n,),
+            in_specs=[self.state_spec(), self.image_spec(n)]
             + self.param_specs()
-            + self.keep_specs()
+            + self.keep_specs((n, n, n, 0, 0, 0))
             + [whole(g.shape) for g in grads],
-            out_specs=[self.image_spec()] + self.grad_specs() + [whole(s.shape) for s in shares],
+            out_specs=[self.image_spec(n)] + [whole(o.shape) for o in outs[1:]],
             scratch_shapes=self.acc
-            + [self.buffer]
-            + [pltpu.VMEM(s.shape, s.dtype) for s in shares[:2]]
-            + Reduce.scratch(chunks, mesh_sizes, grads[2].shape),
+            + [
+                self.buffer,
+                pltpu.VMEM((self.rows, self.width), F32),
+                pltpu.VMEM(self.vec_shape, F32),
+            ]
+            + [pltpu.VMEM(g.shape, BF16) for g in whole_grads]
+            + [pltpu.VMEM(s, BF16) for s in shares]
+            + [pltpu.VMEM(s, BF16) for s in shares]
+            + sum(scratch, []),
             compiler_params=self.comm_params(collective_id),
             cost_estimate=self.cost(2),
         )(flowing, images, *weights, vecs, *keeps, *grads)
-        return out[0], out[1:4], out[4:]
+        return out[0], out[1:4], out[4], out[5]
 
 
 def greet(targets):
@@ -532,14 +643,13 @@
         return ref.at[shard, pl.ds(at + first, size)]
 
 
-def chunks_of(shapes, reps):
-    chips = reps // 2
+def chunks_of(arrays, mesh_sizes, want=1):
+    chips = mesh_sizes[1] // 2
     lists = []
-    for array, (blocks, columns) in enumerate(shapes):
-        by_columns = columns % 256 == 0
+    for array, (_, blocks, _, columns) in enumerate(a.shape for a in arrays):
+        by_columns = columns % 256 == 0 and columns > blocks * 8
         half = columns // 2 if by_columns else blocks // 2
         unit = 128 if by_columns else 1
-        want = 3 if by_columns else 2
         parts = want if half % (want * unit) == 0 else 1
         extent = half // parts
         lists.append(
@@ -548,10 +658,7 @@
                 for j in range(parts)
             ]
         )
-    merged = []
-    for j in range(max(len(part) for part in lists)):
-        merged += [part[j] for part in lists if j < len(part)]
-    return merged
+    return sum(lists, [])
 
 
 class Place:
@@ -639,7 +746,7 @@
         block = chunk.part(self.outs[chunk.array], place.core)
         return [transfer(block, block, self.core_sems, i, place.core_peer)]
 
-    def begin(self):
+    def greet(self):
         place = self.place
         most = max(self.chunks, key=lambda c: c.pieces)
         greet(
@@ -647,12 +754,22 @@
             + [place.at(place.mate(most, e)) for e in range(1, most.pieces)]
             + [place.core_peer]
         )
+
+    def begin(self):
         for i in range(len(self.chunks)):
             start(self.shards(i))
             self.own(i).start()
-            if i == 0:
-                start(self.vectors())
-                self.vector_own().start()
+        if self.vec_in is not None:
+            start(self.vectors())
+            self.vector_own().start()
+
+    def all_to_chips(self):
+        for i in range(len(self.chunks)):
+            self.to_chips(i)
+
+    def all_to_cores(self):
+        for i in range(len(self.chunks)):
+            self.to_cores(i)
 
     def to_chips(self, i):
         self.own(i).wait()
@@ -667,10 +784,11 @@
         every = range(len(self.chunks))
         for i in every:
             arrive(self.cores(i))
-        arrive(self.vectors())
-        self.vector_own().wait()
-        for copy in self.vectors():
-            copy.wait_send()
+        if self.vec_in is not None:
+            arrive(self.vectors())
+            self.vector_own().wait()
+            for copy in self.vectors():
+                copy.wait_send()
         for i in every:
             for copy in self.shards(i) + self.chips(i) + self.cores(i):
                 copy.wait_send()
@@ -687,12 +805,11 @@
 
 
 def gather_kernel(chunks, sizes, *refs):
-    work = Gather(chunks, sizes, refs[:2], refs[2], refs[3:5], refs[5], refs[6:])
+    work = Gather(chunks, sizes, refs[:1], refs[1], refs[2:3], refs[3], refs[4:])
+    work.greet()
     work.begin()
-    for i in range(len(chunks)):
-        work.to_chips(i)
-    for i in range(len(chunks)):
-        work.to_cores(i)
+    work.all_to_chips()
+    work.all_to_cores()
     work.finish()
 
 
@@ -708,19 +825,19 @@
     return [jax.ShapeDtypeStruct((groups,) + s.shape[1:], s.dtype) for s in shards]
 
 
-def gather(shards, sizes, collective_id):
-    chunks = chunks_of([(s.shape[1], s.shape[3]) for s in shards[:2]], sizes[1])
+def gather(shard, vec, sizes, collective_id):
+    chunks = chunks_of([shard], sizes, 2)
     return pl.pallas_call(
         functools.partial(gather_kernel, chunks, sizes),
         name="gather_params",
-        out_shape=gathered_shapes(shards, sizes[0]),
-        in_specs=[VMEM_SPEC] * 3,
-        out_specs=[VMEM_SPEC] * 3,
+        out_shape=gathered_shapes([shard, vec], sizes[0]),
+        in_specs=[VMEM_SPEC] * 2,
+        out_specs=[VMEM_SPEC] * 2,
         scratch_shapes=Gather.semaphores(chunks, sizes),
         compiler_params=pltpu.CompilerParams(
             collective_id=collective_id, has_side_effects=True, vmem_limit_bytes=40 * 2**20
         ),
-    )(*shards)
+    )(shard, vec)
 
 
 def add_up(first, rest):
@@ -735,19 +852,16 @@
         count = len(chunks)
         self.chunks, self.place = chunks, Place(sizes)
         self.ins, self.vec_in, self.outs, self.vec_out = ins, vec_in, outs, vec_out
-        self.from_core, self.core_sum, self.from_chips, self.chip_sum, self.from_shards = (
-            scratch[i * count : (i + 1) * count] for i in range(5)
-        )
-        self.vec_parts, self.vec_held = scratch[5 * count : 5 * count + 2]
-        sems = scratch[5 * count + 2 :]
-        (
-            self.core_sems,
-            self.chip_sems,
-            self.shard_sems,
-            self.spread_sems,
-            self.join_sems,
-            self.vec_sems,
-        ) = (sems[2 * i : 2 * i + 2] for i in range(6))
+        self.core_sum, self.from_chips, self.chip_sum, self.from_shards = (
+            scratch[i * count : (i + 1) * count] for i in range(4)
+        )
+        sems = scratch[4 * count :]
+        names = ("core_sems", "chip_sems", "shard_sems", "spread_sems", "join_sems")
+        for i, name in enumerate(names):
+            setattr(self, name, sems[2 * i : 2 * i + 2])
+        if vec_in is not None:
+            self.vec_sems = sems[10:12]
+            self.vec_parts, self.vec_held = sems[12:]
 
     @staticmethod
     def scratch(chunks, sizes, vec_shape):
@@ -758,22 +872,23 @@
         piece = [(groups, c.run, 8, c.columns) for c in chunks]
         shapes = (
             half
-            + half
             + [(chips - 1,) + p for p in piece]
             + piece
             + [(groups - 1,) + p[1:] for p in piece]
         )
-        terms = chips + groups - 1
-        return (
+        made = (
             [pltpu.VMEM(s, BF16) for s in shapes]
-            + [pltpu.VMEM((terms,) + vec_shape, F32), pltpu.VMEM((2,) + vec_shape, F32)]
             + dma_pair(count)
             + dma_pair(count, chips - 1)
             + dma_pair(count, groups - 1)
             + dma_pair(count, max(most - 1, 1))
             + dma_pair(count)
-            + dma_pair(terms)
-        )
+        )
+        if vec_shape is not None:
+            terms = chips + groups - 1
+            made += dma_pair(terms)
+            made += [pltpu.VMEM((terms,) + vec_shape, F32), pltpu.VMEM((2,) + vec_shape, F32)]
+        return made
 
     def chip_ids(self):
         place = self.place
@@ -782,7 +897,7 @@
     def cores(self, i):
         chunk, place = self.chunks[i], self.place
         src = chunk.part(self.ins[chunk.array], 1 - place.core)
-        return [transfer(src, self.from_core[i], self.core_sems, i, place.core_peer)]
+        return [transfer(src, self.core_sum[i], self.core_sems, i, place.core_peer)]
 
     def chips(self, i):
         chunk, copies = self.chunks[i], []
@@ -847,20 +962,45 @@
             for d, target in enumerate(self.place.shard_peers)
         ]
 
-    def begin(self):
+    def greet(self):
         place = self.place
         greet(
             place.shard_peers + [place.at(c) for c in self.chip_ids()] + [place.core_peer]
         )
+
+    def begin(self):
         for i in range(len(self.chunks)):
             start(self.cores(i))
-        start(self.vec_cores())
+        if self.vec_in is not None:
+            start(self.vec_cores())
+
+    def all_to_chips(self):
+        for i in range(len(self.chunks)):
+            self.to_chips(i)
+        if self.vec_in is not None:
+            self.vec_to_chips()
+
+    def all_to_shards(self):
+        for i in range(len(self.chunks)):
+            self.to_shards(i)
+        if self.vec_in is not None:
+            self.vec_to_shards()
+
+    def all_to_spread(self):
+        for i in range(len(self.chunks)):
+            self.to_spread(i)
+        if self.vec_in is not None:
+            self.vec_end()
+
+    def all_to_join(self):
+        for i in range(len(self.chunks)):
+            self.to_join(i)
 
     def to_chips(self, i):
         chunk = self.chunks[i]
         own = chunk.part(self.ins[chunk.array], self.place.core)[...]
         arrive(self.cores(i))
-        self.core_sum[i][...] = add_up(own, [self.from_core[i][...]]).astype(BF16)
+        self.core_sum[i][...] = own + self.core_sum[i][...]
         start(self.chips(i))
 
     def vec_to_chips(self):
@@ -912,55 +1052,14 @@
         every = range(len(self.chunks))
         for i in every:
             arrive(self.join(i))
-        copies = self.vec_cores() + self.vec_chips() + self.vec_shards()
+        copies = []
+        if self.vec_in is not None:
+            copies = self.vec_cores() + self.vec_chips() + self.vec_shards()
         for i in every:
             copies += self.cores(i) + self.chips(i) + self.shards(i)
             copies += self.spread(i) + self.join(i)
         for copy in copies:
             copy.wait_send()
-
-
-def reduce_kernel(chunks, sizes, *refs):
-    work = Reduce(chunks, sizes, refs[:2], refs[2], refs[3:5], refs[5], refs[6:])
-    count = len(chunks)
-    work.begin()
-    for i in range(count):
-        work.to_chips(i)
-    work.vec_to_chips()
-    for i in range(count):
-        work.to_shards(i)
-        if i == 0:
-            work.vec_to_shards()
-        if i > 0:
-            work.to_spread(i - 1)
-        if i > 1:
-            work.to_join(i - 2)
-    work.to_spread(count - 1)
-    work.vec_end()
-    for i in range(max(count - 2, 0), count):
-        work.to_join(i)
-    work.finish()
-
-
-def reduced_shapes(grads):
-    return [jax.ShapeDtypeStruct((1,) + g.shape[1:], BF16) for g in grads[:2]] + [
-        jax.ShapeDtypeStruct(grads[2].shape, F32)
-    ]
-
-
-def reduce_grads(grads, sizes, collective_id):
-    chunks = chunks_of([(g.shape[1], g.shape[3]) for g in grads[:2]], sizes[1])
-    return pl.pallas_call(
-        functools.partial(reduce_kernel, chunks, sizes),
-        name="reduce_grads",
-        out_shape=reduced_shapes(grads),
-        in_specs=[VMEM_SPEC] * 3,
-        out_specs=[VMEM_SPEC] * 3,
-        scratch_shapes=Reduce.scratch(chunks, sizes, grads[2].shape),
-        compiler_params=pltpu.CompilerParams(
-            collective_id=collective_id, has_side_effects=True, vmem_limit_bytes=40 * 2**20
-        ),
-    )(*grads)
 
 
 def on_device(
@@ -992,64 +1091,50 @@
     packed = jnp.stack(vectors, axis=1)
     packed = jnp.concatenate([packed, up_bias.reshape(layers, extra, part)], axis=1)
     packed = packed.astype(F32)
-    wide = jnp.concatenate([w_qkv, w_proj, w_up], axis=2)
+    joined = jnp.concatenate([w_qkv, w_proj], axis=2)
 
     def shards_of(layer):
-        return [
-            wide[layer].reshape(1, -1, 8, wide.shape[2]),
-            w_down[layer].reshape(1, -1, 8, width),
-            packed[layer][None],
-        ]
-
-    def unpack(gathered):
-        big, down, vecs = gathered
+        return [m[layer].reshape(1, -1, 8, m.shape[2]) for m in (joined, w_up, w_down)]
+
+    def unpack(vecs):
         vectors = vecs[:, :VECTORS].transpose(1, 0, 2).reshape(VECTORS, width)
         up = vecs[:, VECTORS:].reshape(extra, width)
         rest = plan.vec_rows - VECTORS - extra
-        vecs = jnp.concatenate([vectors, up, jnp.zeros((rest, width), F32)], axis=0)
-        return [big.reshape(width, -1), down.reshape(-1, width)], vecs
-
-    def blocks_of(grads):
-        return [
-            grads[0].reshape(groups, -1, 8, grads[0].shape[1]),
-            grads[1].reshape(groups, -1, 8, width),
-            grads[2],
-        ]
-
-    weights0, vecs0 = unpack(gather(shards_of(0), sizes, 0))
-    hidden, keeps, gathered = plan.first(images, weights0, vecs0, shards_of(1), sizes, 1)
-    weights1, vecs1 = unpack(gathered)
-    encoded, flowing, grads1 = plan.middle(hidden, cotangent, weights1, vecs1)
-    images_grad, grads0, reduced1 = plan.last(
-        flowing, images, weights0, vecs0, keeps, blocks_of(grads1), sizes, 2
-    )
-    reduced0 = reduce_grads(blocks_of(grads0), sizes, 3)
-    small0, small1 = reduced0[2], reduced1[2]
-    shares0, shares1 = (
-        [s.reshape(-1, s.shape[3]) for s in reduced[:2]] for reduced in (reduced0, reduced1)
-    )
+        return jnp.concatenate([vectors, up, jnp.zeros((rest, width), F32)], axis=0)
+
+    shards0, shards1 = shards_of(0), shards_of(1)
+    first_matrix, vecs0 = gather(shards0[0], packed[0][None], sizes, 0)
+    first_matrix, vecs0 = first_matrix.reshape(width, -1), unpack(vecs0)
+    hidden, keeps, mlp0, gathered = plan.first(
+        images, first_matrix, vecs0, shards0[1:], shards1 + [packed[1][None]], sizes, 1
+    )
+    weights1 = [g.reshape(-1, g.shape[3]) for g in gathered[:3]]
+    encoded, flowing, grads1 = plan.middle(hidden, cotangent, weights1, unpack(gathered[3]))
+    blocks = [g.reshape(groups, -1, 8, g.shape[1]) for g in grads1[:3]] + [grads1[3]]
+    images_grad, sums, small0, small1 = plan.last(
+        flowing, images, [first_matrix] + list(mlp0), vecs0, keeps, blocks, sizes, 2
+    )
+    full = [x.reshape(layers, -1, x.shape[3]) for x in sums]
     small = jnp.stack([small0, small1])
     me = lax.axis_index("grp")
     vec_out = lax.dynamic_slice_in_dim(small[:, :VECTORS], me * part, part, axis=2)
     up_out = small[:, VECTORS : VECTORS + extra].reshape(layers, -1)
     up_out = lax.dynamic_slice_in_dim(up_out, me * hidden_part, hidden_part, axis=1)
-    full = [jnp.stack([a, b]).astype(F32) for a, b in zip(shares0, shares1)]
-    columns = w_qkv.shape[2], w_qkv.shape[2] + width
     return (
         encoded,
         images_grad,
         vec_out[:, G1],
         vec_out[:, B1],
-        full[0][:, :, : columns[0]],
+        full[0][:, :, : 3 * width],
         vec_out[:, QB],
         vec_out[:, VB],
-        full[0][:, :, columns[0] : columns[1]],
+        full[0][:, :, 3 * width :],
         vec_out[:, PB],
         vec_out[:, G2],
         vec_out[:, B2],
-        full[0][:, :, columns[1] :],
+        full[1],
         up_out,
-        full[1],
+        full[2],
         vec_out[:, DB],
     )
 

time: 277 us -> 248 us (0.90)
  Pallas kernels: 255 us -> 226 us
    pallas_call x3 -> x2, Pallas kernels: 152 us -> 137 us  [the longest x1 83.3 us: last(): pl.pallas_call(functools.partial(last_kernel, self.sizes, n, mesh_sizes,...]
    pallas_call x1, Pallas kernels: 30.6 us -> 17.3 us  [gather(): pl.pallas_call(functools.partial(gather_kernel, chunks, sizes), name='gat...]
    unnamed x44 -> x35, local copies, waits for them, and re-layouts: 9.7 us -> 6.73 us
where the time goes in v4:
time: 248 us
  Pallas kernels  226 us (91%)
  local copies, waits for them, and re-layouts  18.7 us (8%)
    pallas_call x1, Pallas kernels, last(): pl.pallas_call(functools.partial(last_kernel, self.sizes, n, mesh_sizes,...  83.3 us
    pallas_call x1, Pallas kernels, middle(): pl.pallas_call(functools.partial(middle_kernel, self.sizes), name='layer_...  71.9 us
    pallas_call x1, Pallas kernels, first(): pl.pallas_call(functools.partial(first_kernel, self.sizes, n, mesh_sizes,...  53.4 us
    pallas_call x1, Pallas kernels, gather(): pl.pallas_call(functools.partial(gather_kernel, chunks, sizes), name='gat...  17.3 us
    unnamed x35, local copies, waits for them, and re-layouts  6.73 us

profile of v4, /device:TPU:0, one launch (start us, length us, event | category | flops | bytes accessed | tf_op | source)
XLA Modules:
  0.0 247.6 jit_solution(16497483644405925963)
XLA Ops:
  0.7 1.1 constant_dynamic-update-slice_fusion.1
  1.8 0.9 constant_dynamic-update-slice_fusion
  2.8 0.9 slice_bitcast_fusion
  4.1 0.6 fusion.2
  4.7 17.3 %gather_params.1 = (bf16[4,12,8,1536]{3,2,1,0:T(8,128)(2,1)S(1)}, f32[4,12,96]{2,1,0:T(8,128)S(1)}) custom-call(bf16[1,12,8,1536]{3,2,1,0:T(8,128)(2,1)S(1)} %get-tuple-element.74.refs_0_, f32[1,12,96]{2,1,0:T(8,128)S(1)} %get-tuple-element.84.refs_1_), custom_call_target="tpu_custom_call" | custom-call | tf_op jit(solution)/shard_map/gather_params/pallas_call | solution.py:830
  22.0 1.0 copy-done
  23.2 0.7 maximum_maximum_fusion.refs_2_.refs_5_
  23.9 0.9 slice_bitcast_fusion.2
  24.8 53.4 %layer_first.1 = (f32[2080,384]{1,0:T(8,128)}, bf16[2080,1152]{1,0:T(8,128)(2,1)}, f32[10,6,208,208]{3,2,1,0:T(8,128)}, bf16[10,384,208]{2,1,0:T(8,128)(2,1)}, f...) custom-call(bf16[10,197,384]{2,1,0:T(8,128)(2,1)} %refs_1_.3, ...), custom_call_target="tpu_custom_call" | custom-call | flops 6971719680 | bytes 41943040 | tf_op jit(solution)/shard_map/layer_first/pallas_call | solution.py:523
  78.2 0.7 slice_bitcast_fusion.6
  79.0 0.7 slice.83
  79.8 0.7 maximum_maximum_fusion.1.refs_5_
  80.5 71.9 %layer_middle.1 = (bf16[10,197,384]{2,1,0:T(8,128)(2,1)}, f32[2080,384]{1,0:T(8,128)}, bf16[384,1536]{1,0:T(8,128)(2,1)}, bf16[384,1536]{1,0:T(8,128)(2,1)}, bf1...) custom-call(f32[2080,384]{1,0:T(8,128)} %get-tuple-element.44.refs_0_, bf16[10,197,384]{2,1,0:T(8,128)(2,1)} %refs_1_.2, ...), custom_call_target="tpu_custom_call" | custom-call | flops 20915159040 | bytes 41943040 | tf_op jit(solution)/shard_map/layer_middle/pallas_call | solution.py:545
  152.3 83.3 %layer_last.1 = (bf16[10,197,384]{2,1,0:T(8,128)(2,1)}, f32[2,12,8,1536]{3,2,1,0:T(8,128)}, f32[2,12,8,1536]{3,2,1,0:T(8,128)}, f32[2,48,8,384]{3,2,1,0:T(8,128)}, f32[16,384]{1,0:T(8,128)}, /*index=5*/f32[16,384]{1,0:T(8,128)}) custom-call(f32[2080,384]{1,0:T(8,128)} %get-tuple-element.50.refs_0_, bf16[10,197,384]{2,1,0:T(8,128)(2,1)} %refs_1_.3, ...), custom_call_target="tpu_custom_call" | custom-call | flops 13943439360 | bytes 41943040 | tf_op jit(solution)/shard_map/layer_last/pallas_call | solution.py:580
  235.6 0.7 fusion
  237.0 0.7 pad_slice_fusion
  237.7 0.7 pad_slice_fusion.1
  239.1 2.3 slice.104
  241.3 1.7 slice.107
  243.0 1.1 copy.47
  244.1 0.7 copy-done.3
  244.8 1.0 copy.48
  245.9 0.7 copy-done.2
  246.5 1.0 copy.49
  (51 shorter events, 2.0 us)
Async XLA Ops:
  0.6 2.1 copy-start.5
  2.7 1.1 copy-start.6
  2.7 1.1 copy-start.7
  2.7 1.1 copy-start.8
  2.8 1.1 copy-start.9
  2.8 1.1 copy-start.10
  2.8 1.1 copy-start.11
  2.8 1.2 copy-start.12
  2.8 1.2 copy-start.13
  2.8 1.2 copy-start.14
  2.8 21.1 %copy-start.4 = (bf16[2,384,384]{2,1,0:T(8,128)(2,1)S(1)}, bf16[2,384,384]{2,1,0:T(8,128)(2,1)}, u32[]{:S(2)}) copy-start(bf16[2,384,384]{2,1,0:T(8,128)(2,1)} %param.28) | copy-start | bytes 1769476
  21.9 1.0 copy-start
  239.1 4.0 %copy-start.1 = (bf16[10,197,384]{2,1,0:T(8,128)(2,1)S(1)}, bf16[10,197,384]{2,1,0:T(8,128)(2,1)}, u32[]{:S(2)}) copy-start(bf16[10,197,384]{2,1,0:T(8,128)(2,1)} %get-tuple-element.103) | copy-start | bytes 4538884
  243.0 1.8 copy-start.3
  244.8 1.7 copy-start.2

commit v5 on v4

--- a/solution.py
+++ b/solution.py
@@ -174,9 +174,9 @@
     return out_grad + norm_backward(mid_grad, normed, inv, gain)
 
 
-def attention_backward(mixed_grad, hidden, packed, vecs, keep, acc, images, pad):
-    w_qkv, w_proj = split_attention(packed)
-    g_qkv, g_proj, _, _, vec_grads, _, joint, context_grad = acc
+def attention_backward(mixed_grad, hidden, packed, vecs, keep, acc, joint, images, pad):
+    _, w_proj = split_attention(packed)
+    g_qkv, g_proj, _, _, vec_grads, _, context_grad = acc
     vec_grads[PB : PB + 1, :] += col_sum(mixed_grad)
     mixed_rounded = mixed_grad.astype(BF16)
     part = g_proj[...]
@@ -186,14 +186,18 @@
     context_grad[...] = dot_nt(mixed_rounded, w_proj[...]).astype(BF16)
     for image in range(images):
         attn_backward(keep["qkv"], keep, context_grad, joint, vec_grads, image, pad)
+    normed, _ = norm(hidden)
+    rows_in = (normed * vecs[G1 : G1 + 1] + vecs[B1 : B1 + 1]).astype(BF16)
+    g_qkv[...] += dot(rows_in.T, joint[...])
+
+
+def input_backward(mixed_grad, hidden, packed, vecs, vec_grads, joint):
+    w_qkv, _ = split_attention(packed)
     normed, inv = norm(hidden)
-    gain = vecs[G1 : G1 + 1]
-    rows_in = (normed * gain + vecs[B1 : B1 + 1]).astype(BF16)
-    g_qkv[...] += dot(rows_in.T, joint[...])
     in_grad = dot_nt(joint[...], w_qkv[...])
     vec_grads[G1 : G1 + 1, :] += col_sum(in_grad * normed)
     vec_grads[B1 : B1 + 1, :] += col_sum(in_grad)
-    return mixed_grad + norm_backward(in_grad, normed, inv, gain)
+    return mixed_grad + norm_backward(in_grad, normed, inv, vecs[G1 : G1 + 1])
 
 
 def load_padded(ref, buf, pad):
@@ -277,10 +281,6 @@
     def _():
         now.all_to_chips()
 
-    @step_at(4 * steps // 5)
-    def _():
-        later.all_to_chips()
-
     @pl.when(step < steps)
     def _():
         load_padded(images, buf, pad)
@@ -290,6 +290,7 @@
     @step_at(steps)
     def _():
         now.all_to_cores()
+        later.all_to_chips()
         now.finish()
         for matrix, source in zip(mlp_out, landed):
             flat = source[...].astype(F32).reshape(matrix.shape)
@@ -315,17 +316,16 @@
     hidden, cotangent, packed, w_up, w_down, vecs, encoded, flowing = refs[:8]
     outs, vec_out = refs[8:11], refs[11]
     keep = dict(zip(KEEP, refs[12:18]))
-    acc = refs[18:26]
-    (buf,) = refs[26:]
+    acc = refs[18:25]
+    joint, buf = refs[25:]
     init_grads(acc)
     mixed = attention_part(hidden[...], packed, vecs, keep, group, seq, pad)
     result = mlp_part(mixed, w_up, w_down, vecs, keep)
     store_images(encoded, result, pad)
     load_padded(cotangent, buf, pad)
     mixed_grad = mlp_backward(buf[...], w_up, w_down, vecs, keep, acc)
-    flowing[...] = attention_backward(
-        mixed_grad, hidden[...], packed, vecs, keep, acc, group, pad
-    )
+    attention_backward(mixed_grad, hidden[...], packed, vecs, keep, acc, joint, group, pad)
+    flowing[...] = input_backward(mixed_grad, hidden[...], packed, vecs, acc[4], joint)
 
     @step_at(pl.num_programs(0) - 1)
     def _():
@@ -342,22 +342,33 @@
     flowing, images, packed, w_up, w_down, vecs = refs[:6]
     keep = dict(zip(KEEP, refs[6:12]))
     grads1, vec1 = refs[12:15], refs[15]
-    images_grad, sums, vec_out0, vec_out1 = refs[16], refs[17:20], refs[20], refs[21]
-    acc = refs[22:30]
-    buf, grad_rows, vec0 = refs[30:33]
-    grads0, shares0, shares1 = refs[33:36], refs[36:39], refs[39:42]
-    scratch = refs[42:]
+    images_grad, sums, vec_out0, vec_out1 = refs[16], refs[17:21], refs[21], refs[22]
+    acc = refs[23:30]
+    buf, grad_rows, joint_rows, vec0 = refs[30:34]
+    grads0, shares0, shares1 = refs[34:37], refs[37:40], refs[40:43]
+    scratch = refs[43:]
     ends = [sum(counts[: i + 1]) for i in range(3)]
     later = Reduce(chunks[0], mesh_sizes, grads1, vec1, shares1, vec_out1, scratch[: ends[0]])
     mlp = Reduce(
         chunks[1], mesh_sizes, grads0[1:], None, shares0[1:], None, scratch[ends[0] : ends[1]]
     )
     tail = Reduce(
-        chunks[2], mesh_sizes, grads0[:1], vec0, shares0[:1], vec_out0, scratch[ends[1] :]
+        chunks[2],
+        mesh_sizes,
+        grads0[:1],
+        vec0,
+        shares0[:1],
+        vec_out0,
+        scratch[ends[1] :],
+        vec_along=False,
     )
     step = pl.program_id(0)
     rows = group * pad
-    last = 2 * steps - 1
+    last = 3 * steps - 1
+    three = acc[0].shape[1]
+
+    def rows_at(start):
+        return pl.ds(pl.multiple_of((step - start) * rows, rows), rows)
 
     @step_at(0)
     def _():
@@ -372,8 +383,7 @@
 
     @pl.when(step < steps)
     def _():
-        mixed_grad = mlp_backward(flowing[...], w_up, w_down, vecs, keep, acc)
-        grad_rows[pl.ds(pl.multiple_of(step * rows, rows), rows), :] = mixed_grad
+        grad_rows[rows_at(0), :] = mlp_backward(flowing[...], w_up, w_down, vecs, keep, acc)
 
     @step_at(steps)
     def _():
@@ -389,55 +399,94 @@
     @step_at(steps + 3 * steps // 5)
     def _():
         later.all_to_spread()
-        mlp.all_to_shards()
-
-    @step_at(last)
+
+    @step_at(2 * steps - 1)
     def _():
         later.all_to_join()
 
-    @pl.when(step >= steps)
+    @pl.when((step >= steps) & (step < 2 * steps))
     def _():
         load_padded(images, buf, pad)
-        at = pl.multiple_of((step - steps) * rows, rows)
-        result = attention_backward(
-            grad_rows[pl.ds(at, rows), :], buf[...], packed, vecs, keep, acc, group, pad
-        )
-        store_images(images_grad, result, pad)
-
-    @step_at(last)
+        attention_backward(
+            grad_rows[rows_at(steps), :],
+            buf[...],
+            packed,
+            vecs,
+            keep,
+            acc,
+            joint_rows.at[rows_at(steps), :],
+            group,
+            pad,
+        )
+
+    @step_at(2 * steps)
     def _():
         shape = grads0[0].shape
-        three = acc[0].shape[1]
         grads0[0][:, :, :, :three] = acc[0][...].reshape(shape[:3] + (three,)).astype(BF16)
         grads0[0][:, :, :, three:] = (
             acc[1][...].reshape(shape[:3] + (shape[3] - three,)).astype(BF16)
         )
+        tail.begin()
+        mlp.all_to_shards()
+
+    @step_at(2 * steps + 2 * steps // 5)
+    def _():
+        tail.all_to_chips()
+
+    @step_at(last)
+    def _():
+        mlp.all_to_spread()
+
+    @pl.when(step >= 2 * steps)
+    def _():
+        load_padded(images, buf, pad)
+        result = input_backward(
+            grad_rows[rows_at(2 * steps), :],
+            buf[...],
+            packed,
+            vecs,
+            acc[4],
+            joint_rows.at[rows_at(2 * steps), :],
+        )
+        store_images(images_grad, result, pad)
+
+    def store_sums(layer, shares):
+        sums[0][layer] = shares[0][0, :, :, :three].astype(F32)
+        sums[1][layer] = shares[0][0, :, :, three:].astype(F32)
+
+    @step_at(last)
+    def _():
         flush_vectors(acc, vec0)
-        tail.begin()
-        mlp.all_to_spread()
-        tail.all_to_chips()
+        tail.vec_begin()
+        tail.all_to_shards()
+        tail.vec_to_chips()
+        mlp.all_to_join()
         later.finish()
-        for total, share in zip(sums, shares1):
+        store_sums(1, shares1)
+        for total, share in zip(sums[2:], shares1[1:]):
             total[1] = share[0].astype(F32)
-        tail.all_to_shards()
-        mlp.all_to_join()
+        tail.vec_to_shards()
         tail.all_to_spread()
         mlp.finish()
-        for total, share in zip(sums[1:], shares0[1:]):
+        for total, share in zip(sums[2:], shares0[1:]):
             total[0] = share[0].astype(F32)
         tail.all_to_join()
+        tail.vec_end()
         tail.finish()
-        sums[0][0] = shares0[0][0].astype(F32)
+        store_sums(0, shares0)
 
 
 def whole(shape):
     return pl.BlockSpec(shape, lambda i: (0,) * len(shape), pipeline_mode=pl.Buffered(1))
 
 
-def rows_spec(shape, steps, start=0):
+def rows_spec(shape, steps, start=0, again=False):
+    def block(i):
+        at = jnp.maximum(i - start, 0)
+        return lax.rem(at, steps) if again else jnp.minimum(at, steps - 1)
+
     return pl.BlockSpec(
-        (shape[0] // steps,) + tuple(shape[1:]),
-        lambda i: (jnp.clip(i - start, 0, steps - 1),) + (0,) * (len(shape) - 1),
+        (shape[0] // steps,) + tuple(shape[1:]), lambda i: (block(i),) + (0,) * (len(shape) - 1)
     )
 
 
@@ -467,9 +516,9 @@
             pltpu.VMEM((self.width, hidden_width), F32),
             pltpu.VMEM((8, self.width), F32),
             pltpu.VMEM((1, hidden_width), F32),
-            pltpu.VMEM((block_rows, 3 * self.width), BF16),
             pltpu.VMEM((block_rows, self.width), BF16),
         ]
+        self.joint = pltpu.VMEM((block_rows, 3 * self.width), BF16)
         self.vec_rows = -(-(VECTORS + hidden_width // self.width) // 8) * 8
         self.packed_shapes = [
             (self.width, 4 * self.width),
@@ -484,8 +533,8 @@
             dimension_semantics=("arbitrary",), vmem_limit_bytes=60 * 2**20
         )
 
-    def image_spec(self, start=0):
-        return rows_spec((self.count, self.seq, self.width), self.steps, start)
+    def image_spec(self, start=0, again=False):
+        return rows_spec((self.count, self.seq, self.width), self.steps, start, again)
 
     def state_spec(self, start=0):
         return rows_spec((self.rows, self.width), self.steps, start)
@@ -551,7 +600,7 @@
             out_specs=[self.image_spec(), self.state_spec()] + self.grad_specs(),
             scratch_shapes=[pltpu.VMEM(*self.keep_block[k]) for k in KEEP]
             + self.acc
-            + [self.buffer],
+            + [self.joint, self.buffer],
             compiler_params=self.params,
             cost_estimate=self.cost(3),
         )(hidden, cotangent, *weights, vecs)
@@ -563,12 +612,21 @@
             jax.ShapeDtypeStruct(g.shape, BF16) for g in grads[:3]
         ]
         chunks = [
-            chunks_of(whole_grads, mesh_sizes),
-            chunks_of(whole_grads[1:], mesh_sizes),
-            chunks_of(whole_grads[:1], mesh_sizes, 2),
+            chunks_of(whole_grads, mesh_sizes, 1, (1,)),
+            chunks_of(whole_grads[1:], mesh_sizes, 1, (0,)),
+            chunks_of(whole_grads[:1], mesh_sizes, 3, (0,)),
         ]
         shares = [(1,) + g.shape[1:] for g in whole_grads]
-        sums = [jax.ShapeDtypeStruct((2,) + g.shape[1:], F32) for g in whole_grads]
+        blocks = whole_grads[0].shape[1:3]
+        sums = [
+            jax.ShapeDtypeStruct((2,) + shape, F32)
+            for shape in (
+                blocks + (3 * self.width,),
+                blocks + (self.width,),
+                whole_grads[1].shape[1:],
+                whole_grads[2].shape[1:],
+            )
+        ]
         vec = jax.ShapeDtypeStruct(self.vec_shape, F32)
         scratch = [
             Reduce.scratch(chunks[0], mesh_sizes, self.vec_shape),
@@ -583,16 +641,17 @@
             ),
             name="layer_last",
             out_shape=outs,
-            grid=(2 * n,),
-            in_specs=[self.state_spec(), self.image_spec(n)]
+            grid=(3 * n,),
+            in_specs=[self.state_spec(), self.image_spec(n, True)]
             + self.param_specs()
             + self.keep_specs((n, n, n, 0, 0, 0))
             + [whole(g.shape) for g in grads],
-            out_specs=[self.image_spec(n)] + [whole(o.shape) for o in outs[1:]],
+            out_specs=[self.image_spec(2 * n)] + [whole(o.shape) for o in outs[1:]],
             scratch_shapes=self.acc
             + [
                 self.buffer,
                 pltpu.VMEM((self.rows, self.width), F32),
+                pltpu.VMEM((self.rows, 3 * self.width), BF16),
                 pltpu.VMEM(self.vec_shape, F32),
             ]
             + [pltpu.VMEM(g.shape, BF16) for g in whole_grads]
@@ -602,7 +661,7 @@
             compiler_params=self.comm_params(collective_id),
             cost_estimate=self.cost(2),
         )(flowing, images, *weights, vecs, *keeps, *grads)
-        return out[0], out[1:4], out[4], out[5]
+        return out[0], out[1:5], out[5], out[6]
 
 
 def greet(targets):
@@ -626,7 +685,8 @@
 
 
 class Chunk:
-    def __init__(self, array, blocks, columns, by_columns, extent, start, chips):
+    def __init__(self, array, blocks, columns, by_columns, extent, start, chips, shards_first):
+        self.shards_first = shards_first
         self.array, self.by_columns, self.start, self.extent = array, by_columns, start, extent
         self.blocks = blocks if by_columns else extent
         self.columns = extent if by_columns else columns
@@ -643,7 +703,7 @@
         return ref.at[shard, pl.ds(at + first, size)]
 
 
-def chunks_of(arrays, mesh_sizes, want=1):
+def chunks_of(arrays, mesh_sizes, want=1, shards_first=()):
     chips = mesh_sizes[1] // 2
     lists = []
     for array, (_, blocks, _, columns) in enumerate(a.shape for a in arrays):
@@ -654,7 +714,10 @@
         extent = half // parts
         lists.append(
             [
-                Chunk(array, blocks, columns, by_columns, extent, j * extent, chips)
+                Chunk(
+                    array, blocks, columns, by_columns, extent, j * extent, chips,
+                    array * want + j in shards_first,
+                )
                 for j in range(parts)
             ]
         )
@@ -848,7 +911,8 @@
 
 
 class Reduce:
-    def __init__(self, chunks, sizes, ins, vec_in, outs, vec_out, scratch):
+    def __init__(self, chunks, sizes, ins, vec_in, outs, vec_out, scratch, vec_along=True):
+        self.vec_along = vec_along and vec_in is not None
         count = len(chunks)
         self.chunks, self.place = chunks, Place(sizes)
         self.ins, self.vec_in, self.outs, self.vec_out = ins, vec_in, outs, vec_out
@@ -868,14 +932,17 @@
         groups, reps = sizes
         chips, count = reps // 2, len(chunks)
         most = max(c.pieces for c in chunks)
-        half = [(groups, c.blocks, 8, c.columns) for c in chunks]
-        piece = [(groups, c.run, 8, c.columns) for c in chunks]
-        shapes = (
-            half
-            + [(chips - 1,) + p for p in piece]
-            + piece
-            + [(groups - 1,) + p[1:] for p in piece]
-        )
+        shapes = [(groups, c.blocks, 8, c.columns) for c in chunks]
+        for lead in ("chips", "sum", "shards"):
+            for c in chunks:
+                piece, block = (c.run, 8, c.columns), (c.blocks, 8, c.columns)
+                shapes.append(
+                    {
+                        "chips": (chips - 1,) + (piece if c.shards_first else (groups,) + piece),
+                        "sum": block if c.shards_first else (groups,) + piece,
+                        "shards": (groups - 1,) + (block if c.shards_first else piece),
+                    }[lead]
+                )
         made = (
             [pltpu.VMEM(s, BF16) for s in shapes]
             + dma_pair(count)
@@ -903,16 +970,18 @@
         chunk, copies = self.chunks[i], []
         for e, chip in enumerate(self.chip_ids()):
             piece = lax.rem(chip, chunk.pieces)
-            src = self.core_sum[i].at[:, pl.ds(piece * chunk.run, chunk.run)]
+            run = pl.ds(piece * chunk.run, chunk.run)
+            src = self.chip_sum[i].at[run] if chunk.shards_first else self.core_sum[i].at[:, run]
             dst = self.from_chips[i].at[e]
             copies.append(transfer(src, dst, self.chip_sems, (i, e), self.place.at(chip)))
         return copies
 
     def shards(self, i):
         place = self.place
+        source = self.core_sum[i] if self.chunks[i].shards_first else self.chip_sum[i]
         return [
             transfer(
-                self.chip_sum[i].at[lax.rem(place.mine + d + 1, place.groups)],
+                source.at[lax.rem(place.mine + d + 1, place.groups)],
                 self.from_shards[i].at[d],
                 self.shard_sems,
                 (i, d),
@@ -971,25 +1040,28 @@
     def begin(self):
         for i in range(len(self.chunks)):
             start(self.cores(i))
-        if self.vec_in is not None:
-            start(self.vec_cores())
+        if self.vec_along:
+            self.vec_begin()
+
+    def vec_begin(self):
+        start(self.vec_cores())
 
     def all_to_chips(self):
         for i in range(len(self.chunks)):
             self.to_chips(i)
-        if self.vec_in is not None:
+        if self.vec_along:
             self.vec_to_chips()
 
     def all_to_shards(self):
         for i in range(len(self.chunks)):
             self.to_shards(i)
-        if self.vec_in is not None:
+        if self.vec_along:
             self.vec_to_shards()
 
     def all_to_spread(self):
         for i in range(len(self.chunks)):
             self.to_spread(i)
-        if self.vec_in is not None:
+        if self.vec_along:
             self.vec_end()
 
     def all_to_join(self):
@@ -1001,7 +1073,7 @@
         own = chunk.part(self.ins[chunk.array], self.place.core)[...]
         arrive(self.cores(i))
         self.core_sum[i][...] = own + self.core_sum[i][...]
-        start(self.chips(i))
+        start(self.shards(i) if chunk.shards_first else self.chips(i))
 
     def vec_to_chips(self):
         arrive(self.vec_cores())
@@ -1011,12 +1083,15 @@
     def to_shards(self, i):
         chunk = self.chunks[i]
         piece = self.place.piece(chunk)
-        own = self.core_sum[i][:, pl.ds(piece * chunk.run, chunk.run)]
-        copies = self.chips(i)
+        if chunk.shards_first:
+            own, copies, terms = self.core_sum[i][self.place.mine], self.shards(i), self.from_shards[i]
+        else:
+            own = self.core_sum[i][:, pl.ds(piece * chunk.run, chunk.run)]
+            copies, terms = self.chips(i), self.from_chips[i]
         arrive(copies)
-        total = add_up(own, [self.from_chips[i][e] for e in range(len(copies))])
+        total = add_up(own, [terms[e] for e in range(len(copies))])
         self.chip_sum[i][...] = total.astype(BF16)
-        start(self.shards(i))
+        start(self.chips(i) if chunk.shards_first else self.shards(i))
 
     def vec_to_shards(self):
         copies = self.vec_chips()
@@ -1028,11 +1103,13 @@
 
     def to_spread(self, i):
         chunk, place = self.chunks[i], self.place
-        copies = self.shards(i)
+        if chunk.shards_first:
+            own = self.chip_sum[i][pl.ds(place.piece(chunk) * chunk.run, chunk.run)]
+            copies, terms = self.chips(i), self.from_chips[i]
+        else:
+            own, copies, terms = self.chip_sum[i][place.mine], self.shards(i), self.from_shards[i]
         arrive(copies)
-        total = add_up(
-            self.chip_sum[i][place.mine], [self.from_shards[i][d] for d in range(len(copies))]
-        )
+        total = add_up(own, [terms[d] for d in range(len(copies))])
         block = chunk.part(self.outs[chunk.array], place.core, place.piece(chunk), 0)
         block[...] = total.astype(BF16)
         start(self.spread(i))
@@ -1125,16 +1202,16 @@
         images_grad,
         vec_out[:, G1],
         vec_out[:, B1],
-        full[0][:, :, : 3 * width],
+        full[0],
         vec_out[:, QB],
         vec_out[:, VB],
-        full[0][:, :, 3 * width :],
+        full[1],
         vec_out[:, PB],
         vec_out[:, G2],
         vec_out[:, B2],
-        full[1],
+        full[2],
         up_out,
-        full[2],
+        full[3],
         vec_out[:, DB],
     )
 

time: 248 us -> 244 us (0.984)
    pallas_call x1, Pallas kernels: 83.3 us -> 79.3 us  [last(): pl.pallas_call(functools.partial(last_kernel, self.sizes, n, mesh_sizes,...]
    slice x2 -> x0, local copies, waits for them, and re-layouts: 3.95 us -> none  [the longest x1 2.25 us: on_device(): full[0][:, :, :3 * width]]
    unnamed x35 -> x39, local copies, waits for them, and re-layouts: 6.73 us -> 8.83 us
where the time goes in v5:
time: 244 us
  Pallas kernels  224 us (92%)
  local copies, waits for them, and re-layouts  16.9 us (7%)
    pallas_call x1, Pallas kernels, last(): pl.pallas_call(functools.partial(last_kernel, self.sizes, n, mesh_sizes,...  79.3 us
    pallas_call x1, Pallas kernels, middle(): pl.pallas_call(functools.partial(middle_kernel, self.sizes), name='layer_...  72 us
    pallas_call x1, Pallas kernels, first(): pl.pallas_call(functools.partial(first_kernel, self.sizes, n, mesh_sizes,...  55.3 us
    pallas_call x1, Pallas kernels, gather(): pl.pallas_call(functools.partial(gather_kernel, chunks, sizes), name='gat...  17.3 us
    unnamed x39, local copies, waits for them, and re-layouts  8.83 us

profile of v5, /device:TPU:0, one launch (start us, length us, event | category | flops | bytes accessed | tf_op | source)
XLA Modules:
  0.0 243.7 jit_solution(14460671652348721485)
XLA Ops:
  0.7 1.1 constant_dynamic-update-slice_fusion.1
  1.9 1.0 constant_dynamic-update-slice_fusion
  2.9 0.9 slice_bitcast_fusion
  4.1 0.6 fusion.2
  4.7 17.3 %gather_params.1 = (bf16[4,12,8,1536]{3,2,1,0:T(8,128)(2,1)S(1)}, f32[4,12,96]{2,1,0:T(8,128)S(1)}) custom-call(bf16[1,12,8,1536]{3,2,1,0:T(8,128)(2,1)S(1)} %get-tuple-element.76.refs_0_, f32[1,12,96]{2,1,0:T(8,128)S(1)} %get-tuple-element.86.refs_1_), custom_call_target="tpu_custom_call" | custom-call | tf_op jit(solution)/shard_map/gather_params/pallas_call | solution.py:893
  22.0 1.0 copy-done
  23.2 0.7 maximum_maximum_fusion.refs_2_.refs_5_
  23.9 0.9 slice_bitcast_fusion.2
  24.8 55.3 %layer_first.1 = (f32[2080,384]{1,0:T(8,128)}, bf16[2080,1152]{1,0:T(8,128)(2,1)}, f32[10,6,208,208]{3,2,1,0:T(8,128)}, bf16[10,384,208]{2,1,0:T(8,128)(2,1)}, f...) custom-call(bf16[10,197,384]{2,1,0:T(8,128)(2,1)} %refs_1_.3, ...), custom_call_target="tpu_custom_call" | custom-call | flops 6971719680 | bytes 41943040 | tf_op jit(solution)/shard_map/layer_first/pallas_call | solution.py:572
  80.1 0.7 slice_bitcast_fusion.6
  80.9 0.7 slice.77
  81.7 0.7 maximum_maximum_fusion.1.refs_5_
  82.4 72.0 %layer_middle.1 = (bf16[10,197,384]{2,1,0:T(8,128)(2,1)}, f32[2080,384]{1,0:T(8,128)}, bf16[384,1536]{1,0:T(8,128)(2,1)}, bf16[384,1536]{1,0:T(8,128)(2,1)}, bf1...) custom-call(f32[2080,384]{1,0:T(8,128)} %get-tuple-element.45.refs_0_, bf16[10,197,384]{2,1,0:T(8,128)(2,1)} %refs_1_.2, ...), custom_call_target="tpu_custom_call" | custom-call | flops 20915159040 | bytes 41943040 | tf_op jit(solution)/shard_map/layer_middle/pallas_call | solution.py:594
  154.3 79.3 %layer_last.1 = (bf16[10,197,384]{2,1,0:T(8,128)(2,1)}, f32[2,12,8,1152]{3,2,1,0:T(8,128)}, f32[2,12,8,384]{3,2,1,0:T(8,128)}, f32[2,12,8,1536]{3,2,1,0:T(8,128)...) custom-call(f32[2080,384]{1,0:T(8,128)} %get-tuple-element.51.refs_0_, ...), custom_call_target="tpu_custom_call" | custom-call | flops 13943439360 | bytes 41943040 | tf_op jit(solution)/shard_map/layer_last/pallas_call | solution.py:638
  233.6 0.7 fusion
  234.4 0.6 constant_dynamic-slice_fusion
  234.9 0.7 pad_slice_fusion
  235.7 0.7 pad_slice_fusion.1
  236.4 0.6 fusion.1
  237.0 2.8 %copy.49 = bf16[10,197,384]{2,1,0:T(8,128)(2,1)} copy(bf16[10,197,384]{2,1,0:T(8,128)(2,1)} %get-tuple-element.105) | data formatting | bytes 3025920
  239.8 0.9 copy.50
  240.9 0.7 copy.51
  241.6 1.0 copy.52
  242.7 1.0 copy.53
  (53 shorter events, 1.0 us)
Async XLA Ops:
  0.6 2.2 copy-start.5
  1.8 2.0 copy-start.7
  1.8 2.1 copy-start.8
  1.8 2.1 copy-start.9
  1.8 2.1 copy-start.10
  1.8 2.1 copy-start.11
  1.8 2.1 copy-start.12
  1.8 2.1 copy-start.13
  1.9 2.2 copy-start.14
  1.9 2.2 copy-start.15
  2.9 21.1 %copy-start.4 = (bf16[2,384,384]{2,1,0:T(8,128)(2,1)S(1)}, bf16[2,384,384]{2,1,0:T(8,128)(2,1)}, u32[]{:S(2)}) copy-start(bf16[2,384,384]{2,1,0:T(8,128)(2,1)} %param.28) | copy-start | bytes 1769476
  22.0 1.0 copy-start
  237.0 2.8 %copy-start.3 = (f32[2,12,8,1152]{3,2,1,0:T(8,128)S(1)}, f32[2,12,8,1152]{3,2,1,0:T(8,128)}, u32[]{:S(2)}) copy-start(f32[2,12,8,1152]{3,2,1,0:T(8,128)} %get-tuple-element.67) | copy-start | bytes 2654212
  239.8 1.1 copy-start.6
  239.8 1.8 copy-start.2
  240.9 1.7 copy-start.1

commit v6 on v5

--- a/solution.py
+++ b/solution.py
@@ -287,18 +287,29 @@
         mixed = attention_part(buf[...], packed, vecs, keep, group, seq, pad)
         mixed_rows[pl.ds(pl.multiple_of(step * rows, rows), rows), :] = mixed
 
+    @step_at(4 * steps // 5)
+    def _():
+        now.to_cores(0)
+        later.to_chips(0)
+        later.to_chips(1)
+
     @step_at(steps)
     def _():
-        now.all_to_cores()
-        later.all_to_chips()
+        now.to_cores(1)
         now.finish()
         for matrix, source in zip(mlp_out, landed):
             flat = source[...].astype(F32).reshape(matrix.shape)
             matrix[...] = flat.astype(BF16)
 
+    @step_at(steps + 3 * steps // 5)
+    def _():
+        later.to_chips(2)
+        later.to_cores(2)
+
     @step_at(2 * steps - 1)
     def _():
-        later.all_to_cores()
+        later.to_cores(0)
+        later.to_cores(1)
 
     @pl.when(step >= steps)
     def _():
@@ -402,6 +413,7 @@
 
     @step_at(2 * steps - 1)
     def _():
+        mlp.all_to_shards()
         later.all_to_join()
 
     @pl.when((step >= steps) & (step < 2 * steps))
@@ -427,15 +439,18 @@
             acc[1][...].reshape(shape[:3] + (shape[3] - three,)).astype(BF16)
         )
         tail.begin()
-        mlp.all_to_shards()
+
+    @step_at(2 * steps + steps // 5)
+    def _():
+        tail.all_to_chips()
 
     @step_at(2 * steps + 2 * steps // 5)
     def _():
-        tail.all_to_chips()
+        mlp.all_to_spread()
 
     @step_at(last)
     def _():
-        mlp.all_to_spread()
+        tail.all_to_shards()
 
     @pl.when(step >= 2 * steps)
     def _():
@@ -451,25 +466,24 @@
         store_images(images_grad, result, pad)
 
     def store_sums(layer, shares):
-        sums[0][layer] = shares[0][0, :, :, :three].astype(F32)
-        sums[1][layer] = shares[0][0, :, :, three:].astype(F32)
+        sums[0][layer] = shares[0][0, :, :, :three]
+        sums[1][layer] = shares[0][0, :, :, three:]
 
     @step_at(last)
     def _():
         flush_vectors(acc, vec0)
         tail.vec_begin()
-        tail.all_to_shards()
         tail.vec_to_chips()
         mlp.all_to_join()
         later.finish()
         store_sums(1, shares1)
         for total, share in zip(sums[2:], shares1[1:]):
-            total[1] = share[0].astype(F32)
+            total[1] = share[0]
         tail.vec_to_shards()
         tail.all_to_spread()
         mlp.finish()
         for total, share in zip(sums[2:], shares0[1:]):
-            total[0] = share[0].astype(F32)
+            total[0] = share[0]
         tail.all_to_join()
         tail.vec_end()
         tail.finish()
@@ -558,7 +572,7 @@
     def comm_params(self, collective_id):
         return pltpu.CompilerParams(
             dimension_semantics=("arbitrary",),
-            vmem_limit_bytes=62 * 2**20,
+            vmem_limit_bytes=67_043_328,
             collective_id=collective_id,
             has_side_effects=True,
         )
@@ -567,7 +581,10 @@
         state = jax.ShapeDtypeStruct((self.rows, self.width), F32)
         keeps = [jax.ShapeDtypeStruct(*self.keep[k]) for k in KEEP]
         mlp = [jax.ShapeDtypeStruct(s, BF16) for s in self.packed_shapes[1:]]
-        chunks = [chunks_of(shards0, mesh_sizes), chunks_of(shards1[:3], mesh_sizes)]
+        chunks = [
+            chunks_of(shards0, mesh_sizes),
+            chunks_of(shards1[:3], mesh_sizes, undivided=(2,)),
+        ]
         n = self.steps
         out = pl.pallas_call(
             functools.partial(first_kernel, self.sizes, n, mesh_sizes, chunks),
@@ -613,13 +630,13 @@
         ]
         chunks = [
             chunks_of(whole_grads, mesh_sizes, 1, (1,)),
-            chunks_of(whole_grads[1:], mesh_sizes, 1, (0,)),
+            chunks_of(whole_grads[1:], mesh_sizes, 1, ()),
             chunks_of(whole_grads[:1], mesh_sizes, 3, (0,)),
         ]
         shares = [(1,) + g.shape[1:] for g in whole_grads]
         blocks = whole_grads[0].shape[1:3]
         sums = [
-            jax.ShapeDtypeStruct((2,) + shape, F32)
+            jax.ShapeDtypeStruct((2,) + shape, BF16)
             for shape in (
                 blocks + (3 * self.width,),
                 blocks + (self.width,),
@@ -703,7 +720,7 @@
         return ref.at[shard, pl.ds(at + first, size)]
 
 
-def chunks_of(arrays, mesh_sizes, want=1, shards_first=()):
+def chunks_of(arrays, mesh_sizes, want=1, shards_first=(), undivided=()):
     chips = mesh_sizes[1] // 2
     lists = []
     for array, (_, blocks, _, columns) in enumerate(a.shape for a in arrays):
@@ -715,7 +732,8 @@
         lists.append(
             [
                 Chunk(
-                    array, blocks, columns, by_columns, extent, j * extent, chips,
+                    array, blocks, columns, by_columns, extent, j * extent,
+                    1 if array in undivided else chips,
                     array * want + j in shards_first,
                 )
                 for j in range(parts)
@@ -1191,7 +1209,7 @@
     images_grad, sums, small0, small1 = plan.last(
         flowing, images, [first_matrix] + list(mlp0), vecs0, keeps, blocks, sizes, 2
     )
-    full = [x.reshape(layers, -1, x.shape[3]) for x in sums]
+    full = [x.reshape(layers, -1, x.shape[3]).astype(F32) for x in sums]
     small = jnp.stack([small0, small1])
     me = lax.axis_index("grp")
     vec_out = lax.dynamic_slice_in_dim(small[:, :VECTORS], me * part, part, axis=2)

time: 244 us -> 235 us (0.963)
  Pallas kernels: 224 us -> 214 us
  other arithmetic: 2.16 us -> 7.94 us
  local copies, waits for them, and re-layouts: 16.9 us -> 11.4 us
    pallas_call x1, Pallas kernels: 55.3 us -> 47.4 us  [first(): pl.pallas_call(functools.partial(first_kernel, self.sizes, n, mesh_sizes,...]
    unnamed x39 -> x37, local copies, waits for them, and re-layouts: 8.83 us -> 3.34 us
    convert_element_type x0 -> x4, other arithmetic: none -> 5.05 us  [on_device(): full = [x.reshape(layers, -1, x.shape[3]).astype(F32) for x in sums]]
where the time goes in v6:
time: 235 us; the launch traced here: 234 us
  Pallas kernels  214 us (91%)
  local copies, waits for them, and re-layouts  11.4 us (5%)
  other arithmetic  7.94 us (3%)
    pallas_call x1, Pallas kernels, last(): pl.pallas_call(functools.partial(last_kernel, self.sizes, n, mesh_sizes,...  77.3 us
    pallas_call x1, Pallas kernels, middle(): pl.pallas_call(functools.partial(middle_kernel, self.sizes), name='layer_...  72.1 us
    pallas_call x1, Pallas kernels, first(): pl.pallas_call(functools.partial(first_kernel, self.sizes, n, mesh_sizes,...  47.4 us
    pallas_call x1, Pallas kernels, gather(): pl.pallas_call(functools.partial(gather_kernel, chunks, sizes), name='gat...  17.3 us
    convert_element_type x4, other arithmetic, on_device(): full = [x.reshape(layers, -1, x.shape[3]).astype(F32) for x in sums]  5.05 us

profile of v6, /device:TPU:0, one launch (start us, length us, event | category | flops | bytes accessed | tf_op | source)
XLA Modules:
  0.0 234.3 jit_solution(11335791368943764910)
XLA Ops:
  0.7 1.1 constant_dynamic-update-slice_fusion.1
  1.9 1.0 constant_dynamic-update-slice_fusion
  2.9 0.9 slice_bitcast_fusion
  4.1 0.6 fusion.2
  4.7 17.3 %gather_params.1 = (bf16[4,12,8,1536]{3,2,1,0:T(8,128)(2,1)S(1)}, f32[4,12,96]{2,1,0:T(8,128)S(1)}) custom-call(bf16[1,12,8,1536]{3,2,1,0:T(8,128)(2,1)S(1)} %get-tuple-element.76.refs_0_, f32[1,12,96]{2,1,0:T(8,128)S(1)} %get-tuple-element.86.refs_1_), custom_call_target="tpu_custom_call" | custom-call | tf_op jit(solution)/shard_map/gather_params/pallas_call | solution.py:911
  22.0 1.0 copy-done
  23.3 0.7 maximum_maximum_fusion.refs_2_.refs_5_
  23.9 0.9 slice_bitcast_fusion.2
  24.8 47.4 %layer_first.1 = (f32[2080,384]{1,0:T(8,128)}, bf16[2080,1152]{1,0:T(8,128)(2,1)}, f32[10,6,208,208]{3,2,1,0:T(8,128)}, bf16[10,384,208]{2,1,0:T(8,128)(2,1)}, f...) custom-call(bf16[10,197,384]{2,1,0:T(8,128)(2,1)} %refs_1_.3, ...), custom_call_target="tpu_custom_call" | custom-call | flops 6971719680 | bytes 41943040 | tf_op jit(solution)/shard_map/layer_first/pallas_call | solution.py:589
  72.2 0.7 slice_bitcast_fusion.6
  73.0 0.7 slice.77
  73.8 1.3 maximum_maximum_fusion.1.refs_5_
  75.1 72.1 %layer_middle.1 = (bf16[10,197,384]{2,1,0:T(8,128)(2,1)}, f32[2080,384]{1,0:T(8,128)}, bf16[384,1536]{1,0:T(8,128)(2,1)}, bf16[384,1536]{1,0:T(8,128)(2,1)}, bf1...) custom-call(f32[2080,384]{1,0:T(8,128)} %get-tuple-element.45.refs_0_, bf16[10,197,384]{2,1,0:T(8,128)(2,1)} %refs_1_.2, ...), custom_call_target="tpu_custom_call" | custom-call | flops 20915159040 | bytes 41943040 | tf_op jit(solution)/shard_map/layer_middle/pallas_call | solution.py:611
  147.3 77.3 %layer_last.1 = (bf16[10,197,384]{2,1,0:T(8,128)(2,1)}, bf16[2,12,8,1152]{3,2,1,0:T(8,128)(2,1)}, bf16[2,12,8,384]{3,2,1,0:T(8,128)(2,1)}, bf16[2,12,8,1536]{3,2...) custom-call(f32[2080,384]{1,0:T(8,128)} %get-tuple-element.51.refs_0_, ...), custom_call_target="tpu_custom_call" | custom-call | flops 13943439360 | bytes 41943040 | tf_op jit(solution)/shard_map/layer_last/pallas_call | solution.py:655
  224.6 0.8 fusion
  225.4 0.6 constant_dynamic-slice_fusion
  226.0 0.7 pad_slice_fusion
  226.7 0.7 pad_slice_fusion.1
  227.5 0.6 fusion.1
  228.1 2.2 bitcast_convert_fusion
  230.3 1.1 bitcast_convert_fusion.1
  231.4 1.0 bitcast_convert_fusion.2
  232.4 0.7 bitcast_convert_fusion.3
  233.2 1.1 copy.45
  (55 shorter events, 0.8 us)
Async XLA Ops:
  0.6 2.2 copy-start.4
  1.8 2.0 copy-start.8
  1.8 2.1 copy-start.9
  1.8 2.1 copy-start.10
  1.8 2.1 copy-start.11
  1.8 2.1 copy-start.12
  1.8 2.1 copy-start.13
  1.8 2.1 copy-start.14
  1.9 2.2 copy-start.15
  1.9 2.2 copy-start.16
  2.9 21.1 %copy-start.3 = (bf16[2,384,384]{2,1,0:T(8,128)(2,1)S(1)}, bf16[2,384,384]{2,1,0:T(8,128)(2,1)}, u32[]{:S(2)}) copy-start(bf16[2,384,384]{2,1,0:T(8,128)(2,1)} %param.28) | copy-start | bytes 1769476
  22.0 1.0 copy-start
  23.2 1.6 copy-start.7
  224.6 5.7 %copy-start.2 = (bf16[2,12,8,1536]{3,2,1,0:T(8,128)(2,1)S(1)}, bf16[2,12,8,1536]{3,2,1,0:T(8,128)(2,1)}, u32[]{:S(2)}) copy-start(bf16[2,12,8,1536]{3,2,1,0:T(8,128)(2,1)} %get-tuple-element.69) | copy-start | bytes 1769476
  228.1 3.4 %copy-start.5 = (bf16[2,12,8,1152]{3,2,1,0:T(8,128)(2,1)S(1)}, bf16[2,12,8,1152]{3,2,1,0:T(8,128)(2,1)}, u32[]{:S(2)}) copy-start(bf16[2,12,8,1152]{3,2,1,0:T(8,128)(2,1)} %get-tuple-element.67) | copy-start | bytes 1327108
  230.3 2.1 copy-start.6
  230.3 2.9 %copy-start.1 = (bf16[10,197,384]{2,1,0:T(8,128)(2,1)S(1)}, bf16[10,197,384]{2,1,0:T(8,128)(2,1)}, u32[]{:S(2)}) copy-start(bf16[10,197,384]{2,1,0:T(8,128)(2,1)} %get-tuple-element.105) | copy-start | bytes 4538884

commit v7 on v6

--- a/solution.py
+++ b/solution.py
@@ -733,7 +733,7 @@
             [
                 Chunk(
                     array, blocks, columns, by_columns, extent, j * extent,
-                    1 if array in undivided else chips,
+                    1 if array * want + j in undivided else chips,
                     array * want + j in shards_first,
                 )
                 for j in range(parts)
@@ -907,7 +907,7 @@
 
 
 def gather(shard, vec, sizes, collective_id):
-    chunks = chunks_of([shard], sizes, 2)
+    chunks = chunks_of([shard], sizes, 3, undivided=(2,))
     return pl.pallas_call(
         functools.partial(gather_kernel, chunks, sizes),
         name="gather_params",

time: 235 us -> 235 us (level)
  no operation moved by 1% of the time
where the time goes in v7:
time: 235 us; the launch traced here: 234 us
  Pallas kernels  214 us (91%)
  local copies, waits for them, and re-layouts  11.4 us (5%)
  other arithmetic  7.94 us (3%)
    pallas_call x1, Pallas kernels, last(): pl.pallas_call(functools.partial(last_kernel, self.sizes, n, mesh_sizes,...  78.6 us
    pallas_call x1, Pallas kernels, middle(): pl.pallas_call(functools.partial(middle_kernel, self.sizes), name='layer_...  72.1 us
    pallas_call x1, Pallas kernels, first(): pl.pallas_call(functools.partial(first_kernel, self.sizes, n, mesh_sizes,...  46.8 us
    pallas_call x1, Pallas kernels, gather(): pl.pallas_call(functools.partial(gather_kernel, chunks, sizes), name='gat...  16.7 us
    convert_element_type x4, other arithmetic, on_device(): full = [x.reshape(layers, -1, x.shape[3]).astype(F32) for x in sums]  5.05 us

profile of v7, /device:TPU:0, one launch (start us, length us, event | category | flops | bytes accessed | tf_op | source)
XLA Modules:
  0.0 234.4 jit_solution(14011764113544215243)
XLA Ops:
  0.7 1.1 constant_dynamic-update-slice_fusion.1
  1.9 1.0 constant_dynamic-update-slice_fusion
  2.9 0.9 slice_bitcast_fusion
  4.1 0.6 fusion.2
  4.7 16.7 %gather_params.1 = (bf16[4,12,8,1536]{3,2,1,0:T(8,128)(2,1)S(1)}, f32[4,12,96]{2,1,0:T(8,128)S(1)}) custom-call(bf16[1,12,8,1536]{3,2,1,0:T(8,128)(2,1)S(1)} %get-tuple-element.76.refs_0_, f32[1,12,96]{2,1,0:T(8,128)S(1)} %get-tuple-element.86.refs_1_), custom_call_target="tpu_custom_call" | custom-call | tf_op jit(solution)/shard_map/gather_params/pallas_call | solution.py:911
  21.4 1.0 copy-done
  22.6 0.7 maximum_maximum_fusion.refs_2_.refs_5_
  23.3 0.9 slice_bitcast_fusion.2
  24.2 46.8 %layer_first.1 = (f32[2080,384]{1,0:T(8,128)}, bf16[2080,1152]{1,0:T(8,128)(2,1)}, f32[10,6,208,208]{3,2,1,0:T(8,128)}, bf16[10,384,208]{2,1,0:T(8,128)(2,1)}, f...) custom-call(bf16[10,197,384]{2,1,0:T(8,128)(2,1)} %refs_1_.3, ...), custom_call_target="tpu_custom_call" | custom-call | flops 6971719680 | bytes 41943040 | tf_op jit(solution)/shard_map/layer_first/pallas_call | solution.py:589
  71.0 0.7 slice_bitcast_fusion.6
  71.8 0.7 slice.77
  72.6 1.3 maximum_maximum_fusion.1.refs_5_
  73.9 72.1 %layer_middle.1 = (bf16[10,197,384]{2,1,0:T(8,128)(2,1)}, f32[2080,384]{1,0:T(8,128)}, bf16[384,1536]{1,0:T(8,128)(2,1)}, bf16[384,1536]{1,0:T(8,128)(2,1)}, bf1...) custom-call(f32[2080,384]{1,0:T(8,128)} %get-tuple-element.45.refs_0_, bf16[10,197,384]{2,1,0:T(8,128)(2,1)} %refs_1_.2, ...), custom_call_target="tpu_custom_call" | custom-call | flops 20915159040 | bytes 41943040 | tf_op jit(solution)/shard_map/layer_middle/pallas_call | solution.py:611
  146.1 78.6 %layer_last.1 = (bf16[10,197,384]{2,1,0:T(8,128)(2,1)}, bf16[2,12,8,1152]{3,2,1,0:T(8,128)(2,1)}, bf16[2,12,8,384]{3,2,1,0:T(8,128)(2,1)}, bf16[2,12,8,1536]{3,2...) custom-call(f32[2080,384]{1,0:T(8,128)} %get-tuple-element.51.refs_0_, ...), custom_call_target="tpu_custom_call" | custom-call | flops 13943439360 | bytes 41943040 | tf_op jit(solution)/shard_map/layer_last/pallas_call | solution.py:655
  224.7 0.8 fusion
  225.5 0.6 constant_dynamic-slice_fusion
  226.1 0.7 pad_slice_fusion
  226.8 0.7 pad_slice_fusion.1
  227.6 0.6 fusion.1
  228.2 2.2 bitcast_convert_fusion
  230.4 1.1 bitcast_convert_fusion.1
  231.5 1.0 bitcast_convert_fusion.2
  232.5 0.7 bitcast_convert_fusion.3
  233.2 1.1 copy.45
  (55 shorter events, 0.8 us)
Async XLA Ops:
  0.6 2.2 copy-start.4
  1.8 2.0 copy-start.8
  1.8 2.1 copy-start.9
  1.8 2.1 copy-start.10
  1.8 2.1 copy-start.11
  1.8 2.1 copy-start.12
  1.8 2.1 copy-start.13
  1.8 2.1 copy-start.14
  1.9 2.2 copy-start.15
  1.9 2.2 copy-start.16
  2.9 20.5 %copy-start.3 = (bf16[2,384,384]{2,1,0:T(8,128)(2,1)S(1)}, bf16[2,384,384]{2,1,0:T(8,128)(2,1)}, u32[]{:S(2)}) copy-start(bf16[2,384,384]{2,1,0:T(8,128)(2,1)} %param.28) | copy-start | bytes 1769476
  21.4 1.0 copy-start
  22.6 1.6 copy-start.7
  224.7 5.7 %copy-start.2 = (bf16[2,12,8,1536]{3,2,1,0:T(8,128)(2,1)S(1)}, bf16[2,12,8,1536]{3,2,1,0:T(8,128)(2,1)}, u32[]{:S(2)}) copy-start(bf16[2,12,8,1536]{3,2,1,0:T(8,128)(2,1)} %get-tuple-element.69) | copy-start | bytes 1769476
  228.2 3.4 %copy-start.5 = (bf16[2,12,8,1152]{3,2,1,0:T(8,128)(2,1)S(1)}, bf16[2,12,8,1152]{3,2,1,0:T(8,128)(2,1)}, u32[]{:S(2)}) copy-start(bf16[2,12,8,1152]{3,2,1,0:T(8,128)(2,1)} %get-tuple-element.67) | copy-start | bytes 1327108
  230.4 2.1 copy-start.6
  230.4 2.9 %copy-start.1 = (bf16[10,197,384]{2,1,0:T(8,128)(2,1)S(1)}, bf16[10,197,384]{2,1,0:T(8,128)(2,1)}, u32[]{:S(2)}) copy-start(bf16[10,197,384]{2,1,0:T(8,128)(2,1)} %get-tuple-element.105) | copy-start | bytes 4538884
